TPU v7x, 32 devices: a whole 2x2x4 slice. The times are simulated.
32 devices in a mesh: shard: 2 (over core), ctx: 8 (over z, x), tp: 2 (over y).
Axes of the slice: x: 2, y: 2, z: 4, core: 2. Of those that a mesh axis runs over, the one named last changes fastest.
Arguments:
- tokens: bfloat16 [2, 4096, 1024], P('shard', ('ctx', 'tp')), may hold values from -6 to 6
- value_first: bfloat16 [2, 4096, 1024], P('shard', ('ctx', 'tp')), may hold values from -6 to 6
- teacher: bfloat16 [2, 4096, 1024], P('shard', ('ctx', 'tp')), may hold values from -13 to 13
- valid: int32 [2, 4096], P('shard', ('ctx', 'tp')), may hold values from 0 to 1, as said below
- blocks: int32 [2, 4096], P('shard'), may hold values from 0 to 31, never falling along the last dimension, each value on 1 to 256 neighbouring positions
- gain_attn: float32 [1024], replicated, may hold values from 0.1 to 1.9
- gain_ffn: float32 [1024], replicated, may hold values from 0.1 to 1.9
- w_query: bfloat16 [1024, 1024], P('shard', 'tp'), may hold values from -0.375 to 0.375
- w_key: bfloat16 [1024, 1024], P('shard', 'tp'), may hold values from -0.1875 to 0.1875
- w_value: bfloat16 [1024, 1024], P('shard', 'tp'), may hold values from -0.1875 to 0.1875
- w_out: bfloat16 [1024, 1024], P('tp', 'shard'), may hold values from -0.75 to 0.75
- w_gate: bfloat16 [1024, 2816], P('shard', 'tp'), may hold values from -0.1875 to 0.1875
- w_up: bfloat16 [1024, 2816], P('shard', 'tp'), may hold values from -0.1875 to 0.1875
- w_down: bfloat16 [2816, 1024], P('tp', 'shard'), may hold values from -0.109375 to 0.109375
Outputs:
- output: bfloat16 [2, 4096, 1024], P('shard', ('ctx', 'tp'))
- loss: float32 [], replicated
- tokens_grad: float32 [2, 4096, 1024], P('shard', ('ctx', 'tp'))
- value_first_grad: float32 [2, 4096, 1024], P('shard', ('ctx', 'tp'))
- gain_attn_grad: float32 [1024], replicated
- gain_ffn_grad: float32 [1024], replicated
- w_query_grad: float32 [1024, 1024], P('shard', 'tp')
- w_key_grad: float32 [1024, 1024], P('shard', 'tp')
- w_value_grad: float32 [1024, 1024], P('shard', 'tp')
- w_out_grad: float32 [1024, 1024], P('tp', 'shard')
- w_gate_grad: float32 [1024, 2816], P('shard', 'tp')
- w_up_grad: float32 [1024, 2816], P('shard', 'tp')
- w_down_grad: float32 [2816, 1024], P('tp', 'shard')
Inputs may be any that keep to these rules, and one draw needn't show every extreme that they name: `blocks`: block numbers count from 0 and never fall along a sequence; each block holds 1 to 256 tokens, one exactly 256. The first token of every sequence is valid.
All inputs are finite; a program needn't handle non-finite values.
Results may differ from a plain program's by a relative error of at most 0.019.
Values may be sent and summed in bfloat16 or wider, within the bound.
No kernel may reach another device: no remote copies, remote signals or barrier semaphores. Data moves between devices by JAX's collectives and lax.ppermute only.
A program may use at most 256 MiB of HBM per device.

v0:
```python
import jax
import jax.numpy as jnp
from jax import lax
from jax.sharding import PartitionSpec as P

HEAD_DIM = 64


epsilon = 1e-06


def rms_norm(values, gain):
    return values * lax.rsqrt(jnp.mean(values * values, axis=-1, keepdims=True) + epsilon) * gain


def product(left, right):
    return jnp.dot(left, right, preferred_element_type=jnp.float32)


def product_nt(left, right):
    return lax.dot_general(
        left, right, (((1,), (1,)), ((), ())), preferred_element_type=jnp.float32
    )


def product_tn(left, right):
    return lax.dot_general(
        left, right, (((0,), (0,)), ((), ())), preferred_element_type=jnp.float32
    )


def head_slice(values, head_index):
    return lax.dynamic_slice_in_dim(values, head_index * HEAD_DIM, HEAD_DIM, 1)


def block_layout(query_count):
    return (query_count, query_count // query_count)


def heads_to_columns(stacked):
    return jnp.transpose(stacked, (1, 0, 2)).reshape(
        stacked.shape[1], stacked.shape[0] * stacked.shape[2]
    )


def attend_forward(queries, keys_all, values_all, query_marks, key_marks):
    query_count = queries.shape[0]
    block_size, block_count = block_layout(query_count)
    score_scale = HEAD_DIM ** (-0.5)

    def one_head(head_index):
        query_head = head_slice(queries, head_index)
        key_head = head_slice(keys_all, head_index)
        value_head = head_slice(values_all, head_index)

        def one_block(block_index):
            scores = product_nt(query_head, key_head) * score_scale
            scores = jnp.where(key_marks[None, :] <= query_marks[:, None], scores, -1e30)
            highest = jnp.max(scores, axis=1, keepdims=True)
            exponent = jnp.exp(scores - highest)
            totals = jnp.sum(exponent, axis=1, keepdims=True)
            weights = (exponent / totals).astype(jnp.bfloat16)
            return (product(weights, value_head), (highest + jnp.log(totals))[:, 0])

        outputs, log_totals = lax.map(one_block, jnp.arange(block_count))
        return (outputs.reshape(query_count, HEAD_DIM), log_totals.reshape(query_count))

    outputs, log_totals = lax.map(one_head, jnp.arange(queries.shape[1] // HEAD_DIM))
    return (heads_to_columns(outputs), log_totals)


def attend_backward(
    queries, keys_all, values_all, grad_attended, log_totals, query_marks, key_marks
):
    query_count = queries.shape[0]
    block_size, block_count = block_layout(query_count)
    score_scale = HEAD_DIM ** (-0.5)

    def one_head(item):
        head_index, head_totals = item
        query_head = head_slice(queries, head_index)
        key_head = head_slice(keys_all, head_index)
        value_head = head_slice(values_all, head_index)
        grad_head = head_slice(grad_attended, head_index)

        def one_block(carry, block_index):
            scores = product_nt(query_head, key_head) * score_scale
            scores = jnp.where(key_marks[None, :] <= query_marks[:, None], scores, -1e30)
            probs = jnp.exp(scores - head_totals[:, None])
            grad_probs = product_nt(grad_head, value_head)
            inner = jnp.sum(probs * grad_probs, axis=1, keepdims=True)
            grad_scores = (probs * (grad_probs - inner)).astype(jnp.bfloat16)
            query_grad = product(grad_scores, key_head) * score_scale
            key_grad, value_grad = carry
            key_grad = key_grad + product_tn(grad_scores, query_head) * score_scale
            value_grad = value_grad + product_tn(probs.astype(jnp.bfloat16), grad_head)
            return ((key_grad, value_grad), (query_grad, inner[:, 0]))

        empty = jnp.zeros((keys_all.shape[0], HEAD_DIM), jnp.float32)
        start_carry = (empty, empty)
        sums, outs = lax.scan(one_block, start_carry, jnp.arange(block_count))
        query_grad = outs[0].reshape(query_count, HEAD_DIM)
        return (query_grad, sums[0], sums[1])

    head_count = queries.shape[1] // HEAD_DIM
    results = lax.map(one_head, (jnp.arange(head_count), log_totals))
    return (
        heads_to_columns(results[0]),
        heads_to_columns(results[1]),
        heads_to_columns(results[2]),
    )


def on_device(
    tokens,
    value_first,
    teacher,
    valid,
    blocks,
    gain_attn,
    gain_ffn,
    w_query,
    w_key,
    w_value,
    w_out,
    w_gate,
    w_up,
    w_down,
):
    width = tokens.shape[2]
    own_rows = tokens.shape[1]
    group_rows = own_rows * lax.axis_size("tp")
    inputs = tokens.reshape(own_rows, width).astype(jnp.float32)
    key_marks = blocks.reshape(-1)
    query_marks = lax.dynamic_slice_in_dim(
        key_marks, lax.axis_index("ctx") * group_rows, group_rows, 0
    )
    gathered = (
        lax.all_gather(w_query, "shard", axis=0, tiled=True),
        lax.all_gather(w_key, "shard", axis=0, tiled=True),
        lax.all_gather(w_value, "shard", axis=0, tiled=True),
        lax.all_gather(w_gate, "shard", axis=0, tiled=True),
        lax.all_gather(w_up, "shard", axis=0, tiled=True),
        lax.all_gather(w_out, "shard", axis=1, tiled=True),
        lax.all_gather(w_down, "shard", axis=1, tiled=True),
    )
    weight_query, weight_key, weight_value, weight_gate, weight_up, weight_out, weight_down = (
        gathered
    )

    def spread(values):
        return lax.all_gather(values, "tp", axis=0, tiled=True)

    def collect(terms):
        return lax.psum_scatter(terms, "tp", scatter_dimension=0, tiled=True)

    normed_one = spread(rms_norm(inputs, gain_attn).astype(jnp.bfloat16))
    first_mine = lax.all_to_all(
        value_first.reshape(own_rows, width), "tp", split_axis=1, concat_axis=0, tiled=True
    )
    queries = product(normed_one, weight_query).astype(jnp.bfloat16)
    keys = product(normed_one, weight_key).astype(jnp.bfloat16)
    mixed = (0.5 * product(normed_one, weight_value) + 0.5 * first_mine.astype(jnp.float32)).astype(
        jnp.bfloat16
    )
    keys_all, mixed_all = (
        lax.all_gather(keys, "ctx", axis=0, tiled=True),
        lax.all_gather(mixed, "ctx", axis=0, tiled=True),
    )
    attended, log_totals = attend_forward(queries, keys_all, mixed_all, query_marks, key_marks)
    attended = attended.astype(jnp.bfloat16)
    hidden = inputs + collect(product(attended, weight_out))
    normed_two = spread(rms_norm(hidden, gain_ffn).astype(jnp.bfloat16))
    gate_value = product(normed_two, weight_gate)
    up_value = product(normed_two, weight_up)
    logistic = jax.nn.sigmoid(gate_value)
    activated = (gate_value * logistic * up_value).astype(jnp.bfloat16)
    final = hidden + collect(product(activated, weight_down))
    target = teacher.reshape(own_rows, width).astype(jnp.float32)
    keep = valid.reshape(own_rows).astype(jnp.float32)
    difference = final - target
    local_error = jnp.sum(jnp.mean(difference * difference, axis=1) * keep)
    error_sum, valid_count = lax.psum((local_error, jnp.sum(keep)), ("shard", "ctx", "tp"))
    loss = error_sum / valid_count
    token_total = group_rows * lax.axis_size("ctx") * lax.axis_size("shard")
    grad_final = token_total / valid_count * keep[:, None] * difference
    grad_round = spread(grad_final.astype(jnp.bfloat16))
    grad_act = product_nt(grad_round, weight_down)
    grad_gate = (grad_act * up_value * logistic * (1.0 + gate_value * (1.0 - logistic))).astype(
        jnp.bfloat16
    )
    grad_up = (grad_act * gate_value * logistic).astype(jnp.bfloat16)
    grad_two = collect(product_nt(grad_gate, weight_gate) + product_nt(grad_up, weight_up))
    norm_two_back = jax.vjp(rms_norm, hidden, gain_ffn)[1]
    hidden_part, gain_ffn_term = norm_two_back(grad_two)
    grad_hidden = grad_final + hidden_part
    hidden_round = spread(grad_hidden.astype(jnp.bfloat16))
    grad_attended = product_nt(hidden_round, weight_out).astype(jnp.bfloat16)
    query_grad, key_term, value_term = attend_backward(
        queries, keys_all, mixed_all, grad_attended, log_totals, query_marks, key_marks
    )
    key_sum, value_sum = (
        lax.psum_scatter(
            key_term.astype(jnp.bfloat16), "ctx", scatter_dimension=0, tiled=True
        ).astype(jnp.float32),
        lax.psum_scatter(
            value_term.astype(jnp.bfloat16), "ctx", scatter_dimension=0, tiled=True
        ).astype(jnp.float32),
    )
    query_round = query_grad.astype(jnp.bfloat16)
    key_round = key_sum.astype(jnp.bfloat16)
    value_half = (0.5 * value_sum).astype(jnp.bfloat16)
    grad_one = collect(
        product_nt(query_round, weight_query)
        + product_nt(key_round, weight_key)
        + product_nt(value_half, weight_value)
    )
    norm_one_back = jax.vjp(rms_norm, inputs, gain_attn)[1]
    input_part, gain_attn_term = norm_one_back(grad_one)
    tokens_grad = grad_hidden + input_part
    first_grad = lax.all_to_all(value_half, "tp", split_axis=0, concat_axis=1, tiled=True).astype(
        jnp.float32
    )
    gain_attn_grad, gain_ffn_grad = lax.psum(
        (gain_attn_term, gain_ffn_term), ("shard", "ctx", "tp")
    )
    piece = lax.psum_scatter(
        jnp.concatenate(
            [
                product_tn(normed_one, query_round),
                product_tn(normed_one, key_round),
                product_tn(normed_one, value_half),
                product_tn(hidden_round, attended),
                product_tn(normed_two, grad_gate),
                product_tn(normed_two, grad_up),
                product_tn(grad_round, activated),
            ],
            axis=1,
        ).astype(jnp.bfloat16),
        "shard",
        scatter_dimension=0,
        tiled=True,
    )
    summed = lax.psum(piece, "ctx").astype(jnp.float32)
    half_width = w_query.shape[1]
    hidden_width = w_gate.shape[1]
    offset_gate = 4 * half_width
    offset_up = offset_gate + hidden_width
    offset_down = offset_up + hidden_width
    w_query_grad = summed[:, 0:half_width]
    w_key_grad = summed[:, half_width : 2 * half_width]
    w_value_grad = summed[:, 2 * half_width : 3 * half_width]
    w_out_grad = jnp.transpose(summed[:, 3 * half_width : offset_gate])
    w_gate_grad = summed[:, offset_gate:offset_up]
    w_up_grad = summed[:, offset_up:offset_down]
    w_down_grad = jnp.transpose(summed[:, offset_down : offset_down + hidden_width])
    output = final.astype(jnp.bfloat16).reshape(1, own_rows, width)
    return (
        output,
        loss,
        tokens_grad.reshape(1, own_rows, width),
        first_grad.reshape(1, own_rows, width),
        gain_attn_grad,
        gain_ffn_grad,
        w_query_grad,
        w_key_grad,
        w_value_grad,
        w_out_grad,
        w_gate_grad,
        w_up_grad,
        w_down_grad,
    )


def solution(mesh):
    placed = (
        P("shard", ("ctx", "tp"), None),
        P("shard", ("ctx", "tp"), None),
        P("shard", ("ctx", "tp"), None),
        P("shard", ("ctx", "tp")),
        P("shard", None),
        P(),
        P(),
        P("shard", "tp"),
        P("shard", "tp"),
        P("shard", "tp"),
        P("tp", "shard"),
        P("shard", "tp"),
        P("shard", "tp"),
        P("tp", "shard"),
    )
    return jax.shard_map(
        on_device,
        mesh=mesh,
        in_specs=placed,
        out_specs=(
            P("shard", ("ctx", "tp"), None),
            P(),
            P("shard", ("ctx", "tp"), None),
            P("shard", ("ctx", "tp"), None),
            P(),
            P(),
            P("shard", "tp"),
            P("shard", "tp"),
            P("shard", "tp"),
            P("tp", "shard"),
            P("shard", "tp"),
            P("shard", "tp"),
            P("tp", "shard"),
        ),
        check_vma=False,
    )
```

profile of v0, /device:TPU:0, one launch (start us, length us, event | category | flops | bytes accessed | tf_op | source)
XLA Modules:
  0.0 1274.1 jit_solution(9744088578391808102)
XLA Ops:
  21.3 24.6 %all-gather.14.cloned.1.call-done = bf16[512,1024]{1,0:T(8,128)(2,1)} async-done(((bf16[256,1024]{1,0:T(8,128)(2,1)}), bf16[512,1024]{1,0:T(8,128)(2,1)}) %all-gather.14.cloned.1.call-update) | async-done | bytes 1048592 | tf_op jit(solution)/shard_map/all_gather | solution.py:152
  49.5 10.7 all_to_all.26
  70.1 75.2 %all-gather.20.cloned.1.call-done = bf16[4096,512]{1,0:T(8,128)(2,1)} async-done(((bf16[512,512]{1,0:T(8,128)(2,1)}), bf16[4096,512]{1,0:T(8,128)(2,1)}) %all-gather.20.cloned.1.call-update) | async-done | bytes 4194320 | tf_op jit(solution)/shard_map/all_gather | solution.py:167
  145.3 74.2 %all-gather.24.cloned.1.call-done = bf16[4096,512]{1,0:T(8,128)(2,1)} async-done(((bf16[512,512]{1,0:T(8,128)(2,1)}), bf16[4096,512]{1,0:T(8,128)(2,1)}) %all-gather.24.cloned.1.call-update) | async-done | bytes 4194320 | tf_op jit(solution)/shard_map/all_gather | solution.py:168
  219.6 73.0 %while.10 = (s32[]{:T(128)}, bf16[8,512,64]{1,2,0:T(8,128)(2,1)S(1)}, f32[8,512]{1,0:T(8,128)S(1)}, s32[1,4096]{1,0:T(1,128)S(1)}, s32[512]{0:T(512)S(1)}, /*ind...) while((s32[]{:T(128)}, ...), condition=%wide.region_4.0_spmd, body=%wide.region_1.4_spmd.sunk | while | flops 555744768 | bytes 27565260 | solution.py:68
  297.0 29.4 %reduce-scatter.8.cloned.1.call-done = f32[256,1024]{1,0:T(8,128)} async-done(((f32[512,1024]{1,0:T(8,128)}), f32[256,1024]{1,0:T(8,128)}) %reduce-scatter.8.cloned.1.call-update) | async-done | bytes 1048592 | tf_op jit(solution)/shard_map/reduce_scatter | solution.py:155
  330.5 9.3 all-gather.30.cloned.1.call-done
  339.8 24.6 %all-gather.28.cloned.1.call-done = bf16[512,1024]{1,0:T(8,128)(2,1)} async-done(((bf16[256,1024]{1,0:T(8,128)(2,1)}), bf16[512,1024]{1,0:T(8,128)(2,1)}) %all-gather.28.cloned.1.call-update) | async-done | bytes 1048592 | tf_op jit(solution)/shard_map/all_gather | solution.py:152
  398.3 40.9 %psum.36 = f32[]{:T(128)} all-reduce(f32[]{:T(128)} %convert_reduce_fusion), channel_id=1, replica_groups=mesh['shard'=2,'ctx'=8,'tp'=2] {'shard','ctx','tp'}, use_global_device_ids=true, to_apply=%region_12.13 | all-reduce | flops 1 | bytes 8 | tf_op jit(solution)/shard_map/psum | solution.py:183
  442.2 21.4 %all-gather.36.cloned.1.call-done = bf16[512,1024]{1,0:T(8,128)(2,1)} async-done(((bf16[256,1024]{1,0:T(8,128)(2,1)}), bf16[512,1024]{1,0:T(8,128)(2,1)}) %all-gather.36.cloned.1.call-update) | async-done | bytes 1048592 | tf_op jit(solution)/shard_map/all_gather | solution.py:152
  476.3 31.9 %reduce-scatter.12.cloned.1.call-done = f32[256,1024]{1,0:T(8,128)} async-done(((f32[512,1024]{1,0:T(8,128)}), f32[256,1024]{1,0:T(8,128)}) %reduce-scatter.12.cloned.1.call-update) | async-done | bytes 1048592 | tf_op jit(solution)/shard_map/reduce_scatter | solution.py:155
  512.9 20.9 %all-gather.38.cloned.1.call-done = bf16[512,1024]{1,0:T(8,128)(2,1)} async-done(((bf16[256,1024]{1,0:T(8,128)(2,1)}), bf16[512,1024]{1,0:T(8,128)(2,1)}) %all-gather.38.cloned.1.call-update) | async-done | bytes 1048592 | tf_op jit(solution)/shard_map/all_gather | solution.py:152
  536.2 233.1 %while.27 = (s32[]{:T(128)}, bf16[8,512,64]{1,2,0:T(8,128)(2,1)S(1)}, bf16[8,4096,64]{1,2,0:T(8,128)(2,1)}, bf16[8,4096,64]{1,2,0:T(8,128)(2,1)}, s32[1,4096]{1,...) while((s32[]{:T(128)}, ...), condition=%wide.region_17.18_spmd, body=%wide.region_15.17_spmd.sunk | while | flops 1363443200 | bytes 102398224 | solution.py:106
  576.6 7.9 multiply_convert_fusion.10
  605.7 7.9 multiply_convert_fusion.10
  634.8 7.9 multiply_convert_fusion.10
  693.1 7.9 multiply_convert_fusion.10
  783.3 74.6 %reduce-scatter.14.cloned.1.call-done = bf16[512,512]{0,1:T(8,128)(2,1)} async-done(((bf16[4096,512]{0,1:T(8,128)(2,1)}), bf16[512,512]{0,1:T(8,128)(2,1)}) %reduce-scatter.14.cloned.1.call-update) | async-done | bytes 524304 | tf_op jit(solution)/shard_map/reduce_scatter | solution.py:203
  860.5 88.5 %reduce-scatter.16.cloned.1.call-done = bf16[512,512]{1,0:T(8,128)(2,1)} async-done(((bf16[4096,512]{1,0:T(8,128)(2,1)}), bf16[512,512]{1,0:T(8,128)(2,1)}) %reduce-scatter.16.cloned.1.call-update) | async-done | bytes 524304 | tf_op jit(solution)/shard_map/reduce_scatter | solution.py:206
  973.6 15.7 %reduce-scatter.20.cloned.1.call-done = bf16[512,6272]{1,0:T(8,128)(2,1)} async-done(((bf16[1024,6272]{1,0:T(8,128)(2,1)}), bf16[512,6272]{1,0:T(8,128)(2,1)}) %reduce-scatter.20.cloned.1.call-update) | async-done | bytes 6422544 | tf_op jit(solution)/shard_map/reduce_scatter | solution.py:227
  994.6 10.0 all-to-all-done.1
  1007.4 19.1 %reduce-scatter.18.cloned.1.call-done = f32[256,1024]{1,0:T(8,128)} async-done(((f32[512,1024]{1,0:T(8,128)}), f32[256,1024]{1,0:T(8,128)}) %reduce-scatter.18.cloned.1.call-update) | async-done | bytes 1048592 | tf_op jit(solution)/shard_map/reduce_scatter | solution.py:155
  1028.1 43.6 %all-reduce = (f32[]{:T(128)}, f32[1024]{0:T(1024)}, f32[1024]{0:T(1024)}) all-reduce(f32[]{:T(128)} %multiply_reduce_fusion.5, f32[1024]{0:T(1024)S(1)} %get-tuple-element.215, f32[1024]{0:T(1024)S(1)} %copy-done.19), channel_id=1, replica_groups=mesh['shard'=2,'ctx'=8,'tp'=2] {'shard','ctx','tp'}, use_global_device_ids=true, to_apply=%region_10.11 | all-reduce | flops 2049 | bytes 16392 | tf_op jit(solution)/shard_map/psum | solution.py:183
  1075.6 172.7 %all-reduce.3.cloned.1.call-done = bf16[512,6272]{1,0:T(8,128)(2,1)} async-done(((bf16[512,6272]{1,0:T(8,128)(2,1)}), bf16[512,6272]{1,0:T(8,128)(2,1)}) %all-reduce.3.cloned.1.call-update) | async-done | bytes 6422544 | tf_op jit(solution)/shard_map/psum | solution.py:244
  (317 shorter events, 425.8 us)
Async XLA Ops:
  7.2 14.1 %all-gather.18.cloned.1.call-start = ((), (), s32[]{:S(2)}) async-start(), calls=%async_computation.11 | async-start | bytes 1572864 | tf_op jit(solution)/shard_map/all_gather | solution.py:140
  7.9 38.0 %all-gather.14.cloned.1.call-start = ((), (), s32[]{:S(2)}) async-start(), calls=%async_computation.9 | async-start | bytes 1572864 | tf_op jit(solution)/shard_map/all_gather | solution.py:152
  12.4 48.0 %all-gather.22.cloned.1.call-start = ((), (), s32[]{:S(2)}) async-start(), calls=%async_computation.13 | async-start | bytes 1572864 | tf_op jit(solution)/shard_map/all_gather | solution.py:141
  13.1 55.1 %all-gather.16.cloned.1.call-start = ((), (), s32[]{:S(2)}) async-start(), calls=%async_computation.10 | async-start | bytes 1572864 | tf_op jit(solution)/shard_map/all_gather | solution.py:139
  13.7 131.7 %all-gather.20.cloned.1.call-start = ((), (), s32[]{:S(2)}) async-start(), calls=%async_computation.12 | async-start | bytes 4718592 | tf_op jit(solution)/shard_map/all_gather | solution.py:167
  49.0 170.6 %all-gather.24.cloned.1.call-start = ((), (), s32[]{:S(2)}) async-start(), calls=%async_computation.14 | async-start | bytes 4718592 | tf_op jit(solution)/shard_map/all_gather | solution.py:168
  63.1 229.6 %all-gather.26.cloned.1.call-start = ((), (), s32[]{:S(2)}) async-start(), calls=%async_computation.15 | async-start | bytes 1572864 | tf_op jit(solution)/shard_map/all_gather | solution.py:144
  63.9 262.6 %reduce-scatter.8.cloned.1.call-start = ((), (), s32[]{:S(2)}) async-start(), calls=%async_computation.16 | async-start | bytes 3145728 | tf_op jit(solution)/shard_map/reduce_scatter | solution.py:155
  296.2 43.6 %all-gather.30.cloned.1.call-start = ((), (), s32[]{:S(2)}) async-start(), calls=%async_computation.18 | async-start | bytes 4325376 | tf_op jit(solution)/shard_map/all_gather | solution.py:142
  297.0 67.4 %all-gather.28.cloned.1.call-start = ((), (), s32[]{:S(2)}) async-start(), calls=%async_computation.17 | async-start | bytes 1572864 | tf_op jit(solution)/shard_map/all_gather | solution.py:152
  328.9 48.9 %all-gather.32.cloned.1.call-start = ((), (), s32[]{:S(2)}) async-start(), calls=%async_computation.19 | async-start | bytes 4325376 | tf_op jit(solution)/shard_map/all_gather | solution.py:143
  329.6 62.6 %all-gather.34.cloned.1.call-start = ((), (), s32[]{:S(2)}) async-start(), calls=%async_computation.20 | async-start | bytes 4325376 | tf_op jit(solution)/shard_map/all_gather | solution.py:145
  330.2 109.8 %reduce-scatter.10.cloned.1.call-start = ((), (), s32[]{:S(2)}) async-start(), calls=%async_computation.21 | async-start | bytes 3145728 | tf_op jit(solution)/shard_map/reduce_scatter | solution.py:155
  397.7 66.0 %all-gather.36.cloned.1.call-start = ((), (), s32[]{:S(2)}) async-start(), calls=%async_computation.22 | async-start | bytes 1572864 | tf_op jit(solution)/shard_map/all_gather | solution.py:152
  442.2 66.0 %reduce-scatter.12.cloned.1.call-start = ((), (), s32[]{:S(2)}) async-start(), calls=%async_computation.23 | async-start | bytes 3145728 | tf_op jit(solution)/shard_map/reduce_scatter | solution.py:155
  476.2 57.6 %all-gather.38.cloned.1.call-start = ((), (), s32[]{:S(2)}) async-start(), calls=%async_computation.24 | async-start | bytes 1572864 | tf_op jit(solution)/shard_map/all_gather | solution.py:152
  512.4 345.5 %reduce-scatter.14.cloned.1.call-start = ((), (), s32[]{:S(2)}) async-start(), calls=%async_computation.25 | async-start | bytes 4718592 | tf_op jit(solution)/shard_map/reduce_scatter | solution.py:203
  769.3 179.8 %reduce-scatter.16.cloned.1.call-start = ((), (), s32[]{:S(2)}) async-start(), calls=%async_computation.26 | async-start | bytes 4718592 | tf_op jit(solution)/shard_map/reduce_scatter | solution.py:206
  775.9 213.4 %reduce-scatter.20.cloned.1.call-start = ((), (), s32[]{:S(2)}) async-start(), calls=%async_computation.28 | async-start | bytes 19267584 | tf_op jit(solution)/shard_map/reduce_scatter | solution.py:227
  967.6 58.9 %reduce-scatter.18.cloned.1.call-start = ((), (), s32[]{:S(2)}) async-start(), calls=%async_computation.27 | async-start | bytes 3145728 | tf_op jit(solution)/shard_map/reduce_scatter | solution.py:155
  973.6 274.7 %all-reduce.3.cloned.1.call-start = ((), (), s32[]{:S(2)}) async-start(), calls=%async_computation.29 | async-start | bytes 12845056 | tf_op jit(solution)/shard_map/psum | solution.py:244
  990.2 14.3 %all-to-all-start.1 = ((bf16[2,256,512]{2,1,0:T(8,128)(2,1)}), bf16[2,256,512]{2,1,0:T(8,128)(2,1)S(1)}, u32[]{:S(2)}, u32[]{:S(2)}) async-start(bf16[2,256,512]{2,1,0:T(8,128)(2,1)} %bitcast.27), calls=%async_computation.7 | async-start | bytes 1048576 | tf_op jit(solution)/shard_map/all_to_all | solution.py:221
  1004.7 68.3 %copy-start.23 = (f32[256]{0:T(256)S(1)}, f32[256]{0:T(256)}, u32[]{:S(2)}) copy-start(f32[256]{0:T(256)} %copy-done.22) | copy-start | bytes 3076
  1004.7 68.3 %copy-start.5 = (f32[256,1024]{1,0:T(8,128)S(1)}, f32[256,1024]{1,0:T(8,128)}, u32[]{:S(2)}) copy-start(f32[256,1024]{1,0:T(8,128)} %get-tuple-element.264) | copy-start | bytes 3145732
  (43 other events, 496.3 us)
Sparse Core Ops, SparseCore 0:
  9.6 11.7 all-gather.17
  23.4 22.4 all-gather.13
  47.5 9.0 all-gather.21
  58.0 10.1 all-gather.15
  70.8 74.5 all-gather.19
  147.9 71.6 all-gather.23
  221.1 7.2 all-gather.25
  296.3 30.0 reduce-scatter.7
  328.1 11.7 all-gather.29
  341.9 22.4 all-gather.27
  366.0 11.7 all-gather.31
  379.3 12.8 all-gather.33
  397.8 33.4 reduce-scatter.9
  442.3 21.2 all-gather.35
  476.3 31.8 reduce-scatter.11
  512.5 21.2 all-gather.37
  769.4 88.4 reduce-scatter.13
  861.3 87.6 reduce-scatter.15
  967.7 21.5 reduce-scatter.19
  992.1 34.3 reduce-scatter.17
  1030.3 217.8 all-reduce.2
where the time goes:
time: 1280 us; the launch traced here: 1270 us
  waiting for transfers between devices  724 us (57%)
  matrix products  278 us (22%)
  other arithmetic  95.9 us (7%)
  blocking collectives  95.1 us (7%)
  local copies, waits for them, and re-layouts  45.4 us (4%)
  between operations  18.3 us (1%)
    psum x1, waiting for transfers between devices, on_device(): summed = lax.psum(piece, 'ctx').astype(jnp.float32)  173 us
    dot_general x31, matrix products, product_nt(): lax.dot_general(left, right, (((1,), (1,)), ((), ())), preferred_element_...  124 us
    all_gather x4, waiting for transfers between devices, spread(): return lax.all_gather(values, 'tp', axis=0, tiled=True)  91.5 us
    reduce_scatter x1, waiting for transfers between devices, on_device(): lax.psum_scatter(value_term.astype(jnp.bfloat16), 'ctx', scatter_dimensio...  88.5 us
    psum x2, blocking collectives, on_device(): lax.psum((local_error, jnp.sum(keep)), ('shard', 'ctx', 'tp'))  84.5 us
    reduce_scatter x4, waiting for transfers between devices, collect(): return lax.psum_scatter(terms, 'tp', scatter_dimension=0, tiled=True)  80.5 us
    dot_general x23, matrix products, product(): return jnp.dot(left, right, preferred_element_type=jnp.float32)  79.6 us
    dot_general x23, matrix products, product_tn(): lax.dot_general(left, right, (((0,), (0,)), ((), ())), preferred_element_...  75.3 us
  transfers between devices with their start and end apart: 22, of which 19 were waited for; matrix products, arithmetic and copies ran while one was open for 10% of the time, Pallas kernels for 0%

commit v1 on v0

v1 whole, which is shorter than its diff:
```python
import functools

import jax
import jax.numpy as jnp
from jax import lax
from jax.experimental import pallas as pl
from jax.experimental.pallas import tpu as pltpu
from jax.sharding import PartitionSpec as P

HEAD_DIM = 64
PAIR = 2 * HEAD_DIM
LN2 = 0.6931471805599453
QUERY_SCALE = HEAD_DIM ** (-0.5) / LN2
F32 = jnp.float32
BF16 = jnp.bfloat16
BOUNDARY = 256

epsilon = 1e-06


def rms_norm(values, gain):
    return values * lax.rsqrt(jnp.mean(values * values, axis=-1, keepdims=True) + epsilon) * gain


def dot(left, right, left_dim, right_dim):
    return lax.dot_general(
        left, right, (((left_dim,), (right_dim,)), ((), ())), preferred_element_type=F32
    )


def nn(left, right):
    return dot(left, right, 1, 0)


def nt(left, right):
    return dot(left, right, 1, 1)


def tn(left, right):
    return dot(left, right, 0, 0)


def split_heads(pair):
    lane = lax.broadcasted_iota(jnp.int32, (1, PAIR), 1)
    zero = jnp.zeros_like(pair)
    return [jnp.where(lane < HEAD_DIM, pair, zero), jnp.where(lane >= HEAD_DIM, pair, zero)]


def forward_kernel(
    step_keys, index_ref, q_ref, k_ref, v_ref, qmark_ref, kmark_ref, out_ref, lse_ref, vt_ref
):
    rows, length = q_ref.shape[0], k_ref.shape[0]
    index = index_ref[0]
    queries = split_heads(q_ref[...])
    vt_ref[...] = v_ref[...].T

    def step(masked):
        def body(at, state):
            start = pl.multiple_of(at * step_keys, step_keys)
            keys = k_ref[pl.ds(start, step_keys), :]
            if masked:
                allowed = kmark_ref[pl.ds(start, step_keys), :] <= qmark_ref[...]
            scores = [nt(keys, queries[h]) for h in range(2)]
            new = []
            for h in range(2):
                highest, total, out = state[3 * h : 3 * h + 3]
                score = scores[h]
                if masked:
                    score = jnp.where(allowed, score, -1e30)
                top = jnp.maximum(highest, jnp.max(score, axis=0, keepdims=True))
                power = jnp.exp2(score - top)
                shrink = jnp.exp2(highest - top)
                total = total * shrink + jnp.sum(power, axis=0, keepdims=True)
                values = vt_ref[pl.ds(HEAD_DIM * h, HEAD_DIM), pl.ds(start, step_keys)]
                new += [top, total, out * shrink + nn(values, power.astype(BF16))]
            return tuple(new)

        return body

    empty = (
        jnp.full((1, rows), -1e30, F32),
        jnp.zeros((1, rows), F32),
        jnp.zeros((HEAD_DIM, rows), F32),
    )
    full = (index * rows) // step_keys
    end = jnp.minimum(
        ((index + 1) * rows + BOUNDARY + step_keys - 1) // step_keys, length // step_keys
    )
    state = lax.fori_loop(full, end, step(True), empty + empty)
    state = lax.fori_loop(0, full, step(False), state)
    out = jnp.concatenate([state[2] / state[1], state[5] / state[4]], axis=0)
    out_ref[...] = out.T.astype(out_ref.dtype)
    lse_ref[0] = jnp.concatenate(
        [state[0] + jnp.log2(state[1]), state[3] + jnp.log2(state[4])], axis=0
    )


def attend_forward(index, queries, kv_all, qmark, kmark, step_keys=1024):
    rows, width = queries.shape
    length = kv_all.shape[0]
    pairs = width // PAIR
    return pl.pallas_call(
        functools.partial(forward_kernel, step_keys),
        grid_spec=pltpu.PrefetchScalarGridSpec(
            num_scalar_prefetch=1,
            grid=(pairs,),
            in_specs=[
                pl.BlockSpec((rows, PAIR), lambda h, s: (0, h)),
                pl.BlockSpec((length, PAIR), lambda h, s: (0, h)),
                pl.BlockSpec((length, PAIR), lambda h, s: (0, pairs + h)),
                pl.BlockSpec((1, rows), lambda h, s: (0, 0)),
                pl.BlockSpec((length, 1), lambda h, s: (0, 0)),
            ],
            out_specs=[
                pl.BlockSpec((rows, PAIR), lambda h, s: (0, h)),
                pl.BlockSpec((1, 2, rows), lambda h, s: (h, 0, 0)),
            ],
            scratch_shapes=[pltpu.VMEM((PAIR, length), BF16)],
        ),
        out_shape=[
            jax.ShapeDtypeStruct((rows, width), BF16),
            jax.ShapeDtypeStruct((pairs, 2, rows), F32),
        ],
        compiler_params=pltpu.CompilerParams(vmem_limit_bytes=56 << 20),
        cost_estimate=pl.CostEstimate(
            flops=4 * rows * length * width,
            bytes_accessed=4 * length * width,
            transcendentals=rows * length * width // HEAD_DIM,
        ),
    )(index, queries, kv_all, kv_all, qmark, kmark)


def delta_kernel(grad_ref, out_ref, delta_ref):
    terms = (grad_ref[...].astype(F32) * out_ref[...].astype(F32)).T
    delta_ref[0] = jnp.concatenate(
        [
            jnp.sum(terms[:HEAD_DIM], axis=0, keepdims=True),
            jnp.sum(terms[HEAD_DIM:], axis=0, keepdims=True),
        ],
        axis=0,
    )


def attend_delta(grad, out):
    rows, width = grad.shape
    pairs = width // PAIR
    return pl.pallas_call(
        delta_kernel,
        grid=(pairs,),
        in_specs=[pl.BlockSpec((rows, PAIR), lambda h: (0, h))] * 2,
        out_specs=pl.BlockSpec((1, 2, rows), lambda h: (h, 0, 0)),
        out_shape=jax.ShapeDtypeStruct((pairs, 2, rows), F32),
    )(grad, out)


def query_kernel(
    step_keys,
    index_ref,
    q_ref,
    grad_ref,
    k_ref,
    v_ref,
    lse_ref,
    delta_ref,
    qmark_ref,
    kmark_ref,
    out_ref,
    kt_ref,
):
    rows, length = q_ref.shape[0], k_ref.shape[0]
    index = index_ref[0]
    queries, grads = split_heads(q_ref[...]), split_heads(grad_ref[...])
    kt_ref[...] = k_ref[...].T

    def step(masked):
        def body(at, state):
            start = pl.multiple_of(at * step_keys, step_keys)
            keys = k_ref[pl.ds(start, step_keys), :]
            values = v_ref[pl.ds(start, step_keys), :]
            if masked:
                allowed = kmark_ref[pl.ds(start, step_keys), :] <= qmark_ref[...]
            new = []
            for h in range(2):
                score = nt(keys, queries[h])
                slope = nt(values, grads[h])
                prob = jnp.exp2(score - lse_ref[0, h : h + 1, :])
                if masked:
                    prob = jnp.where(allowed, prob, 0.0)
                grad = (prob * (slope - delta_ref[0, h : h + 1, :])).astype(BF16)
                turned = kt_ref[pl.ds(HEAD_DIM * h, HEAD_DIM), pl.ds(start, step_keys)]
                new.append(state[h] + nn(turned, grad))
            return tuple(new)

        return body

    empty = jnp.zeros((HEAD_DIM, rows), F32)
    full = (index * rows) // step_keys
    end = jnp.minimum(
        ((index + 1) * rows + BOUNDARY + step_keys - 1) // step_keys, length // step_keys
    )
    state = lax.fori_loop(full, end, step(True), (empty, empty))
    state = lax.fori_loop(0, full, step(False), state)
    out_ref[...] = (jnp.concatenate(state, axis=0).T * HEAD_DIM ** (-0.5)).astype(out_ref.dtype)


def query_gradient(index, queries, grad, kv_all, lse, delta, qmark, kmark, step_keys=1024):
    rows, width = queries.shape
    length = kv_all.shape[0]
    pairs = width // PAIR
    return pl.pallas_call(
        functools.partial(query_kernel, step_keys),
        grid_spec=pltpu.PrefetchScalarGridSpec(
            num_scalar_prefetch=1,
            grid=(pairs,),
            in_specs=[
                pl.BlockSpec((rows, PAIR), lambda h, s: (0, h)),
                pl.BlockSpec((rows, PAIR), lambda h, s: (0, h)),
                pl.BlockSpec((length, PAIR), lambda h, s: (0, h)),
                pl.BlockSpec((length, PAIR), lambda h, s: (0, pairs + h)),
                pl.BlockSpec((1, 2, rows), lambda h, s: (h, 0, 0)),
                pl.BlockSpec((1, 2, rows), lambda h, s: (h, 0, 0)),
                pl.BlockSpec((1, rows), lambda h, s: (0, 0)),
                pl.BlockSpec((length, 1), lambda h, s: (0, 0)),
            ],
            out_specs=pl.BlockSpec((rows, PAIR), lambda h, s: (0, h)),
            scratch_shapes=[pltpu.VMEM((PAIR, length), BF16)],
        ),
        out_shape=jax.ShapeDtypeStruct((rows, width), BF16),
        compiler_params=pltpu.CompilerParams(vmem_limit_bytes=56 << 20),
        cost_estimate=pl.CostEstimate(
            flops=6 * rows * length * width,
            bytes_accessed=4 * length * width,
            transcendentals=rows * length * width // HEAD_DIM,
        ),
    )(index, queries, grad, kv_all, kv_all, lse, delta, qmark, kmark)


def key_kernel(
    step_queries,
    index_ref,
    k_ref,
    v_ref,
    q_ref,
    grad_ref,
    lse_ref,
    delta_ref,
    qmark_ref,
    kmark_ref,
    dk_ref,
    dv_ref,
):
    rows, length = k_ref.shape[0], q_ref.shape[0]
    index = index_ref[0]
    keys, values = split_heads(k_ref[...]), split_heads(v_ref[...])

    def step(masked):
        def body(at, state):
            start = pl.multiple_of(at * step_queries, step_queries)
            queries = q_ref[pl.ds(start, step_queries), :]
            grads = grad_ref[pl.ds(start, step_queries), :]
            if masked:
                allowed = kmark_ref[...] <= qmark_ref[:, pl.ds(start, step_queries)]
            new = []
            for h in range(2):
                score = nt(keys[h], queries)
                slope = nt(values[h], grads)
                prob = jnp.exp2(score - lse_ref[0, h : h + 1, pl.ds(start, step_queries)])
                if masked:
                    prob = jnp.where(allowed, prob, 0.0)
                grad = prob * (slope - delta_ref[0, h : h + 1, pl.ds(start, step_queries)])
                new += [
                    state[2 * h] + nn(grad.astype(BF16), queries),
                    state[2 * h + 1] + nn(prob.astype(BF16), grads),
                ]
            return tuple(new)

        return body

    empty = jnp.zeros((rows, PAIR), F32)
    first = jnp.maximum((index * rows - BOUNDARY) // step_queries, 0)
    own = ((index + 1) * rows + step_queries - 1) // step_queries
    state = lax.fori_loop(first, own, step(True), (empty,) * 4)
    state = lax.fori_loop(own, length // step_queries, step(False), state)
    lane = lax.broadcasted_iota(jnp.int32, (1, PAIR), 1)
    dk_ref[...] = (jnp.where(lane < HEAD_DIM, state[0], state[2]) * LN2).astype(dk_ref.dtype)
    dv_ref[...] = jnp.where(lane < HEAD_DIM, state[1], state[3]).astype(dv_ref.dtype)


def key_gradient(index, kv, q_all, grad_all, lse, delta, qmark, kmark, step_queries=512):
    rows = kv.shape[0]
    length, width = q_all.shape
    pairs = width // PAIR
    return pl.pallas_call(
        functools.partial(key_kernel, step_queries),
        grid_spec=pltpu.PrefetchScalarGridSpec(
            num_scalar_prefetch=1,
            grid=(pairs,),
            in_specs=[
                pl.BlockSpec((rows, PAIR), lambda h, s: (0, h)),
                pl.BlockSpec((rows, PAIR), lambda h, s: (0, pairs + h)),
                pl.BlockSpec((length, PAIR), lambda h, s: (0, h)),
                pl.BlockSpec((length, PAIR), lambda h, s: (0, h)),
                pl.BlockSpec((1, 2, length), lambda h, s: (h, 0, 0)),
                pl.BlockSpec((1, 2, length), lambda h, s: (h, 0, 0)),
                pl.BlockSpec((1, length), lambda h, s: (0, 0)),
                pl.BlockSpec((rows, 1), lambda h, s: (0, 0)),
            ],
            out_specs=[pl.BlockSpec((rows, PAIR), lambda h, s: (0, h))] * 2,
        ),
        out_shape=[jax.ShapeDtypeStruct((rows, width), BF16)] * 2,
        compiler_params=pltpu.CompilerParams(vmem_limit_bytes=56 << 20),
        cost_estimate=pl.CostEstimate(
            flops=8 * rows * length * width,
            bytes_accessed=4 * length * width,
            transcendentals=rows * length * width // HEAD_DIM,
        ),
    )(index, kv, kv, q_all, grad_all, lse, delta, qmark, kmark)


def on_device(
    tokens,
    value_first,
    teacher,
    valid,
    blocks,
    gain_attn,
    gain_ffn,
    w_query,
    w_key,
    w_value,
    w_out,
    w_gate,
    w_up,
    w_down,
):
    width = tokens.shape[2]
    own_rows = tokens.shape[1]
    sizes = {axis: lax.axis_size(axis) for axis in ("shard", "ctx", "tp")}
    shard, ctx, tp = (lax.axis_index(axis) for axis in ("shard", "ctx", "tp"))
    group_rows = own_rows * sizes["tp"]
    half = w_query.shape[1]
    part = w_query.shape[0]

    def flip(values, axis, bit=1):
        return lax.ppermute(values, axis, [(i, i ^ bit) for i in range(sizes[axis])])

    def tree_sum(values):
        for axis, size in sizes.items():
            bit = 1
            while bit < size:
                values = values + flip(values, axis, bit)
                bit *= 2
        return values

    def in_order(position, mine, other, axis):
        first = position == 0
        return jnp.concatenate(
            [jnp.where(first, mine, other), jnp.where(first, other, mine)], axis=axis
        )

    def shard_gather(values, axis):
        if sizes["shard"] == 2:
            return in_order(shard, values, flip(values, "shard"), axis)
        return lax.all_gather(values, "shard", axis=axis, tiled=True)

    def rows_of(values, position):
        return lax.dynamic_slice_in_dim(values, position * own_rows, own_rows, 0)

    def cols_of(values, position, size):
        return lax.dynamic_slice_in_dim(values, position * size, size, 1)

    mine = tokens.reshape(own_rows, width)
    first_own = value_first.reshape(own_rows, width)
    key_marks = blocks.reshape(-1)
    query_marks = lax.dynamic_slice_in_dim(key_marks, ctx * group_rows, group_rows, 0)
    keep = valid.reshape(own_rows).astype(F32)
    index = ctx.reshape(1).astype(jnp.int32)

    theirs = flip(mine, "tp")
    first_theirs = flip(cols_of(first_own, 1 - tp, half), "tp")
    weight_qkv = shard_gather(jnp.concatenate([w_query, w_key, w_value], axis=1), 0)
    count = tree_sum(jnp.broadcast_to(jnp.sum(keep), (1, 128)))[0, 0]

    theirs, w_gate, w_up, w_down, w_out = lax.optimization_barrier(
        (theirs, w_gate, w_up, w_down, w_out)
    )
    gates = [shard_gather(w_gate, 0), shard_gather(flip(w_gate, "tp"), 0)]
    ups = [shard_gather(w_up, 0), shard_gather(flip(w_up, "tp"), 0)]
    downs = [shard_gather(w_down, 1), shard_gather(flip(w_down, "tp"), 1)]
    outs = [shard_gather(w_out, 1), shard_gather(flip(w_out, "tp"), 1)]

    group = in_order(tp, mine, theirs, 0).astype(F32)
    normed_one = rms_norm(group, gain_attn).astype(BF16)
    first_group = in_order(tp, cols_of(first_own, tp, half), first_theirs, 0).astype(F32)
    qkv = nn(normed_one, weight_qkv)
    queries = (qkv[:, :half] * QUERY_SCALE).astype(BF16)
    kv = jnp.concatenate(
        [qkv[:, half : 2 * half], 0.5 * qkv[:, 2 * half :] + 0.5 * first_group], axis=1
    ).astype(BF16)
    kv_all = lax.all_gather(kv, "ctx", axis=0, tiled=True)
    qmark, kmark = query_marks.reshape(1, -1), key_marks.reshape(-1, 1)
    attended, lse = attend_forward(index, queries, kv_all, qmark, kmark)

    q_all = lax.all_gather(queries, "ctx", axis=0, tiled=True)
    att = [rows_of(attended, tp), flip(rows_of(attended, 1 - tp), "tp")]
    inputs = mine.astype(F32)
    hidden = inputs + (nn(att[0], outs[0]) + nn(att[1], outs[1]))
    normed_two = rms_norm(hidden, gain_ffn).astype(BF16)
    gate = [nn(normed_two, w) for w in gates]
    up = [nn(normed_two, w) for w in ups]
    logistic = [jax.nn.sigmoid(g) for g in gate]
    act = [(g * s * u).astype(BF16) for g, s, u in zip(gate, logistic, up)]
    final = hidden + (nn(act[0], downs[0]) + nn(act[1], downs[1]))
    difference = final - teacher.reshape(own_rows, width).astype(F32)
    local_error = jnp.sum(jnp.mean(difference * difference, axis=1) * keep)
    token_total = group_rows * sizes["ctx"] * sizes["shard"]
    grad_final = token_total / count * keep[:, None] * difference
    grad_round = grad_final.astype(BF16)
    grad_act = [nt(grad_round, w) for w in downs]
    grad_gate = [
        (a * u * s * (1.0 + g * (1.0 - s))).astype(BF16)
        for a, u, s, g in zip(grad_act, up, logistic, gate)
    ]
    grad_up = [(a * g * s).astype(BF16) for a, g, s in zip(grad_act, gate, logistic)]
    grad_two = (
        nt(grad_gate[0], gates[0])
        + nt(grad_gate[1], gates[1])
        + nt(grad_up[0], ups[0])
        + nt(grad_up[1], ups[1])
    )
    hidden_part, gain_ffn_term = jax.vjp(rms_norm, hidden, gain_ffn)[1](grad_two)
    grad_hidden = grad_final + hidden_part
    hidden_round = grad_hidden.astype(BF16)
    grad_att = [nt(hidden_round, w).astype(BF16) for w in outs]
    grad_attended = in_order(tp, grad_att[0], flip(grad_att[1], "tp"), 0)
    delta = attend_delta(grad_attended, attended)
    grad_all = lax.all_gather(grad_attended, "ctx", axis=0, tiled=True)
    stats = lax.all_gather(jnp.stack([lse, delta]), "ctx", axis=3, tiled=True)

    def reduce_shard(left, right, slice_left):
        if sizes["shard"] != 2:
            return lax.psum_scatter(
                tn(left, right).astype(BF16),
                "shard",
                scatter_dimension=0 if slice_left else 1,
                tiled=True,
            ).astype(F32)
        if slice_left:
            kept, sent = (
                tn(cols_of(left, shard, part), right),
                tn(cols_of(left, 1 - shard, part), right),
            )
        else:
            kept, sent = (
                tn(left, cols_of(right, shard, part)),
                tn(left, cols_of(right, 1 - shard, part)),
            )
        return kept + flip(sent.astype(BF16), "shard").astype(F32)

    def reduce_pair(lefts, rights, slice_left):
        other = flip(reduce_shard(lefts[1], rights[1], slice_left).astype(BF16), "tp")
        own = reduce_shard(lefts[0], rights[0], slice_left)
        return (own + other.astype(F32)).astype(BF16)

    down_part = reduce_pair(act, [grad_round] * 2, False)
    gate_part = reduce_pair([normed_two] * 2, grad_gate, True)
    up_part = reduce_pair([normed_two] * 2, grad_up, True)
    out_part = reduce_pair(att, [hidden_round] * 2, False)
    w_down_grad, w_gate_grad, w_up_grad, w_out_grad = lax.psum(
        (down_part, gate_part, up_part, out_part), "ctx"
    )

    query_grad = query_gradient(
        index, queries, grad_attended, kv_all, lse, delta, qmark, kmark
    )
    key_grad, value_grad = key_gradient(
        index,
        kv,
        q_all,
        grad_all,
        stats[0],
        stats[1],
        key_marks.reshape(1, -1),
        query_marks.reshape(-1, 1),
    )
    value_half = (0.5 * value_grad.astype(F32)).astype(BF16)
    grads = jnp.concatenate([query_grad, key_grad, value_half], axis=1)
    grad_one_theirs = flip(nt(rows_of(grads, 1 - tp), weight_qkv).astype(BF16), "tp")
    grad_one = nt(rows_of(grads, tp), weight_qkv) + grad_one_theirs.astype(F32)
    input_part, gain_attn_term = jax.vjp(rms_norm, inputs, gain_attn)[1](grad_one)
    tokens_grad = grad_hidden + input_part
    first_grad = in_order(
        tp, rows_of(value_half, tp), flip(rows_of(value_half, 1 - tp), "tp"), 1
    ).astype(F32)
    qkv_part = reduce_shard(normed_one, grads, True).astype(BF16)
    qkv_grad = lax.psum(qkv_part, "ctx").astype(F32)

    small = jnp.concatenate(
        [gain_attn_term, gain_ffn_term, jnp.broadcast_to(local_error, (128,))]
    )
    small = tree_sum(small.reshape(1, -1)).reshape(-1)
    return (
        final.astype(BF16).reshape(1, own_rows, width),
        small[2 * width] / count,
        tokens_grad.reshape(1, own_rows, width),
        first_grad.reshape(1, own_rows, width),
        small[:width],
        small[width : 2 * width],
        qkv_grad[:, :half],
        qkv_grad[:, half : 2 * half],
        qkv_grad[:, 2 * half :],
        w_out_grad.astype(F32),
        w_gate_grad.astype(F32),
        w_up_grad.astype(F32),
        w_down_grad.astype(F32),
    )


def solution(mesh):
    rows = P("shard", ("ctx", "tp"), None)
    wide, tall = P("shard", "tp"), P("tp", "shard")
    return jax.shard_map(
        on_device,
        mesh=mesh,
        in_specs=(
            rows,
            rows,
            rows,
            P("shard", ("ctx", "tp")),
            P("shard", None),
            P(),
            P(),
            wide,
            wide,
            wide,
            tall,
            wide,
            wide,
            tall,
        ),
        out_specs=(rows, P(), rows, rows, P(), P(), wide, wide, wide, tall, wide, wide, tall),
        check_vma=False,
    )
```

time: 1280 us -> 688 us (0.54)
  waiting for transfers between devices: 724 us -> 342 us
  matrix products: 278 us -> 54.1 us
  Pallas kernels: 0 us -> 79.2 us
  starting transfers between devices: 5.54 us -> 55.3 us
  blocking collectives: 95.1 us -> 51.4 us
  other arithmetic: 95.9 us -> 56.1 us
  local copies, waits for them, and re-layouts: 45.4 us -> 23.5 us
    all_gather x13 -> x3, waiting for transfers between devices: 278 us -> 0.01 us  [the longest x1 0.01 us: on_device(): kv_all = lax.all_gather(kv, 'ctx', axis=0, tiled=True)]
    reduce_scatter x7 -> x0, waiting for transfers between devices: 259 us -> none  [the longest x1 88.5 us: on_device(): lax.psum_scatter(value_term.astype(jnp.bfloat16), 'ctx', scatter_dimensio...]
    dot_general x77 -> x37, matrix products: 278 us -> 54.1 us  [dot(): lax.dot_general(left, right, (((left_dim,), (right_dim,)), ((), ())), pre...]
    ppermute x0 -> x42, waiting for transfers between devices: none -> 163 us  [flip(): lax.ppermute(values, axis, [(i, i ^ bit) for i in range(sizes[axis])])]
    psum x2 -> x0, blocking collectives: 84.5 us -> none  [on_device(): lax.psum((local_error, jnp.sum(keep)), ('shard', 'ctx', 'tp'))]
    pallas_call x0 -> x4, Pallas kernels: none -> 79.2 us  [the longest x1 49.9 us: key_gradient(): pl.pallas_call(functools.partial(key_kernel, step_queries), grid_spec=plt...]
    ppermute x0 -> x42, starting transfers between devices: none -> 55.1 us  [flip(): lax.ppermute(values, axis, [(i, i ^ bit) for i in range(sizes[axis])])]
    convert_element_type x17 -> x14, other arithmetic: 75.2 us -> 23.4 us  [the longest x4 11.9 us: reduce_pair(): return (own + other.astype(F32)).astype(BF16)]
  transfers between devices with their start and end apart: 22 -> 46, of which waited for: 19 -> 17; matrix products, arithmetic and copies ran while one was open for 10% -> 15% of each run, Pallas kernels for 0% -> 12%
where the time goes in v1:
time: 688 us; the launch traced here: 679 us
  waiting for transfers between devices  342 us (50%)
  Pallas kernels  79.2 us (12%)
  other arithmetic  56.1 us (8%)
  starting transfers between devices  55.3 us (8%)
  matrix products  54.1 us (8%)
  blocking collectives  51.4 us (7%)
  local copies, waits for them, and re-layouts  23.5 us (3%)
  between operations  16.8 us (2%)
    psum x1, waiting for transfers between devices, on_device(): qkv_grad = lax.psum(qkv_part, 'ctx').astype(F32)  179 us
    ppermute x42, waiting for transfers between devices, flip(): lax.ppermute(values, axis, [(i, i ^ bit) for i in range(sizes[axis])])  163 us
    ppermute x42, starting transfers between devices, flip(): lax.ppermute(values, axis, [(i, i ^ bit) for i in range(sizes[axis])])  55.1 us
    dot_general x37, matrix products, dot(): lax.dot_general(left, right, (((left_dim,), (right_dim,)), ((), ())), pre...  54.1 us
    all_gather x1, blocking collectives, on_device(): stats = lax.all_gather(jnp.stack([lse, delta]), 'ctx', axis=3, tiled=True)  51.4 us
    pallas_call x1, Pallas kernels, key_gradient(): pl.pallas_call(functools.partial(key_kernel, step_queries), grid_spec=plt...  49.9 us
    select_n x12, other arithmetic, in_order(): jnp.where(first, mine, other)  23.7 us
  transfers between devices with their start and end apart: 46, of which 17 were waited for; matrix products, arithmetic and copies ran while one was open for 15% of the time, Pallas kernels for 12%

profile of v1, /device:TPU:0, one launch (start us, length us, event | category | flops | bytes accessed | tf_op | source)
XLA Modules:
  0.0 678.9 jit_solution(7207915488971028250)
XLA Ops:
  13.5 17.4 %collective-permute-done.2 = bf16[256,512]{1,0:T(8,128)(2,1)S(1)} collective-permute-done((bf16[256,512]{1,0:T(8,128)(2,1)}, bf16[256,512]{1,0:T(8,128)(2,1)S(1)}, u32[]{:S(2)}, u32[]{:S(2)}) %collective-permute-start.2) | collective-permute-done | bytes 262176 | tf_op jit(solution)/shard_map/ppermute | solution.py:345
  56.7 48.4 %collective-permute-done.20 = f32[1,128]{1,0:T(1,128)S(1)} collective-permute-done((f32[1,128]{1,0:T(1,128)S(1)}, f32[1,128]{1,0:T(1,128)S(1)}, u32[]{:S(2)}, u32[]{:S(2)}) %collective-permute-start.20) | collective-permute-done | bytes 544 | tf_op jit(solution)/shard_map/ppermute | solution.py:345
  105.1 10.8 %collective-permute-done.5 = bf16[512,512]{1,0:T(8,128)(2,1)} collective-permute-done((bf16[512,512]{1,0:T(8,128)(2,1)S(1)}, bf16[512,512]{1,0:T(8,128)(2,1)}, u32[]{:S(2)}, u32[]{:S(2)}) %collective-permute-start.5) | collective-permute-done | bytes 524320 | tf_op jit(solution)/shard_map/ppermute | solution.py:345
  126.0 3.3 broadcast_select_fusion.13
  129.3 3.4 broadcast_select_fusion.11
  132.6 23.0 %collective-permute-done.14 = bf16[1408,512]{1,0:T(8,128)(2,1)} collective-permute-done((bf16[1408,512]{1,0:T(8,128)(2,1)}, bf16[1408,512]{1,0:T(8,128)(2,1)}, u32[]{:S(2)}, u32[]{:S(2)}) %collective-permute-start.14) | collective-permute-done | bytes 1441824 | tf_op jit(solution)/shard_map/ppermute | solution.py:345
  158.8 3.2 broadcast_select_fusion.9
  162.0 3.3 broadcast_select_fusion.7
  165.3 12.2 %shard_map.237 = (bf16[512,512]{1,0:T(8,128)(2,1)}, f32[4,2,512]{2,1,0:T(2,128)}) custom-call(s32[1]{0:T(128)} %bitcast.1.index_ref, bf16[512,512]{1,0:T(8,128)(2,1)} %get-tuple-element.43.q_ref, bf16[4096,1024]{1,0:T(8,128)(2,1)} %all-gather.4.cloned.1.call-done.k_ref.v_ref, bf16[4096,1024]{1,0:T(8,128)(2,1)} %all-gather.4.cloned.1.call-done.k_ref.v_ref, ...), custom_call_target="tpu_custom_call" | custom-call | flops 4294967296 | bytes 8388608 | tf_op jit(solution)/shard_map/pallas_call | solution.py:102
  182.3 5.0 collective-permute-done.4
  212.6 5.4 collective-permute-done.21
  239.8 3.5 shard_map.238.delta_ref
  244.0 51.4 %all_gather.15 = f32[2,4,2,4096]{3,2,1,0:T(2,128)S(1)} all-gather(f32[2,4,2,512]{3,2,1,0:T(2,128)S(1)} %pad_maximum_fusion.42), channel_id=1, replica_groups=mesh['shard'=2,'ctx'=8,'tp'=2] {'ctx'}, dimensions={3}, use_global_device_ids=true | all-gather | bytes 294912 | tf_op jit(solution)/shard_map/all_gather | solution.py:438
  299.3 13.6 %shard_map.239 = bf16[512,512]{1,0:T(8,128)(2,1)} custom-call(s32[1]{0:T(128)} %bitcast.1.index_ref, bf16[512,512]{1,0:T(8,128)(2,1)} %get-tuple-element.43.q_ref, bf16[512,512]{1,0:T(8,128)(2,1)} %pad_maximum_fusion.41.grad_ref, bf16[4096,1024]{1,0:T(8,128)(2,1)} %all-gather.4.cloned.1.call-done.k_ref.v_ref, ...), custom_call_target="tpu_custom_call" | custom-call | flops 6442450944 | bytes 8388608 | tf_op jit(solution)/shard_map/pallas_call | solution.py:210
  327.0 49.9 %shard_map.240 = (bf16[512,512]{1,0:T(8,128)(2,1)}, bf16[512,512]{1,0:T(8,128)(2,1)}) custom-call(s32[1]{0:T(128)} %bitcast.1.index_ref, bf16[512,1024]{1,0:T(8,128)(2,1)} %pad_maximum_fusion.31.k_ref.v_ref, bf16[512,1024]{1,0:T(8,128)(2,1)} %pad_maximum_fusion.31.k_ref.v_ref, bf16[4096,512]{1,0:T(8,128)(2,1)} %all-gather.6.cloned.1.call-done.q_ref, ...), custom_call_target="tpu_custom_call" | custom-call | flops 8589934592 | bytes 8388608 | tf_op jit(solution)/shard_map/pallas_call | solution.py:293
  381.0 3.5 add_convert_fusion.5
  384.4 3.3 add_convert_fusion.3
  387.8 26.9 %collective-permute-done.41 = bf16[1408,512]{1,0:T(8,128)(2,1)S(1)} collective-permute-done((bf16[1408,512]{1,0:T(8,128)(2,1)S(1)}, bf16[1408,512]{1,0:T(8,128)(2,1)S(1)}, u32[]{:S(2)}, u32[]{:S(2)}) %collective-permute-start.41) | collective-permute-done | bytes 1441824 | tf_op jit(solution)/shard_map/ppermute | solution.py:345
  425.4 12.1 %collective-permute-done.22 = bf16[256,1024]{1,0:T(8,128)(2,1)S(1)} collective-permute-done((bf16[256,1024]{1,0:T(8,128)(2,1)S(1)}, bf16[256,1024]{1,0:T(8,128)(2,1)S(1)}, u32[]{:S(2)}, u32[]{:S(2)}) %collective-permute-start.22) | collective-permute-done | bytes 524320 | tf_op jit(solution)/shard_map/ppermute | solution.py:345
  440.7 9.0 %collective-permute-start.24 = (f32[1,2176]{1,0:T(1,128)S(1)}, f32[1,2176]{1,0:T(1,128)S(1)}, u32[]{:S(2)}, u32[]{:S(2)}) collective-permute-start(f32[1,2176]{1,0:T(1,128)S(1)} %reshape_add_fusion), channel_id=1, source_target_pairs={{0,2},{2,0},{4,6},{6,4},{8,10},{10,8},{12,14},{14,12},{1,3},{3,1},... | collective-permute-start | bytes 26120 | tf_op jit(solution)/shard_map/ppermute | solution.py:345
  451.5 5.3 collective-permute-start.25
  459.0 13.0 %collective-permute-start.26 = (f32[1,2176]{1,0:T(1,128)S(1)}, f32[1,2176]{1,0:T(1,128)S(1)}, u32[]{:S(2)}, u32[]{:S(2)}) collective-permute-start(f32[1,2176]{1,0:T(1,128)S(1)} %add.228), channel_id=1, source_target_pairs={{0,8},{2,10},{4,12},{6,14},{8,0},{10,2},{12,4},{14,6},{1,9},{3,11}... | collective-permute-start | bytes 26120 | tf_op jit(solution)/shard_map/ppermute | solution.py:345
  471.9 3.5 collective-permute-done.26
  481.0 179.2 %all-reduce.3.cloned.1.call-done = (bf16[512,1536]{1,0:T(8,128)(2,1)}, bf16[512,512]{1,0:T(8,128)(2,1)}, bf16[512,1408]{1,0:T(8,128)(2,1)}, bf16[512,1408]{1,0:T(8,128)(2,1)}, bf16[1408,512]{1,0:T(8,128)(2,1)}) async-done(((bf16[512,1536]{1,0:T(8,128)(2,1)}, bf16[512,512]{1,0:T(8,128)(2,1)}, bf16[512,1408]{1,0:T(8,128)(2,1)}, bf16[512,1408]{1,0:T(8,128)(2,1)}, bf16[1408,512]{1,0:T(8,128)(2,1)}), ...) | async-done | bytes 6422544 | tf_op jit(solution)/shard_map/psum | solution.py:496
  (340 shorter events, 152.7 us)
Async XLA Ops:
  7.2 158.1 %all-gather.4.cloned.1.call-start = ((), (), s32[]{:S(2)}) async-start(), calls=%async_computation | async-start | bytes 9437184 | tf_op jit(solution)/shard_map/all_gather | solution.py:400
  38.2 288.7 %all-gather.6.cloned.1.call-start = ((), (), s32[]{:S(2)}) async-start(), calls=%async_computation.1 | async-start | bytes 4718592 | tf_op jit(solution)/shard_map/all_gather | solution.py:404
  39.6 81.8 %collective-permute-start.10 = (bf16[512,1408]{1,0:T(8,128)(2,1)S(1)}, bf16[512,1408]{1,0:T(8,128)(2,1)}, u32[]{:S(2)}, u32[]{:S(2)}) collective-permute-start(bf16[512,1408]{1,0:T(8,128)(2,1)S(1)} %copy-done.34), channel_id=1, source_target_pairs={{0,1},{1,0},{2,3},{3,2},{4,5},{5,4},{6,7},{7,6},{8,9},{9,8},{10,11... | collective-permute-start | bytes 4325384 | tf_op jit(solution)/shard_map/ppermute | solution.py:345
  43.7 81.9 %collective-permute-start.7 = (bf16[512,1408]{1,0:T(8,128)(2,1)S(1)}, bf16[512,1408]{1,0:T(8,128)(2,1)}, u32[]{:S(2)}, u32[]{:S(2)}) collective-permute-start(bf16[512,1408]{1,0:T(8,128)(2,1)S(1)} %copy-done.34), channel_id=1, source_target_pairs={{0,16},{16,0},{1,17},{17,1},{2,18},{18,2},{3,19},{19,3},{4,20},{20... | collective-permute-start | bytes 4325384 | tf_op jit(solution)/shard_map/ppermute | solution.py:345
  43.7 81.7 %collective-permute-start.12 = (bf16[512,1408]{1,0:T(8,128)(2,1)}, bf16[512,1408]{1,0:T(8,128)(2,1)}, u32[]{:S(2)}, u32[]{:S(2)}) collective-permute-start(bf16[512,1408]{1,0:T(8,128)(2,1)} %param.26), channel_id=1, source_target_pairs={{0,1},{1,0},{2,3},{3,2},{4,5},{5,4},{6,7},{7,6},{8,9},{9,8},{10,11... | collective-permute-start | bytes 4325384 | tf_op jit(solution)/shard_map/ppermute | solution.py:345
  54.7 50.4 %collective-permute-start.20 = (f32[1,128]{1,0:T(1,128)S(1)}, f32[1,128]{1,0:T(1,128)S(1)}, u32[]{:S(2)}, u32[]{:S(2)}) collective-permute-start(f32[1,128]{1,0:T(1,128)S(1)} %add.217), channel_id=1, source_target_pairs={{0,1},{1,0},{2,3},{3,2},{4,5},{5,4},{6,7},{7,6},{8,9},{9,8},{10,11... | collective-permute-start | bytes 1544 | tf_op jit(solution)/shard_map/ppermute | solution.py:345
  56.1 59.8 %collective-permute-start.5 = (bf16[512,512]{1,0:T(8,128)(2,1)S(1)}, bf16[512,512]{1,0:T(8,128)(2,1)}, u32[]{:S(2)}, u32[]{:S(2)}) collective-permute-start(bf16[512,512]{1,0:T(8,128)(2,1)S(1)} %copy-done.52), channel_id=1, source_target_pairs={{0,1},{1,0},{2,3},{3,2},{4,5},{5,4},{6,7},{7,6},{8,9},{9,8},{10,11... | collective-permute-start | bytes 1572872 | tf_op jit(solution)/shard_map/ppermute | solution.py:345
  121.3 34.4 %collective-permute-start.9 = (bf16[1408,512]{1,0:T(8,128)(2,1)}, bf16[1408,512]{1,0:T(8,128)(2,1)}, u32[]{:S(2)}, u32[]{:S(2)}) collective-permute-start(bf16[1408,512]{1,0:T(8,128)(2,1)} %param.27), channel_id=1, source_target_pairs={{0,16},{16,0},{1,17},{17,1},{2,18},{18,2},{3,19},{19,3},{4,20},{20... | collective-permute-start | bytes 4325384 | tf_op jit(solution)/shard_map/ppermute | solution.py:345
  121.5 34.2 %collective-permute-start.14 = (bf16[1408,512]{1,0:T(8,128)(2,1)}, bf16[1408,512]{1,0:T(8,128)(2,1)}, u32[]{:S(2)}, u32[]{:S(2)}) collective-permute-start(bf16[1408,512]{1,0:T(8,128)(2,1)} %param.27), channel_id=1, source_target_pairs={{0,1},{1,0},{2,3},{3,2},{4,5},{5,4},{6,7},{7,6},{8,9},{9,8},{10,11... | collective-permute-start | bytes 4325384 | tf_op jit(solution)/shard_map/ppermute | solution.py:345
  125.3 201.6 %all-gather.8.cloned.1.call-start = ((), (), s32[]{:S(2)}) async-start(), calls=%async_computation.2 | async-start | bytes 4718592 | tf_op jit(solution)/shard_map/all_gather | solution.py:437
  125.5 36.5 %collective-permute-start.13 = (bf16[512,1408]{1,0:T(8,128)(2,1)}, bf16[512,1408]{1,0:T(8,128)(2,1)S(1)}, u32[]{:S(2)}, u32[]{:S(2)}) collective-permute-start(bf16[512,1408]{1,0:T(8,128)(2,1)} %collective-permute-done.12), channel_id=1, source_target_pairs={{0,16},{16,0},{1,17},{17,1},{2,18},{18,2},{3,19},{19,3},{4,20},{20... | collective-permute-start | bytes 4325384 | tf_op jit(solution)/shard_map/ppermute | solution.py:345
  218.9 441.3 %all-reduce.3.cloned.1.call-start = ((), (), s32[]{:S(2)}) async-start(), calls=%async_computation.3 | async-start | bytes 12845056 | tf_op jit(solution)/shard_map/psum | solution.py:496
  221.0 75.1 %collective-permute-start.31 = (bf16[512,512]{1,0:T(8,128)(2,1)}, bf16[512,512]{1,0:T(8,128)(2,1)}, u32[]{:S(2)}, u32[]{:S(2)}) collective-permute-start(bf16[512,512]{1,0:T(8,128)(2,1)} %convolution_convert_fusion.7), channel_id=1, source_target_pairs={{0,16},{16,0},{1,17},{17,1},{2,18},{18,2},{3,19},{19,3},{4,20},{20... | collective-permute-start | bytes 1572872 | tf_op jit(solution)/shard_map/ppermute | solution.py:345
  222.2 90.7 %collective-permute-start.30 = (bf16[512,512]{1,0:T(8,128)(2,1)}, bf16[512,512]{1,0:T(8,128)(2,1)}, u32[]{:S(2)}, u32[]{:S(2)}) collective-permute-start(bf16[512,512]{1,0:T(8,128)(2,1)} %convolution_convert_fusion.8), channel_id=1, source_target_pairs={{0,16},{16,0},{1,17},{17,1},{2,18},{18,2},{3,19},{19,3},{4,20},{20... | collective-permute-start | bytes 1572872 | tf_op jit(solution)/shard_map/ppermute | solution.py:345
  224.4 91.1 %collective-permute-start.34 = (bf16[512,1408]{1,0:T(8,128)(2,1)}, bf16[512,1408]{1,0:T(8,128)(2,1)}, u32[]{:S(2)}, u32[]{:S(2)}) collective-permute-start(bf16[512,1408]{1,0:T(8,128)(2,1)} %convolution_convert_fusion.5), channel_id=1, source_target_pairs={{0,16},{16,0},{1,17},{17,1},{2,18},{18,2},{3,19},{19,3},{4,20},{20... | collective-permute-start | bytes 4325384 | tf_op jit(solution)/shard_map/ppermute | solution.py:345
  226.2 92.5 %collective-permute-start.37 = (bf16[512,1408]{1,0:T(8,128)(2,1)}, bf16[512,1408]{1,0:T(8,128)(2,1)}, u32[]{:S(2)}, u32[]{:S(2)}) collective-permute-start(bf16[512,1408]{1,0:T(8,128)(2,1)} %convolution_convert_fusion.3), channel_id=1, source_target_pairs={{0,16},{16,0},{1,17},{17,1},{2,18},{18,2},{3,19},{19,3},{4,20},{20... | collective-permute-start | bytes 4325384 | tf_op jit(solution)/shard_map/ppermute | solution.py:345
  228.3 94.0 %collective-permute-start.40 = (bf16[1408,512]{1,0:T(8,128)(2,1)}, bf16[1408,512]{1,0:T(8,128)(2,1)}, u32[]{:S(2)}, u32[]{:S(2)}) collective-permute-start(bf16[1408,512]{1,0:T(8,128)(2,1)} %convolution_convert_fusion.1), channel_id=1, source_target_pairs={{0,16},{16,0},{1,17},{17,1},{2,18},{18,2},{3,19},{19,3},{4,20},{20... | collective-permute-start | bytes 4325384 | tf_op jit(solution)/shard_map/ppermute | solution.py:345
  312.9 65.2 %collective-permute-start.33 = (bf16[512,1408]{1,0:T(8,128)(2,1)}, bf16[512,1408]{1,0:T(8,128)(2,1)}, u32[]{:S(2)}, u32[]{:S(2)}) collective-permute-start(bf16[512,1408]{1,0:T(8,128)(2,1)} %convolution_convert_fusion.6), channel_id=1, source_target_pairs={{0,16},{16,0},{1,17},{17,1},{2,18},{18,2},{3,19},{19,3},{4,20},{20... | collective-permute-start | bytes 4325384 | tf_op jit(solution)/shard_map/ppermute | solution.py:345
  312.9 71.5 %collective-permute-start.36 = (bf16[512,1408]{1,0:T(8,128)(2,1)}, bf16[512,1408]{1,0:T(8,128)(2,1)}, u32[]{:S(2)}, u32[]{:S(2)}) collective-permute-start(bf16[512,1408]{1,0:T(8,128)(2,1)} %convolution_convert_fusion.4), channel_id=1, source_target_pairs={{0,16},{16,0},{1,17},{17,1},{2,18},{18,2},{3,19},{19,3},{4,20},{20... | collective-permute-start | bytes 4325384 | tf_op jit(solution)/shard_map/ppermute | solution.py:345
  315.5 72.3 %collective-permute-start.39 = (bf16[1408,512]{1,0:T(8,128)(2,1)}, bf16[1408,512]{1,0:T(8,128)(2,1)}, u32[]{:S(2)}, u32[]{:S(2)}) collective-permute-start(bf16[1408,512]{1,0:T(8,128)(2,1)} %convolution_convert_fusion.2), channel_id=1, source_target_pairs={{0,16},{16,0},{1,17},{17,1},{2,18},{18,2},{3,19},{19,3},{4,20},{20... | collective-permute-start | bytes 4325384 | tf_op jit(solution)/shard_map/ppermute | solution.py:345
  318.7 62.1 %collective-permute-start.35 = (bf16[512,1408]{1,0:T(8,128)(2,1)}, bf16[512,1408]{1,0:T(8,128)(2,1)}, u32[]{:S(2)}, u32[]{:S(2)}) collective-permute-start(bf16[512,1408]{1,0:T(8,128)(2,1)} %add_convert_fusion.6), channel_id=1, source_target_pairs={{0,1},{1,0},{2,3},{3,2},{4,5},{5,4},{6,7},{7,6},{8,9},{9,8},{10,11... | collective-permute-start | bytes 4325384 | tf_op jit(solution)/shard_map/ppermute | solution.py:345
  322.4 62.1 %collective-permute-start.38 = (bf16[512,1408]{1,0:T(8,128)(2,1)}, bf16[512,1408]{1,0:T(8,128)(2,1)}, u32[]{:S(2)}, u32[]{:S(2)}) collective-permute-start(bf16[512,1408]{1,0:T(8,128)(2,1)} %add_convert_fusion.4), channel_id=1, source_target_pairs={{0,1},{1,0},{2,3},{3,2},{4,5},{5,4},{6,7},{7,6},{8,9},{9,8},{10,11... | collective-permute-start | bytes 4325384 | tf_op jit(solution)/shard_map/ppermute | solution.py:345
  378.1 36.6 %collective-permute-start.41 = (bf16[1408,512]{1,0:T(8,128)(2,1)S(1)}, bf16[1408,512]{1,0:T(8,128)(2,1)S(1)}, u32[]{:S(2)}, u32[]{:S(2)}) collective-permute-start(bf16[1408,512]{1,0:T(8,128)(2,1)S(1)} %copy-done.33), channel_id=1, source_target_pairs={{0,1},{1,0},{2,3},{3,2},{4,5},{5,4},{6,7},{7,6},{8,9},{9,8},{10,11... | collective-permute-start | bytes 4325384 | tf_op jit(solution)/shard_map/ppermute | solution.py:345
  380.9 36.9 %collective-permute-start.29 = (bf16[512,1536]{1,0:T(8,128)(2,1)S(1)}, bf16[512,1536]{1,0:T(8,128)(2,1)S(1)}, u32[]{:S(2)}, u32[]{:S(2)}) collective-permute-start(bf16[512,1536]{1,0:T(8,128)(2,1)S(1)} %convolution_convert_fusion), channel_id=1, source_target_pairs={{0,16},{16,0},{1,17},{17,1},{2,18},{18,2},{3,19},{19,3},{4,20},{20... | collective-permute-start | bytes 4718600 | tf_op jit(solution)/shard_map/ppermute | solution.py:345
  (99 other events, 995.5 us)
Sparse Core Ops, SparseCore 0:
  38.4 126.4 all-gather.3
  167.0 71.5 all-gather.5
  240.7 75.1 all-gather.7
  420.0 240.1 all-reduce.2

commit v2 on v1

v2 whole, which is shorter than its diff:
```python
import functools

import jax
import jax.numpy as jnp
from jax import lax
from jax.experimental import pallas as pl
from jax.experimental.pallas import tpu as pltpu
from jax.sharding import PartitionSpec as P

HEAD_DIM = 64
PAIR = 2 * HEAD_DIM
LN2 = 0.6931471805599453
QUERY_SCALE = HEAD_DIM ** (-0.5) / LN2
F32 = jnp.float32
BF16 = jnp.bfloat16
BOUNDARY = 256
STAT_ROWS = 3

epsilon = 1e-06


def rms_norm(values, gain):
    return values * lax.rsqrt(jnp.mean(values * values, axis=-1, keepdims=True) + epsilon) * gain


def dot(left, right, left_dim, right_dim):
    return lax.dot_general(
        left, right, (((left_dim,), (right_dim,)), ((), ())), preferred_element_type=F32
    )


def nn(left, right):
    return dot(left, right, 1, 0)


def nt(left, right):
    return dot(left, right, 1, 1)


def tn(left, right):
    return dot(left, right, 0, 0)


def split_heads(pair):
    lane = lax.broadcasted_iota(jnp.int32, (1, PAIR), 1)
    zero = jnp.zeros_like(pair)
    return [jnp.where(lane < HEAD_DIM, pair, zero), jnp.where(lane >= HEAD_DIM, pair, zero)]


def forward_kernel(pieces, first, last, flag_ref, q_ref, *refs):
    refs = list(refs)
    qmark_ref = refs.pop(0)
    arrays = []
    for masked in pieces:
        count = 3 if masked else 2
        arrays.append(refs[:count])
        refs = refs[count:]
    if not first:
        old_high, old_total, old_out = refs[:3]
        refs = refs[3:]
    if last:
        result_ref, lse_ref = refs[:2]
        refs = refs[2:]
    high_ref, total_ref, out_ref = refs
    rows = q_ref.shape[0]
    if first:
        high_ref[0] = jnp.full((2, rows), -1e30, F32)
        total_ref[0] = jnp.zeros((2, rows), F32)
        out_ref[...] = jnp.zeros((PAIR, rows), F32)
    else:
        high_ref[0] = old_high[0]
        total_ref[0] = old_total[0]
        out_ref[...] = old_out[...]
    queries = split_heads(q_ref[...])

    def add_piece(piece, masked):
        keys = piece[0][...]
        turned = piece[1][...].T
        scores = [nt(keys, queries[h]) for h in range(2)]
        if masked:
            allowed = piece[2][...] <= qmark_ref[...]
        for h in range(2):
            score = scores[h]
            if masked:
                score = jnp.where(allowed, score, -1e30)
            highest = high_ref[0, h : h + 1, :]
            top = jnp.maximum(highest, jnp.max(score, axis=0, keepdims=True))
            power = jnp.exp2(score - top)
            shrink = jnp.exp2(highest - top)
            high_ref[0, h : h + 1, :] = top
            total_ref[0, h : h + 1, :] = total_ref[0, h : h + 1, :] * shrink + jnp.sum(
                power, axis=0, keepdims=True
            )
            columns = pl.ds(HEAD_DIM * h, HEAD_DIM)
            out_ref[columns, :] = out_ref[columns, :] * shrink + nn(
                turned[HEAD_DIM * h : HEAD_DIM * (h + 1)], power.astype(BF16)
            )

    for at, masked in enumerate(pieces):
        if masked:
            add_piece(arrays[at], True)
        else:
            pl.when(flag_ref[at] >= 0)(functools.partial(add_piece, arrays[at], False))
    if last:
        for h in range(2):
            columns = pl.ds(HEAD_DIM * h, HEAD_DIM)
            out_ref[columns, :] = out_ref[columns, :] / total_ref[0, h : h + 1, :]
        result_ref[...] = out_ref[...].T.astype(BF16)
        lse_ref[0] = high_ref[0] + jnp.log2(total_ref[0])


def forward_stage(queries, qmark, pieces, state, last):
    rows, width = queries.shape
    pairs = width // PAIR
    flags = jnp.stack([jnp.asarray(place, jnp.int32) for _, place, _ in pieces])
    args = [queries, qmark]
    in_specs = [
        pl.BlockSpec((rows, PAIR), lambda h, s: (0, h)),
        pl.BlockSpec((1, rows), lambda h, s: (0, 0)),
    ]
    keys = 0
    for kv, _, marks in pieces:
        count = kv.shape[0]
        keys += count
        args += [kv, kv]
        in_specs += [
            pl.BlockSpec((count, PAIR), lambda h, s: (0, h)),
            pl.BlockSpec((count, PAIR), lambda h, s: (0, pairs + h)),
        ]
        if marks is not None:
            args.append(marks)
            in_specs.append(pl.BlockSpec((count, 1), lambda h, s: (0, 0)))
    stat = jax.ShapeDtypeStruct((pairs, 2, rows), F32)
    stat_spec = pl.BlockSpec((1, 2, rows), lambda h, s: (h, 0, 0))
    state_specs = [stat_spec, stat_spec, pl.BlockSpec((PAIR, rows), lambda h, s: (h, 0))]
    state_shapes = [stat, stat, jax.ShapeDtypeStruct((width, rows), F32)]
    if state is not None:
        args += list(state)
        in_specs += state_specs
    if last:
        out_specs = [pl.BlockSpec((rows, PAIR), lambda h, s: (0, h)), stat_spec]
        out_shape = [jax.ShapeDtypeStruct((rows, width), BF16), stat]
        scratch = [
            pltpu.VMEM((1, 2, rows), F32),
            pltpu.VMEM((1, 2, rows), F32),
            pltpu.VMEM((PAIR, rows), F32),
        ]
    else:
        out_specs, out_shape, scratch = state_specs, state_shapes, []
    return pl.pallas_call(
        functools.partial(
            forward_kernel, [m is not None for _, _, m in pieces], state is None, last
        ),
        grid_spec=pltpu.PrefetchScalarGridSpec(
            num_scalar_prefetch=1,
            grid=(pairs,),
            in_specs=in_specs,
            out_specs=out_specs,
            scratch_shapes=scratch,
        ),
        out_shape=out_shape,
        compiler_params=pltpu.CompilerParams(vmem_limit_bytes=40 << 20),
        cost_estimate=pl.CostEstimate(
            flops=16 * rows * keys * width,
            bytes_accessed=8 * keys * width,
            transcendentals=rows * keys * width // HEAD_DIM,
        ),
    )(flags, *args)


def stats_kernel(rows, place_ref, mine_ref, other_ref, out_ref, lse_ref, sent_ref, stat_ref):
    half = mine_ref.shape[0]
    place = place_ref[0]
    sent_ref[pl.ds(pl.multiple_of(place * half, half), half), :] = mine_ref[...]
    sent_ref[pl.ds(pl.multiple_of((1 - place) * half, half), half), :] = other_ref[...]
    width = mine_ref.shape[1]
    heads = width // HEAD_DIM
    deltas = []
    for pair in range(width // PAIR):
        columns = pl.ds(pair * PAIR, PAIR)
        grad = sent_ref[pl.ds(0, rows), columns]
        terms = (grad.astype(F32) * out_ref[:, columns].astype(F32)).T
        deltas += [
            jnp.sum(terms[:HEAD_DIM], axis=0, keepdims=True),
            jnp.sum(terms[HEAD_DIM:], axis=0, keepdims=True),
        ]
    stat = jnp.concatenate(
        [lse_ref[pair] for pair in range(width // PAIR)] + deltas, axis=0
    )
    stat_ref[...] = stat
    for at in range(STAT_ROWS):
        piece = stat.astype(BF16)
        sent_ref[pl.ds(rows + at * 2 * heads, 2 * heads), :] = piece
        stat = stat - piece.astype(F32)


def pack_gradient(place, mine, other, attended, lse):
    rows, width = attended.shape
    stat_rows = 2 * width // HEAD_DIM
    return pl.pallas_call(
        functools.partial(stats_kernel, rows),
        in_specs=[pl.BlockSpec(memory_space=pltpu.SMEM)]
        + [pl.BlockSpec(memory_space=pltpu.VMEM)] * 4,
        out_specs=[pl.BlockSpec(memory_space=pltpu.VMEM)] * 2,
        out_shape=[
            jax.ShapeDtypeStruct((rows + STAT_ROWS * stat_rows, width), BF16),
            jax.ShapeDtypeStruct((stat_rows, rows), F32),
        ],
    )(place, mine, other, attended, lse)


def query_kernel(
    sizes, step_keys, place_ref, q_ref, grad_ref, stat_ref, qmark_ref, kmark_ref, *refs
):
    count = len(sizes)
    pieces, out_ref, kv_ref, kt_ref, sems = refs[:count], *refs[count:]
    rows, length = q_ref.shape[0], kv_ref.shape[0]
    width = kv_ref.shape[1] // 2
    pair = pl.program_id(0)
    index = place_ref[0]
    full = (index * rows) // step_keys
    end = jnp.minimum(
        ((index + 1) * rows + BOUNDARY + step_keys - 1) // step_keys, length // step_keys
    )

    def copy(at):
        start = pl.multiple_of(place_ref[at] * rows, rows)
        return pltpu.make_async_copy(
            pieces[at], kv_ref.at[pl.ds(start, sizes[at]), :], sems.at[at]
        )

    @pl.when(pair == 0)
    def _():
        for at in range(count):
            pl.when(place_ref[at] >= 0)(lambda at=at: copy(at).start())

        def clear(at, _):
            start = pl.multiple_of(at * BOUNDARY, BOUNDARY)
            kv_ref[pl.ds(start, BOUNDARY), :] = jnp.zeros((BOUNDARY, 2 * width), BF16)
            return 0

        ratio = rows // BOUNDARY
        lax.fori_loop((index + 1) * ratio + 1, end * (step_keys // BOUNDARY), clear, 0)
        for at in range(count):
            pl.when(place_ref[at] >= 0)(lambda at=at: copy(at).wait())

    queries, grads = split_heads(q_ref[...]), split_heads(grad_ref[...])
    k_columns = pl.ds(pl.multiple_of(pair * PAIR, PAIR), PAIR)
    v_columns = pl.ds(pl.multiple_of(width + pair * PAIR, PAIR), PAIR)
    lse = [stat_ref[pl.ds(2 * pair + h, 1), :] for h in range(2)]
    delta = [
        stat_ref[pl.ds(stat_ref.shape[0] // 2 + 2 * pair + h, 1), :] for h in range(2)
    ]

    def turn(at, _):
        start = pl.multiple_of(at * step_keys, step_keys)
        kt_ref[:, pl.ds(start, step_keys)] = kv_ref[pl.ds(start, step_keys), k_columns].T
        return 0

    lax.fori_loop(0, end, turn, 0)

    def step(masked):
        def body(at, state):
            start = pl.multiple_of(at * step_keys, step_keys)
            keys = kv_ref[pl.ds(start, step_keys), k_columns]
            values = kv_ref[pl.ds(start, step_keys), v_columns]
            if masked:
                allowed = kmark_ref[pl.ds(start, step_keys), :] <= qmark_ref[...]
            new = []
            for h in range(2):
                score = nt(keys, queries[h])
                slope = nt(values, grads[h])
                prob = jnp.exp2(score - lse[h])
                if masked:
                    prob = jnp.where(allowed, prob, 0.0)
                grad = (prob * (slope - delta[h])).astype(BF16)
                turned = kt_ref[pl.ds(HEAD_DIM * h, HEAD_DIM), pl.ds(start, step_keys)]
                new.append(state[h] + nn(turned, grad))
            return tuple(new)

        return body

    empty = jnp.zeros((HEAD_DIM, rows), F32)
    state = lax.fori_loop(full, end, step(True), (empty, empty))
    state = lax.fori_loop(0, full, step(False), state)
    out_ref[...] = (jnp.concatenate(state, axis=0).T * HEAD_DIM ** (-0.5)).astype(out_ref.dtype)


def query_gradient(queries, sent, stat, pieces, qmark, kmark, step_keys=1024):
    rows, width = queries.shape
    length = kmark.shape[0]
    pairs = width // PAIR
    places = jnp.stack([jnp.asarray(place, jnp.int32) for _, place in pieces])
    sizes = [kv.shape[0] for kv, _ in pieces]
    return pl.pallas_call(
        functools.partial(query_kernel, sizes, step_keys),
        grid_spec=pltpu.PrefetchScalarGridSpec(
            num_scalar_prefetch=1,
            grid=(pairs,),
            in_specs=[
                pl.BlockSpec((rows, PAIR), lambda h, s: (0, h)),
                pl.BlockSpec((rows, PAIR), lambda h, s: (0, h)),
                pl.BlockSpec(stat.shape, lambda h, s: (0, 0)),
                pl.BlockSpec((1, rows), lambda h, s: (0, 0)),
                pl.BlockSpec((length, 1), lambda h, s: (0, 0)),
            ]
            + [pl.BlockSpec(memory_space=pl.ANY)] * len(pieces),
            out_specs=pl.BlockSpec((rows, PAIR), lambda h, s: (0, h)),
            scratch_shapes=[
                pltpu.VMEM((length, 2 * width), BF16),
                pltpu.VMEM((PAIR, length), BF16),
                pltpu.SemaphoreType.DMA((len(pieces),)),
            ],
        ),
        out_shape=jax.ShapeDtypeStruct((rows, width), BF16),
        compiler_params=pltpu.CompilerParams(vmem_limit_bytes=56 << 20),
        cost_estimate=pl.CostEstimate(
            flops=16 * rows * length * width,
            bytes_accessed=4 * length * width,
            transcendentals=rows * length * width // HEAD_DIM,
        ),
    )(places, queries, sent, stat, qmark, kmark, *[kv for kv, _ in pieces])


def key_kernel(
    sizes, step_queries, place_ref, k_ref, v_ref, q_ref, qmark_ref, kmark_ref, *refs
):
    count = len(sizes)
    pieces = refs[:count]
    dk_ref, dv_ref, grad_ref, raw_ref, stat_ref, sems = refs[count:]
    rows, length = k_ref.shape[0], q_ref.shape[0]
    width = grad_ref.shape[1]
    stat_rows = stat_ref.shape[0]
    packed = STAT_ROWS * stat_rows
    pair = pl.program_id(0)
    index = place_ref[0]

    def copies(at):
        size = sizes[at]
        start = pl.multiple_of(place_ref[at] * rows + rows - size, BOUNDARY)
        return (
            pltpu.make_async_copy(
                pieces[at].at[pl.ds(0, size), :],
                grad_ref.at[pl.ds(start, size), :],
                sems.at[2 * at],
            ),
            pltpu.make_async_copy(
                pieces[at].at[pl.ds(size, packed), :],
                raw_ref.at[at],
                sems.at[2 * at + 1],
            ),
        )

    @pl.when(pair == 0)
    def _():
        for at in range(count):

            @pl.when(place_ref[at] >= 0)
            def _(at=at):
                for one in copies(at):
                    one.start()

        @pl.when(index > 0)
        def _():
            start = pl.multiple_of((index - 1) * rows, rows)
            grad_ref[pl.ds(start, rows - BOUNDARY), :] = jnp.zeros(
                (rows - BOUNDARY, width), BF16
            )

        for at in range(count):

            @pl.when(place_ref[at] >= 0)
            def _(at=at):
                for one in copies(at):
                    one.wait()
                stat = raw_ref[at, :stat_rows].astype(F32)
                for part in range(1, STAT_ROWS):
                    stat = stat + raw_ref[
                        at, part * stat_rows : (part + 1) * stat_rows
                    ].astype(F32)
                start = pl.multiple_of(place_ref[at] * rows, rows)
                stat_ref[:, pl.ds(start, rows)] = stat

    keys, values = split_heads(k_ref[...]), split_heads(v_ref[...])
    columns = pl.ds(pl.multiple_of(pair * PAIR, PAIR), PAIR)

    def step(masked):
        def body(at, state):
            start = pl.multiple_of(at * step_queries, step_queries)
            span = pl.ds(start, step_queries)
            queries = q_ref[span, :]
            grads = grad_ref[span, columns]
            if masked:
                allowed = kmark_ref[...] <= qmark_ref[:, span]
            new = []
            for h in range(2):
                lse = stat_ref[pl.ds(2 * pair + h, 1), span]
                delta = stat_ref[pl.ds(stat_rows // 2 + 2 * pair + h, 1), span]
                score = nt(keys[h], queries)
                slope = nt(values[h], grads)
                prob = jnp.exp2(score - lse)
                if masked:
                    prob = jnp.where(allowed, prob, 0.0)
                grad = prob * (slope - delta)
                new += [
                    state[2 * h] + nn(grad.astype(BF16), queries),
                    state[2 * h + 1] + nn(prob.astype(BF16), grads),
                ]
            return tuple(new)

        return body

    empty = jnp.zeros((rows, PAIR), F32)
    first = jnp.maximum((index * rows - BOUNDARY) // step_queries, 0)
    own = ((index + 1) * rows + step_queries - 1) // step_queries
    state = lax.fori_loop(first, own, step(True), (empty,) * 4)
    state = lax.fori_loop(own, length // step_queries, step(False), state)
    lane = lax.broadcasted_iota(jnp.int32, (1, PAIR), 1)
    dk_ref[...] = (jnp.where(lane < HEAD_DIM, state[0], state[2]) * LN2).astype(dk_ref.dtype)
    dv_ref[...] = (0.5 * jnp.where(lane < HEAD_DIM, state[1], state[3])).astype(dv_ref.dtype)


def key_gradient(kv, q_all, pieces, qmark, kmark, step_queries=512):
    rows = kv.shape[0]
    length, width = q_all.shape
    pairs = width // PAIR
    stat_rows = 2 * width // HEAD_DIM
    packed = STAT_ROWS * stat_rows
    places = jnp.stack([jnp.asarray(place, jnp.int32) for _, place in pieces])
    sizes = [sent.shape[0] - packed for sent, _ in pieces]
    return pl.pallas_call(
        functools.partial(key_kernel, sizes, step_queries),
        grid_spec=pltpu.PrefetchScalarGridSpec(
            num_scalar_prefetch=1,
            grid=(pairs,),
            in_specs=[
                pl.BlockSpec((rows, PAIR), lambda h, s: (0, h)),
                pl.BlockSpec((rows, PAIR), lambda h, s: (0, pairs + h)),
                pl.BlockSpec((length, PAIR), lambda h, s: (0, h)),
                pl.BlockSpec((1, length), lambda h, s: (0, 0)),
                pl.BlockSpec((rows, 1), lambda h, s: (0, 0)),
            ]
            + [pl.BlockSpec(memory_space=pl.ANY)] * len(pieces),
            out_specs=[pl.BlockSpec((rows, PAIR), lambda h, s: (0, h))] * 2,
            scratch_shapes=[
                pltpu.VMEM((length, width), BF16),
                pltpu.VMEM((len(pieces), packed, rows), BF16),
                pltpu.VMEM((stat_rows, length), F32),
                pltpu.SemaphoreType.DMA((2 * len(pieces),)),
            ],
        ),
        out_shape=[jax.ShapeDtypeStruct((rows, width), BF16)] * 2,
        compiler_params=pltpu.CompilerParams(vmem_limit_bytes=56 << 20),
        cost_estimate=pl.CostEstimate(
            flops=rows * length * width,
            bytes_accessed=4 * length * width,
            transcendentals=rows * length * width // HEAD_DIM,
        ),
    )(places, kv, kv, q_all, qmark, kmark, *[sent for sent, _ in pieces])


def on_device(
    tokens,
    value_first,
    teacher,
    valid,
    blocks,
    gain_attn,
    gain_ffn,
    w_query,
    w_key,
    w_value,
    w_out,
    w_gate,
    w_up,
    w_down,
):
    width = tokens.shape[2]
    own_rows = tokens.shape[1]
    sizes = {axis: lax.axis_size(axis) for axis in ("shard", "ctx", "tp")}
    shard, ctx, tp = (lax.axis_index(axis) for axis in ("shard", "ctx", "tp"))
    group_rows = own_rows * sizes["tp"]
    half = w_query.shape[1]
    part = w_query.shape[0]
    line = sizes["ctx"] // 2

    def flip(values, axis, bit=1):
        return lax.ppermute(values, axis, [(i, i ^ bit) for i in range(sizes[axis])])

    def tree_sum(values):
        for axis, size in sizes.items():
            bit = 1
            while bit < size:
                values = values + flip(values, axis, bit)
                bit *= 2
        return values

    def in_order(position, mine, other, axis):
        first = position == 0
        return jnp.concatenate(
            [jnp.where(first, mine, other), jnp.where(first, other, mine)], axis=axis
        )

    def shard_gather(values, axis):
        if sizes["shard"] == 2:
            return in_order(shard, values, flip(values, "shard"), axis)
        return lax.all_gather(values, "shard", axis=axis, tiled=True)

    def rows_of(values, position):
        return lax.dynamic_slice_in_dim(values, position * own_rows, own_rows, 0)

    def cols_of(values, position, size):
        return lax.dynamic_slice_in_dim(values, position * size, size, 1)

    level, column = ctx // 2, ctx % 2

    def spread(own, step, edge, between):
        if line != 4:
            gathered = lax.all_gather(own, "ctx", axis=0, tiled=False)
            below = [(place < ctx) if step == 1 else (place > ctx) for place in range(2 * line)]
            pieces = [
                (gathered[place], jnp.where(below[place], place, -1)) for place in range(2 * line)
            ]
            beside = jnp.clip(ctx + step, 0, 2 * line - 1)
            rows = lax.dynamic_index_in_dim(gathered, beside, 0, keepdims=False)[edge]
            gathered, rows = between(0, [pieces[0][0], rows])
            pieces[0] = (gathered, pieces[0][1])
            stages = [pieces[:2]]
            for i in range(2, 2 * line, 2):
                (first,) = between(i // 2, [pieces[i][0]])
                stages.append([(first, pieces[i][1]), pieces[i + 1]])
            return stages, rows
        along = [(i, i + 2 * step) for i in range(2 * line) if 0 <= i + 2 * step < 2 * line]
        across = flip(own, "ctx")
        near = 1 if step == 1 else 0
        diagonal = [
            (i + step, i) for i in range(2 * line) if i % 2 == near and 0 <= i + step < 2 * line
        ]
        beside = lax.ppermute(own[edge], "ctx", diagonal)
        moving = lax.ppermute(own, "ctx", along)
        across, moving, beside = between(0, [across, moving, beside])
        rows = jnp.where(column == near, beside, across[edge])
        stages = [[(across, jnp.where(column == near, ctx - step, -1))]]
        for hop in range(1, line):
            there = level - step * hop
            exists = (there >= 0) & (there < line)
            stages[-1].append((moving, jnp.where(exists, 2 * there + column, -1)))
            across = flip(moving, "ctx")
            if hop + 1 < line:
                moving = lax.ppermute(moving, "ctx", along)
                across, moving = between(hop, [across, moving])
            else:
                (across,) = between(hop, [across])
            stages.append([(across, jnp.where(exists, 2 * there + 1 - column, -1))])
        return stages, rows

    mine = tokens.reshape(own_rows, width)
    first_own = value_first.reshape(own_rows, width)
    key_marks = blocks.reshape(-1)
    padded_marks = jnp.concatenate([key_marks, jnp.full((BOUNDARY,), 1 << 30, key_marks.dtype)])
    query_marks = lax.dynamic_slice_in_dim(key_marks, ctx * group_rows, group_rows, 0)
    next_marks = lax.dynamic_slice_in_dim(padded_marks, (ctx + 1) * group_rows, BOUNDARY, 0)
    keep = valid.reshape(own_rows).astype(F32)

    theirs = flip(mine, "tp")
    first_theirs = flip(cols_of(first_own, 1 - tp, half), "tp")
    weight_qkv = shard_gather(jnp.concatenate([w_query, w_key, w_value], axis=1), 0)
    count = tree_sum(jnp.broadcast_to(jnp.sum(keep), (1, 128)))[0, 0]

    group = in_order(tp, mine, theirs, 0).astype(F32)
    normed_one = rms_norm(group, gain_attn).astype(BF16)
    first_group = in_order(tp, cols_of(first_own, tp, half), first_theirs, 0).astype(F32)
    qkv = nn(normed_one, weight_qkv)
    queries = (qkv[:, :half] * QUERY_SCALE).astype(BF16)
    kv = jnp.concatenate(
        [qkv[:, half : 2 * half], 0.5 * qkv[:, 2 * half :] + 0.5 * first_group], axis=1
    ).astype(BF16)

    def pair_up(gathered):
        return [
            lax.dynamic_index_in_dim(gathered, at, 0, keepdims=False) for at in (tp, 1 - tp)
        ]

    def gather_rows(values):
        gathered = lax.all_gather(values, ("tp", "shard"), axis=0, tiled=True)
        return pair_up(gathered.reshape(sizes["tp"], width, values.shape[1]))

    def gather_blocks(values):
        if sizes["shard"] == 2:
            both = [values, flip(values, "tp")]
            return [[one, flip(one, "shard")] for one in both]
        gathered = lax.all_gather(values, ("tp", "shard"), axis=0, tiled=False)
        gathered = pair_up(gathered.reshape(sizes["tp"], sizes["shard"], *values.shape))
        return [[one[i] for i in range(sizes["shard"])] for one in gathered]

    def block_of(values, at):
        if sizes["shard"] == 2:
            return cols_of(values, shard if at == 0 else 1 - shard, part)
        return values[:, at * part : (at + 1) * part]

    def join_blocks(terms):
        if sizes["shard"] == 2:
            return in_order(shard, terms[0], terms[1], 1)
        return jnp.concatenate(terms, axis=1)

    def times_blocks(lefts, blocks_of):
        return join_blocks(
            [
                sum(nn(left, blocks[at]) for left, blocks in zip(lefts, blocks_of))
                for at in range(sizes["shard"])
            ]
        )

    def times_turned(left, blocks):
        return sum(nt(block_of(left, at), block) for at, block in enumerate(blocks))

    kv, w_gate, w_up, w_down, w_out = lax.optimization_barrier((kv, w_gate, w_up, w_down, w_out))
    outs, downs = gather_blocks(w_out), gather_blocks(w_down)
    gates, ups = gather_rows(w_gate), gather_rows(w_up)

    qmark, kmark = query_marks.reshape(1, -1), key_marks.reshape(-1, 1)
    forward = {"state": None, "pieces": [(kv, 0, query_marks.reshape(-1, 1))]}

    def advance(last):
        forward["state"] = forward_stage(
            queries, qmark, forward["pieces"], forward["state"], last
        )
        forward["pieces"] = []

    def forward_between(at, arrays):
        advance(False)
        *arrays, out = lax.optimization_barrier((*arrays, forward["state"][2]))
        forward["state"] = (*forward["state"][:2], out)
        if sizes["ctx"] == 8:
            there = level - at
            if at == 0:
                rows = jnp.where(column == 1, arrays[2], arrays[0][:BOUNDARY])
                forward["pieces"] = [(rows, 0, next_marks.reshape(-1, 1))]
                forward["pieces"].append((arrays[0], jnp.where(column == 1, 0, -1), None))
            else:
                forward["pieces"].append((arrays[0], jnp.where(there >= 0, 0, -1), None))
            if len(arrays) > 1:
                forward["pieces"].append((arrays[1], jnp.where(there >= 1, 0, -1), None))
        return arrays

    if line == 4:
        stages, kv_next = spread(kv, 1, slice(0, BOUNDARY), forward_between)
        advance(True)
    else:
        stages, kv_next = spread(kv, 1, slice(0, BOUNDARY), lambda at, arrays: arrays)
        forward["pieces"].append((kv_next, 0, next_marks.reshape(-1, 1)))
        for at, stage in enumerate(stages):
            advance(False)
            forward["pieces"] = [(piece, place, None) for piece, place in stage]
        advance(True)
    attended, lse = forward["state"]

    attended, q_sent = lax.optimization_barrier((attended, queries))
    q_all = lax.all_gather(q_sent, "ctx", axis=0, tiled=True)
    att = [rows_of(attended, tp), flip(rows_of(attended, 1 - tp), "tp")]
    inputs = mine.astype(F32)
    hidden = inputs + times_blocks(att, outs)
    normed_two = rms_norm(hidden, gain_ffn).astype(BF16)
    gate = [nn(normed_two, w) for w in gates]
    up = [nn(normed_two, w) for w in ups]
    logistic = [jax.nn.sigmoid(g) for g in gate]
    act = [(g * s * u).astype(BF16) for g, s, u in zip(gate, logistic, up)]
    normed_pair = flip(normed_two, "tp")
    final = hidden + times_blocks(act, downs)
    final, normed_pair = lax.optimization_barrier((final, normed_pair))
    act_two = flip(act[1], "tp")
    difference = final - teacher.reshape(own_rows, width).astype(F32)
    local_error = jnp.sum(jnp.mean(difference * difference, axis=1) * keep)
    token_total = group_rows * sizes["ctx"] * sizes["shard"]
    grad_final = token_total / count * keep[:, None] * difference
    grad_round = grad_final.astype(BF16)
    grad_act = [times_turned(grad_round, w) for w in downs]
    grad_gate = [
        (a * u * s * (1.0 + g * (1.0 - s))).astype(BF16)
        for a, u, s, g in zip(grad_act, up, logistic, gate)
    ]
    grad_up = [(a * g * s).astype(BF16) for a, g, s in zip(grad_act, gate, logistic)]
    grad_gate[0], act_two, round_sent = lax.optimization_barrier(
        (grad_gate[0], act_two, grad_round)
    )
    round_two = flip(round_sent, "tp")
    grad_two = (
        nt(grad_gate[0], gates[0])
        + nt(grad_gate[1], gates[1])
        + nt(grad_up[0], ups[0])
        + nt(grad_up[1], ups[1])
    )
    hidden_part, gain_ffn_term = jax.vjp(rms_norm, hidden, gain_ffn)[1](grad_two)
    grad_hidden = grad_final + hidden_part
    hidden_round = grad_hidden.astype(BF16)
    grad_att = [times_turned(hidden_round, w).astype(BF16) for w in outs]
    grad_theirs, round_two = lax.optimization_barrier((flip(grad_att[1], "tp"), round_two))
    sent, stat = pack_gradient(
        tp.reshape(1).astype(jnp.int32), grad_att[0], grad_theirs, attended, lse
    )

    sent, hidden_sent, gate_sent = lax.optimization_barrier((sent, hidden_round, grad_gate[1]))
    hidden_two, gate_two = flip(hidden_sent, "tp"), flip(gate_sent, "tp")

    def shard_reduce(term, slice_rows):
        if sizes["shard"] == 2:
            return term(shard) + flip(term(1 - shard).astype(BF16), "shard").astype(F32)
        whole = jnp.concatenate(
            [term(i) for i in range(sizes["shard"])], axis=0 if slice_rows else 1
        )
        return lax.psum_scatter(
            whole.astype(BF16), "shard", scatter_dimension=0 if slice_rows else 1, tiled=True
        ).astype(F32)

    def over_rows(lefts, rights, slice_left):
        def term(position):
            if slice_left:
                return sum(tn(cols_of(a, position, part), b) for a, b in zip(lefts, rights))
            return sum(tn(a, cols_of(b, position, part)) for a, b in zip(lefts, rights))

        return shard_reduce(term, slice_left).astype(BF16)

    kv_pieces = [(kv, ctx), (kv_next, jnp.where(ctx + 1 < 2 * line, ctx + 1, -1))]
    kv_pieces += [piece for stage in stages for piece in stage]
    parts = {}

    def grad_between(at, arrays):
        if at == 0:
            parts["query_grad"] = query_gradient(queries, sent, stat, kv_pieces, qmark, kmark)
            parts["hidden_two"], parts["gate_two"] = hidden_two, gate_two
            hold = ["query_grad", "hidden_two", "gate_two"]
        elif at == 1:
            query_grad, up_sent = lax.optimization_barrier((parts["query_grad"], grad_up[1]))
            parts["query_grad"] = query_grad
            parts["up_two"] = flip(up_sent, "tp")
            parts["down"] = over_rows([grad_round, round_two], [act[0], act_two], True)
            parts["out"] = over_rows(
                [hidden_round, parts["hidden_two"]],
                [rows_of(attended, tp), rows_of(attended, 1 - tp)],
                True,
            )
            hold = ["down", "out", "up_two"]
        elif at == 2:
            parts["gate"] = over_rows([normed_two, normed_pair], [grad_gate[0], parts["gate_two"]], True)
            parts["up"] = over_rows([normed_two, normed_pair], [grad_up[0], parts["up_two"]], True)
            parts["query"] = over_rows([normed_one], [parts["query_grad"]], True)
            parts["all"] = jnp.concatenate(
                [parts[name] for name in ("gate", "up", "down", "query", "out")], axis=1
            )
            hold = ["all"]
        else:
            return arrays
        held = lax.optimization_barrier((*arrays, *[parts[name] for name in hold]))
        parts.update(zip(hold, held[len(arrays) :]))
        return list(held[: len(arrays)])

    grad_stages, sent_before = spread(
        sent, -1, slice(group_rows - BOUNDARY, None), grad_between
    )
    query_grad = parts["query_grad"]
    weight_grads = lax.all_gather(
        lax.psum_scatter(parts["all"], "ctx", scatter_dimension=0, tiled=True),
        "ctx",
        axis=0,
        tiled=True,
    ).astype(F32)
    hidden_half = w_gate.shape[1]
    ends = [hidden_half, 2 * hidden_half, 3 * hidden_half, 3 * hidden_half + half]
    w_gate_grad, w_up_grad, w_down_grad, w_query_grad, w_out_grad = jnp.split(
        weight_grads, ends, axis=1
    )
    grad_pieces = [(sent, ctx), (sent_before, ctx - 1)]
    grad_pieces += [piece for stage in grad_stages for piece in stage]
    key_grad, value_half = key_gradient(
        kv, q_all, grad_pieces, key_marks.reshape(1, -1), query_marks.reshape(-1, 1)
    )
    grads = jnp.concatenate([query_grad, key_grad, value_half], axis=1)
    kv_part = over_rows([normed_one], [grads[:, half:]], True)
    kv_grad = lax.psum(kv_part, "ctx").astype(F32)
    grad_one_theirs = flip(nt(rows_of(grads, 1 - tp), weight_qkv).astype(BF16), "tp")
    grad_one = nt(rows_of(grads, tp), weight_qkv) + grad_one_theirs.astype(F32)
    input_part, gain_attn_term = jax.vjp(rms_norm, inputs, gain_attn)[1](grad_one)
    tokens_grad = grad_hidden + input_part
    first_grad = in_order(
        tp, rows_of(value_half, tp), flip(rows_of(value_half, 1 - tp), "tp"), 1
    ).astype(F32)

    small = jnp.concatenate(
        [gain_attn_term, gain_ffn_term, jnp.broadcast_to(local_error, (128,))]
    )
    small = tree_sum(small.reshape(1, -1)).reshape(-1)
    return (
        final.astype(BF16).reshape(1, own_rows, width),
        small[2 * width] / count,
        tokens_grad.reshape(1, own_rows, width),
        first_grad.reshape(1, own_rows, width),
        small[:width],
        small[width : 2 * width],
        w_query_grad,
        kv_grad[:, :half],
        kv_grad[:, half:],
        w_out_grad.T,
        w_gate_grad,
        w_up_grad,
        w_down_grad.T,
    )


def solution(mesh):
    rows = P("shard", ("ctx", "tp"), None)
    wide, tall = P("shard", "tp"), P("tp", "shard")
    return jax.shard_map(
        on_device,
        mesh=mesh,
        in_specs=(
            rows,
            rows,
            rows,
            P("shard", ("ctx", "tp")),
            P("shard", None),
            P(),
            P(),
            wide,
            wide,
            wide,
            tall,
            wide,
            wide,
            tall,
        ),
        out_specs=(rows, P(), rows, rows, P(), P(), wide, wide, wide, tall, wide, wide, tall),
        check_vma=False,
    )
```

time: 688 us -> 674 us (0.980)
  blocking collectives: 51.4 us -> 0 us
  other arithmetic: 56.1 us -> 18.6 us
  matrix products: 54.1 us -> 77.7 us
  starting transfers between devices: 55.3 us -> 75.1 us
  local copies, waits for them, and re-layouts: 23.5 us -> 42.6 us
    psum x1, waiting for transfers between devices: 179 us -> 40.7 us  [on_device(): kv_grad = lax.psum(kv_part, 'ctx').astype(F32)]
    all_gather x3 -> x4, waiting for transfers between devices: 0.01 us -> 86.5 us  [the longest x1 86.5 us: on_device(): lax.all_gather(lax.psum_scatter(parts['all'], 'ctx', scatter_dimension=0,...]
    all_gather x1 -> x0, blocking collectives: 51.4 us -> none  [on_device(): stats = lax.all_gather(jnp.stack([lse, delta]), 'ctx', axis=3, tiled=True)]
    reduce_scatter x0 -> x1, waiting for transfers between devices: none -> 34.9 us  [on_device(): lax.psum_scatter(parts['all'], 'ctx', scatter_dimension=0, tiled=True)]
    ppermute x0 -> x8, waiting for transfers between devices: none -> 24.4 us  [the longest x4 24.4 us: spread(): moving = lax.ppermute(moving, 'ctx', along)]
    dot_general x37 -> x47, matrix products: 54.1 us -> 77.7 us  [dot(): lax.dot_general(left, right, (((left_dim,), (right_dim,)), ((), ())), pre...]
    select_n x12 -> x3, other arithmetic: 23.7 us -> 2.2 us  [in_order(): jnp.where(first, mine, other)]
    ppermute x0 -> x8, starting transfers between devices: none -> 20.7 us  [the longest x4 11.9 us: spread(): moving = lax.ppermute(moving, 'ctx', along)]
  transfers between devices with their start and end apart: 46 -> 57, of which waited for: 17 -> 31; matrix products, arithmetic and copies ran while one was open for 15% -> 16% of each run, Pallas kernels for 12% -> 13%
where the time goes in v2:
time: 674 us; the launch traced here: 667 us
  waiting for transfers between devices  347 us (51%)
  Pallas kernels  85.8 us (13%)
  matrix products  77.7 us (12%)
  starting transfers between devices  75.1 us (11%)
  local copies, waits for them, and re-layouts  42.6 us (6%)
  between operations  19.7 us (3%)
  other arithmetic  18.6 us (3%)
    ppermute x43, waiting for transfers between devices, flip(): lax.ppermute(values, axis, [(i, i ^ bit) for i in range(sizes[axis])])  160 us
    all_gather x1, waiting for transfers between devices, on_device(): lax.all_gather(lax.psum_scatter(parts['all'], 'ctx', scatter_dimension=0,...  86.5 us
    dot_general x47, matrix products, dot(): lax.dot_general(left, right, (((left_dim,), (right_dim,)), ((), ())), pre...  77.7 us
    ppermute x43, starting transfers between devices, flip(): lax.ppermute(values, axis, [(i, i ^ bit) for i in range(sizes[axis])])  53.7 us
    pallas_call x1, Pallas kernels, key_gradient(): pl.pallas_call(functools.partial(key_kernel, sizes, step_queries), grid_s...  52.6 us
    psum x1, waiting for transfers between devices, on_device(): kv_grad = lax.psum(kv_part, 'ctx').astype(F32)  40.7 us
    reduce_scatter x1, waiting for transfers between devices, on_device(): lax.psum_scatter(parts['all'], 'ctx', scatter_dimension=0, tiled=True)  34.9 us
    ppermute x4, waiting for transfers between devices, spread(): moving = lax.ppermute(moving, 'ctx', along)  24.4 us
  transfers between devices with their start and end apart: 57, of which 31 were waited for; matrix products, arithmetic and copies ran while one was open for 16% of the time, Pallas kernels for 13%

profile of v2, /device:TPU:0, one launch (start us, length us, event | category | flops | bytes accessed | tf_op | source)
XLA Modules:
  0.0 666.7 jit_solution(6713641185984862727)
XLA Ops:
  14.3 17.4 %collective-permute-done.2 = bf16[256,512]{1,0:T(8,128)(2,1)S(1)} collective-permute-done((bf16[256,512]{1,0:T(8,128)(2,1)}, bf16[256,512]{1,0:T(8,128)(2,1)S(1)}, u32[]{:S(2)}, u32[]{:S(2)}) %collective-permute-start.2) | collective-permute-done | bytes 262176 | tf_op jit(solution)/shard_map/ppermute | solution.py:488
  52.3 21.1 %collective-permute-done.3.refs_4_.refs_5_.refs_2_ = bf16[512,1024]{1,0:T(8,128)(2,1)S(1)} collective-permute-done((bf16[512,1024]{1,0:T(8,128)(2,1)S(1)}, bf16[512,1024]{1,0:T(8,128)(2,1)S(1)}, u32[]{:S(2)}, u32[]{:S(2)}) %collective-permute-start.3) | collective-permute-done | bytes 1048608 | tf_op jit(solution)/shard_map/ppermute | solution.py:488
  82.0 4.9 shard_map.238
  87.8 10.5 %collective-permute-done.6.refs_1_.refs_2_.refs_4_ = bf16[512,1024]{1,0:T(8,128)(2,1)} collective-permute-done((bf16[512,1024]{1,0:T(8,128)(2,1)}, bf16[512,1024]{1,0:T(8,128)(2,1)}, u32[]{:S(2)}, u32[]{:S(2)}) %collective-permute-start.6) | collective-permute-done | bytes 1048608 | tf_op jit(solution)/shard_map/ppermute | solution.py:488
  101.1 4.9 collective-permute-start.9
  111.5 12.2 %collective-permute-done.8.refs_1_.refs_2_.refs_6_ = bf16[512,1024]{1,0:T(8,128)(2,1)S(1)} collective-permute-done((bf16[512,1024]{1,0:T(8,128)(2,1)}, bf16[512,1024]{1,0:T(8,128)(2,1)S(1)}, u32[]{:S(2)}, u32[]{:S(2)}) %collective-permute-start.8) | collective-permute-done | bytes 1048608 | tf_op jit(solution)/shard_map/ppermute | solution.py:488
  131.3 11.3 %collective-permute-done.12 = bf16[512,512]{1,0:T(8,128)(2,1)} collective-permute-done((bf16[512,512]{1,0:T(8,128)(2,1)}, bf16[512,512]{1,0:T(8,128)(2,1)}, u32[]{:S(2)}, u32[]{:S(2)}) %collective-permute-start.12) | collective-permute-done | bytes 524320 | tf_op jit(solution)/shard_map/ppermute | solution.py:488
  153.6 17.8 %collective-permute-done.15 = bf16[1408,512]{1,0:T(8,128)(2,1)} collective-permute-done((bf16[1408,512]{1,0:T(8,128)(2,1)}, bf16[1408,512]{1,0:T(8,128)(2,1)}, u32[]{:S(2)}, u32[]{:S(2)}) %collective-permute-start.15) | collective-permute-done | bytes 1441824 | tf_op jit(solution)/shard_map/ppermute | solution.py:488
  181.2 4.5 multiply_convert_fusion.5
  254.7 5.6 collective-permute-done.26
  272.3 14.0 %shard_map.243 = bf16[512,512]{1,0:T(8,128)(2,1)} custom-call(s32[9]{0:T(128)} %stack.107.place_ref, bf16[512,512]{1,0:T(8,128)(2,1)} %copy-done.2, bf16[560,512]{1,0:T(8,128)(2,1)} %get-tuple-element.113.grad_ref.refs_0_, f32[16,512]{1,0:T(8,128)} %get-tuple-element.114.stat_ref, s32[1,512]{1,0:T(1,128)} %copy-done.7, s32[4096,1]{1,0:T(8,128)} %copy.32.kmark_ref, ...), custom_call_target="tpu_custom_call" | custom-call | flops 17179869184 | bytes 8388608 | tf_op jit(solution)/shard_map/pallas_call | solution.py:295
  291.0 12.0 %collective-permute-start.32 = (bf16[560,512]{1,0:T(8,128)(2,1)}, bf16[560,512]{1,0:T(8,128)(2,1)S(1)}, u32[]{:S(2)}, u32[]{:S(2)}) collective-permute-start(bf16[560,512]{1,0:T(8,128)(2,1)} %collective-permute-done.28.refs_3_), channel_id=1, source_target_pairs={{0,2},{2,0},{4,6},{6,4},{8,10},{10,8},{12,14},{14,12},{1,3},{3,1},... | collective-permute-start | bytes 1720328 | tf_op jit(solution)/shard_map/ppermute | solution.py:488
  312.2 4.7 collective-permute-done.32.refs_4_
  316.9 11.8 %collective-permute-done.33.refs_5_ = bf16[560,512]{1,0:T(8,128)(2,1)S(1)} collective-permute-done((bf16[560,512]{1,0:T(8,128)(2,1)}, bf16[560,512]{1,0:T(8,128)(2,1)S(1)}, u32[]{:S(2)}, u32[]{:S(2)}) %collective-permute-start.33) | collective-permute-done | bytes 573472 | tf_op jit(solution)/shard_map/ppermute | solution.py:550
  343.7 5.7 collective-permute-done.37.refs_6_
  349.3 7.9 %collective-permute-done.38.refs_7_ = bf16[560,512]{1,0:T(8,128)(2,1)} collective-permute-done((bf16[560,512]{1,0:T(8,128)(2,1)S(1)}, bf16[560,512]{1,0:T(8,128)(2,1)}, u32[]{:S(2)}, u32[]{:S(2)}) %collective-permute-start.38) | collective-permute-done | bytes 573472 | tf_op jit(solution)/shard_map/ppermute | solution.py:550
  362.5 12.6 %collective-permute-done.42.refs_8_ = bf16[560,512]{1,0:T(8,128)(2,1)S(1)} collective-permute-done((bf16[560,512]{1,0:T(8,128)(2,1)}, bf16[560,512]{1,0:T(8,128)(2,1)S(1)}, u32[]{:S(2)}, u32[]{:S(2)}) %collective-permute-start.42) | collective-permute-done | bytes 573472 | tf_op jit(solution)/shard_map/ppermute | solution.py:488
  376.0 52.6 %shard_map.244 = (bf16[512,512]{1,0:T(8,128)(2,1)}, bf16[512,512]{1,0:T(8,128)(2,1)}) custom-call(s32[9]{0:T(128)} %stack.116.place_ref, bf16[512,1024]{1,0:T(8,128)(2,1)} %copy-done.1, bf16[512,1024]{1,0:T(8,128)(2,1)} %copy-done.1, bf16[4096,512]{1,0:T(8,128)(2,1)} %all-gather.9.cloned.1.call-done.q_ref, s32[1,4096]{1,0:T(1,128)} %qmark_ref.1, ...), custom_call_target="tpu_custom_call" | custom-call | flops 1073741824 | bytes 8388608 | tf_op jit(solution)/shard_map/pallas_call | solution.py:431
  435.2 34.9 %reduce-scatter.2.cloned.1.call-done = bf16[64,5248]{1,0:T(8,128)(2,1)} async-done(((bf16[512,5248]{1,0:T(8,128)(2,1)}), bf16[64,5248]{1,0:T(8,128)(2,1)}) %reduce-scatter.2.cloned.1.call-update) | async-done | bytes 671760 | tf_op jit(solution)/shard_map/reduce_scatter | solution.py:762
  475.2 11.2 %collective-permute-done.43 = bf16[256,1024]{1,0:T(8,128)(2,1)S(1)} collective-permute-done((bf16[256,1024]{1,0:T(8,128)(2,1)S(1)}, bf16[256,1024]{1,0:T(8,128)(2,1)S(1)}, u32[]{:S(2)}, u32[]{:S(2)}) %collective-permute-start.43) | collective-permute-done | bytes 524320 | tf_op jit(solution)/shard_map/ppermute | solution.py:488
  491.6 5.7 collective-permute-done.49
  511.3 40.7 %all-reduce.3.cloned.1.call-done = bf16[512,1024]{1,0:T(8,128)(2,1)} async-done(((bf16[512,1024]{1,0:T(8,128)(2,1)}), bf16[512,1024]{1,0:T(8,128)(2,1)}) %all-reduce.3.cloned.1.call-update) | async-done | bytes 1048592 | tf_op jit(solution)/shard_map/psum | solution.py:779
  554.8 86.5 %all-gather.11.cloned.1.call-done = bf16[512,5248]{1,0:T(8,128)(2,1)} async-done(((bf16[64,5248]{1,0:T(8,128)(2,1)}), bf16[512,5248]{1,0:T(8,128)(2,1)}) %all-gather.11.cloned.1.call-update) | async-done | bytes 5373968 | tf_op jit(solution)/shard_map/all_gather | solution.py:761
  652.8 4.7 fusion.166
  (387 shorter events, 231.8 us)
Async XLA Ops:
  8.0 169.3 %all-gather.5.cloned.1.call-start = ((), (), s32[]{:S(2)}) async-start(), calls=%async_computation.1 | async-start | bytes 7208960 | tf_op jit(solution)/shard_map/all_gather | solution.py:585
  37.3 143.9 %all-gather.7.cloned.1.call-start = ((), (), s32[]{:S(2)}) async-start(), calls=%async_computation.2 | async-start | bytes 7208960 | tf_op jit(solution)/shard_map/all_gather | solution.py:585
  38.1 324.4 %all-gather.9.cloned.1.call-start = ((), (), s32[]{:S(2)}) async-start(), calls=%async_computation.3 | async-start | bytes 4718592 | tf_op jit(solution)/shard_map/all_gather | solution.py:659
  38.1 35.3 %collective-permute-start.3 = (bf16[512,1024]{1,0:T(8,128)(2,1)S(1)}, bf16[512,1024]{1,0:T(8,128)(2,1)S(1)}, u32[]{:S(2)}, u32[]{:S(2)}) collective-permute-start(bf16[512,1024]{1,0:T(8,128)(2,1)S(1)} %pad_maximum_fusion.2.refs_1_.refs_2_.refs_0_.k_ref.v_ref), channel_id=1, source_target_pairs={{0,2},{2,0},{4,6},{6,4},{8,10},{10,8},{12,14},{14,12},{1,3},{3,1},... | collective-permute-start | bytes 3145736 | tf_op jit(solution)/shard_map/ppermute | solution.py:488
  39.9 33.5 %collective-permute-start.4 = (bf16[512,1024]{1,0:T(8,128)(2,1)S(1)}, bf16[512,1024]{1,0:T(8,128)(2,1)}, u32[]{:S(2)}, u32[]{:S(2)}) collective-permute-start(bf16[512,1024]{1,0:T(8,128)(2,1)S(1)} %pad_maximum_fusion.2.refs_1_.refs_2_.refs_0_.k_ref.v_ref), channel_id=1, source_target_pairs={{0,4},{2,6},{4,8},{6,10},{8,12},{10,14},{1,5},{3,7},{5,9},{7,11},{... | collective-permute-start | bytes 3145736 | tf_op jit(solution)/shard_map/ppermute | solution.py:540
  73.4 25.0 %collective-permute-start.6 = (bf16[512,1024]{1,0:T(8,128)(2,1)}, bf16[512,1024]{1,0:T(8,128)(2,1)}, u32[]{:S(2)}, u32[]{:S(2)}) collective-permute-start(bf16[512,1024]{1,0:T(8,128)(2,1)} %collective-permute-done.4.refs_6_.refs_7_.refs_3_), channel_id=1, source_target_pairs={{0,2},{2,0},{4,6},{6,4},{8,10},{10,8},{12,14},{14,12},{1,3},{3,1},... | collective-permute-start | bytes 3145736 | tf_op jit(solution)/shard_map/ppermute | solution.py:488
  75.9 24.9 %collective-permute-start.7 = (bf16[512,1024]{1,0:T(8,128)(2,1)}, bf16[512,1024]{1,0:T(8,128)(2,1)}, u32[]{:S(2)}, u32[]{:S(2)}) collective-permute-start(bf16[512,1024]{1,0:T(8,128)(2,1)} %collective-permute-done.4.refs_6_.refs_7_.refs_3_), channel_id=1, source_target_pairs={{0,4},{2,6},{4,8},{6,10},{8,12},{10,14},{1,5},{3,7},{5,9},{7,11},{... | collective-permute-start | bytes 3145736 | tf_op jit(solution)/shard_map/ppermute | solution.py:550
  100.8 22.9 %collective-permute-start.8 = (bf16[512,1024]{1,0:T(8,128)(2,1)}, bf16[512,1024]{1,0:T(8,128)(2,1)S(1)}, u32[]{:S(2)}, u32[]{:S(2)}) collective-permute-start(bf16[512,1024]{1,0:T(8,128)(2,1)} %collective-permute-done.7.refs_3_.refs_4_.refs_5_), channel_id=1, source_target_pairs={{0,2},{2,0},{4,6},{6,4},{8,10},{10,8},{12,14},{14,12},{1,3},{3,1},... | collective-permute-start | bytes 3145736 | tf_op jit(solution)/shard_map/ppermute | solution.py:488
  101.1 24.9 %collective-permute-start.9 = (bf16[512,1024]{1,0:T(8,128)(2,1)}, bf16[512,1024]{1,0:T(8,128)(2,1)S(1)}, u32[]{:S(2)}, u32[]{:S(2)}) collective-permute-start(bf16[512,1024]{1,0:T(8,128)(2,1)} %collective-permute-done.7.refs_3_.refs_4_.refs_5_), channel_id=1, source_target_pairs={{0,4},{2,6},{4,8},{6,10},{8,12},{10,14},{1,5},{3,7},{5,9},{7,11},{... | collective-permute-start | bytes 3145736 | tf_op jit(solution)/shard_map/ppermute | solution.py:550
  129.0 42.5 %collective-permute-start.15 = (bf16[1408,512]{1,0:T(8,128)(2,1)}, bf16[1408,512]{1,0:T(8,128)(2,1)}, u32[]{:S(2)}, u32[]{:S(2)}) collective-permute-start(bf16[1408,512]{1,0:T(8,128)(2,1)} %param.27), channel_id=1, source_target_pairs={{0,1},{1,0},{2,3},{3,2},{4,5},{5,4},{6,7},{7,6},{8,9},{9,8},{10,11... | collective-permute-start | bytes 4325384 | tf_op jit(solution)/shard_map/ppermute | solution.py:488
  130.7 69.9 %collective-permute-start.19 = (f32[1,128]{1,0:T(1,128)S(1)}, f32[1,128]{1,0:T(1,128)S(1)}, u32[]{:S(2)}, u32[]{:S(2)}) collective-permute-start(f32[1,128]{1,0:T(1,128)S(1)} %broadcast_in_dim.8), channel_id=1, source_target_pairs={{0,16},{16,0},{1,17},{17,1},{2,18},{18,2},{3,19},{19,3},{4,20},{20... | collective-permute-start | bytes 1544 | tf_op jit(solution)/shard_map/ppermute | solution.py:488
  142.6 32.9 %collective-permute-start.14 = (bf16[512,512]{1,0:T(8,128)(2,1)}, bf16[512,512]{1,0:T(8,128)(2,1)S(1)}, u32[]{:S(2)}, u32[]{:S(2)}) collective-permute-start(bf16[512,512]{1,0:T(8,128)(2,1)} %collective-permute-done.12), channel_id=1, source_target_pairs={{0,16},{16,0},{1,17},{17,1},{2,18},{18,2},{3,19},{19,3},{4,20},{20... | collective-permute-start | bytes 1572872 | tf_op jit(solution)/shard_map/ppermute | solution.py:488
  150.6 23.6 %collective-permute-start.11 = (bf16[256,512]{1,0:T(8,128)(2,1)S(1)}, bf16[256,512]{1,0:T(8,128)(2,1)S(1)}, u32[]{:S(2)}, u32[]{:S(2)}) collective-permute-start(bf16[256,512]{1,0:T(8,128)(2,1)S(1)} %constant_dynamic-slice_fusion.1), channel_id=1, source_target_pairs={{0,1},{1,0},{2,3},{3,2},{4,5},{5,4},{6,7},{7,6},{8,9},{9,8},{10,11... | collective-permute-start | bytes 786440 | tf_op jit(solution)/shard_map/ppermute | solution.py:488
  153.6 36.1 %collective-permute-start.16 = (bf16[1408,512]{1,0:T(8,128)(2,1)}, bf16[1408,512]{1,0:T(8,128)(2,1)}, u32[]{:S(2)}, u32[]{:S(2)}) collective-permute-start(bf16[1408,512]{1,0:T(8,128)(2,1)} %param.27), channel_id=1, source_target_pairs={{0,16},{16,0},{1,17},{17,1},{2,18},{18,2},{3,19},{19,3},{4,20},{20... | collective-permute-start | bytes 4325384 | tf_op jit(solution)/shard_map/ppermute | solution.py:488
  171.5 24.5 %collective-permute-start.17 = (bf16[1408,512]{1,0:T(8,128)(2,1)}, bf16[1408,512]{1,0:T(8,128)(2,1)}, u32[]{:S(2)}, u32[]{:S(2)}) collective-permute-start(bf16[1408,512]{1,0:T(8,128)(2,1)} %collective-permute-done.15), channel_id=1, source_target_pairs={{0,16},{16,0},{1,17},{17,1},{2,18},{18,2},{3,19},{19,3},{4,20},{20... | collective-permute-start | bytes 4325384 | tf_op jit(solution)/shard_map/ppermute | solution.py:488
  218.4 251.7 %reduce-scatter.2.cloned.1.call-start = ((), (), s32[]{:S(2)}) async-start(), calls=%async_computation.4 | async-start | bytes 6045696 | tf_op jit(solution)/shard_map/reduce_scatter | solution.py:762
  263.6 24.2 %collective-permute-start.27 = (bf16[560,512]{1,0:T(8,128)(2,1)}, bf16[560,512]{1,0:T(8,128)(2,1)}, u32[]{:S(2)}, u32[]{:S(2)}) collective-permute-start(bf16[560,512]{1,0:T(8,128)(2,1)} %get-tuple-element.113.grad_ref.refs_0_), channel_id=1, source_target_pairs={{0,2},{2,0},{4,6},{6,4},{8,10},{10,8},{12,14},{14,12},{1,3},{3,1},... | collective-permute-start | bytes 1720328 | tf_op jit(solution)/shard_map/ppermute | solution.py:488
  264.4 23.4 %collective-permute-start.28 = (bf16[560,512]{1,0:T(8,128)(2,1)}, bf16[560,512]{1,0:T(8,128)(2,1)}, u32[]{:S(2)}, u32[]{:S(2)}) collective-permute-start(bf16[560,512]{1,0:T(8,128)(2,1)} %get-tuple-element.113.grad_ref.refs_0_), channel_id=1, source_target_pairs={{4,0},{6,2},{8,4},{10,6},{12,8},{14,10},{5,1},{7,3},{9,5},{11,7},{... | collective-permute-start | bytes 1720328 | tf_op jit(solution)/shard_map/ppermute | solution.py:540
  272.2 39.2 %collective-permute-start.34 = (bf16[512,1408]{1,0:T(8,128)(2,1)S(1)}, bf16[512,1408]{1,0:T(8,128)(2,1)S(1)}, u32[]{:S(2)}, u32[]{:S(2)}) collective-permute-start(bf16[512,1408]{1,0:T(8,128)(2,1)S(1)} %fusion.8), channel_id=1, source_target_pairs={{0,16},{16,0},{1,17},{17,1},{2,18},{18,2},{3,19},{19,3},{4,20},{20... | collective-permute-start | bytes 4325384 | tf_op jit(solution)/shard_map/ppermute | solution.py:488
  291.0 25.9 %collective-permute-start.32 = (bf16[560,512]{1,0:T(8,128)(2,1)}, bf16[560,512]{1,0:T(8,128)(2,1)S(1)}, u32[]{:S(2)}, u32[]{:S(2)}) collective-permute-start(bf16[560,512]{1,0:T(8,128)(2,1)} %collective-permute-done.28.refs_3_), channel_id=1, source_target_pairs={{0,2},{2,0},{4,6},{6,4},{8,10},{10,8},{12,14},{14,12},{1,3},{3,1},... | collective-permute-start | bytes 1720328 | tf_op jit(solution)/shard_map/ppermute | solution.py:488
  303.0 25.6 %collective-permute-start.33 = (bf16[560,512]{1,0:T(8,128)(2,1)}, bf16[560,512]{1,0:T(8,128)(2,1)S(1)}, u32[]{:S(2)}, u32[]{:S(2)}) collective-permute-start(bf16[560,512]{1,0:T(8,128)(2,1)} %collective-permute-done.28.refs_3_), channel_id=1, source_target_pairs={{4,0},{6,2},{8,4},{10,6},{12,8},{14,10},{5,1},{7,3},{9,5},{11,7},{... | collective-permute-start | bytes 1720328 | tf_op jit(solution)/shard_map/ppermute | solution.py:550
  309.3 26.4 %collective-permute-start.39 = (bf16[512,1408]{1,0:T(8,128)(2,1)S(1)}, bf16[512,1408]{1,0:T(8,128)(2,1)S(1)}, u32[]{:S(2)}, u32[]{:S(2)}) collective-permute-start(bf16[512,1408]{1,0:T(8,128)(2,1)S(1)} %fusion.9), channel_id=1, source_target_pairs={{0,16},{16,0},{1,17},{17,1},{2,18},{18,2},{3,19},{19,3},{4,20},{20... | collective-permute-start | bytes 4325384 | tf_op jit(solution)/shard_map/ppermute | solution.py:488
  357.3 194.7 %all-reduce.3.cloned.1.call-start = ((), (), s32[]{:S(2)}) async-start(), calls=%async_computation.6 | async-start | bytes 2097152 | tf_op jit(solution)/shard_map/psum | solution.py:779
  435.2 206.2 %all-gather.11.cloned.1.call-start = ((), (), s32[]{:S(2)}) async-start(), calls=%async_computation.5 | async-start | bytes 6045696 | tf_op jit(solution)/shard_map/all_gather | solution.py:761
  (113 other events, 1376.8 us)
Sparse Core Ops, SparseCore 0:
  37.4 44.8 all-gather.4
  83.9 43.3 all-gather.6
Sparse Core Ops, SparseCore 1:
  218.5 89.7 all-gather.8
  357.4 112.7 reduce-scatter.1
  474.5 77.5 all-reduce.2
  554.2 87.1 all-gather.10

commit v3 on v2

--- a/solution.py
+++ b/solution.py
@@ -315,7 +315,7 @@
         out_shape=jax.ShapeDtypeStruct((rows, width), BF16),
         compiler_params=pltpu.CompilerParams(vmem_limit_bytes=56 << 20),
         cost_estimate=pl.CostEstimate(
-            flops=16 * rows * length * width,
+            flops=rows * length * width,
             bytes_accessed=4 * length * width,
             transcendentals=rows * length * width // HEAD_DIM,
         ),
@@ -505,6 +505,29 @@
         if sizes["shard"] == 2:
             return in_order(shard, values, flip(values, "shard"), axis)
         return lax.all_gather(values, "shard", axis=axis, tiled=True)
+
+    def ctx_bits():
+        bit = 1
+        while bit < sizes["ctx"]:
+            yield bit
+            bit *= 2
+
+    def reduce_ctx(parts, orders, between):
+        parts, steps = list(parts), len(orders[0])
+        for step in range(steps):
+            for at, order in enumerate(orders):
+                size = parts[at].shape[0] // 2
+                side = (ctx // order[step]) % 2
+                kept = lax.dynamic_slice_in_dim(parts[at], side * size, size, 0)
+                sent = lax.dynamic_slice_in_dim(parts[at], (1 - side) * size, size, 0)
+                got = flip(sent, "ctx", order[step])
+                parts[at] = (kept.astype(F32) + got.astype(F32)).astype(BF16)
+            parts = between(step, parts)
+        for step in reversed(range(steps)):
+            for at, order in enumerate(orders):
+                side = (ctx // order[step]) % 2
+                parts[at] = in_order(side, parts[at], flip(parts[at], "ctx", order[step]), 0)
+        return parts
 
     def rows_of(values, position):
         return lax.dynamic_slice_in_dim(values, position * own_rows, own_rows, 0)
@@ -554,6 +577,24 @@
             stages.append([(across, jnp.where(exists, 2 * there + 1 - column, -1))])
         return stages, rows
 
+    def shard_reduce(term, slice_rows):
+        if sizes["shard"] == 2:
+            return term(shard) + flip(term(1 - shard).astype(BF16), "shard").astype(F32)
+        whole = jnp.concatenate(
+            [term(i) for i in range(sizes["shard"])], axis=0 if slice_rows else 1
+        )
+        return lax.psum_scatter(
+            whole.astype(BF16), "shard", scatter_dimension=0 if slice_rows else 1, tiled=True
+        ).astype(F32)
+
+    def over_rows(lefts, rights, slice_left):
+        def term(position):
+            if slice_left:
+                return sum(tn(cols_of(a, position, part), b) for a, b in zip(lefts, rights))
+            return sum(tn(a, cols_of(b, position, part)) for a, b in zip(lefts, rights))
+
+        return shard_reduce(term, slice_left).astype(BF16)
+
     mine = tokens.reshape(own_rows, width)
     first_own = value_first.reshape(own_rows, width)
     key_marks = blocks.reshape(-1)
@@ -576,21 +617,12 @@
         [qkv[:, half : 2 * half], 0.5 * qkv[:, 2 * half :] + 0.5 * first_group], axis=1
     ).astype(BF16)
 
-    def pair_up(gathered):
-        return [
-            lax.dynamic_index_in_dim(gathered, at, 0, keepdims=False) for at in (tp, 1 - tp)
-        ]
-
-    def gather_rows(values):
-        gathered = lax.all_gather(values, ("tp", "shard"), axis=0, tiled=True)
-        return pair_up(gathered.reshape(sizes["tp"], width, values.shape[1]))
-
     def gather_blocks(values):
         if sizes["shard"] == 2:
             both = [values, flip(values, "tp")]
             return [[one, flip(one, "shard")] for one in both]
-        gathered = lax.all_gather(values, ("tp", "shard"), axis=0, tiled=False)
-        gathered = pair_up(gathered.reshape(sizes["tp"], sizes["shard"], *values.shape))
+        both = [values, flip(values, "tp")]
+        gathered = [lax.all_gather(one, "shard", axis=0, tiled=False) for one in both]
         return [[one[i] for i in range(sizes["shard"])] for one in gathered]
 
     def block_of(values, at):
@@ -614,9 +646,12 @@
     def times_turned(left, blocks):
         return sum(nt(block_of(left, at), block) for at, block in enumerate(blocks))
 
-    kv, w_gate, w_up, w_down, w_out = lax.optimization_barrier((kv, w_gate, w_up, w_down, w_out))
-    outs, downs = gather_blocks(w_out), gather_blocks(w_down)
-    gates, ups = gather_rows(w_gate), gather_rows(w_up)
+    kv, w_gate, w_up, w_down, w_out, count = lax.optimization_barrier(
+        (kv, w_gate, w_up, w_down, w_out, count)
+    )
+    outs = gather_blocks(w_out)
+    gate_weight, up_weight = shard_gather(w_gate, 0), shard_gather(w_up, 0)
+    down_weight = shard_gather(w_down, 1)
 
     qmark, kmark = query_marks.reshape(1, -1), key_marks.reshape(-1, 1)
     forward = {"state": None, "pieces": [(kv, 0, query_marks.reshape(-1, 1))]}
@@ -661,64 +696,59 @@
     inputs = mine.astype(F32)
     hidden = inputs + times_blocks(att, outs)
     normed_two = rms_norm(hidden, gain_ffn).astype(BF16)
-    gate = [nn(normed_two, w) for w in gates]
-    up = [nn(normed_two, w) for w in ups]
-    logistic = [jax.nn.sigmoid(g) for g in gate]
-    act = [(g * s * u).astype(BF16) for g, s, u in zip(gate, logistic, up)]
-    normed_pair = flip(normed_two, "tp")
-    final = hidden + times_blocks(act, downs)
-    final, normed_pair = lax.optimization_barrier((final, normed_pair))
-    act_two = flip(act[1], "tp")
+    normed = [normed_two, flip(normed_two, "tp")]
+    gate, up, logistic, act = [], [], [], []
+
+    def widen(rows):
+        gate.append(nn(rows, gate_weight))
+        up.append(nn(rows, up_weight))
+        logistic.append(jax.nn.sigmoid(gate[-1]))
+        act.append((gate[-1] * logistic[-1] * up[-1]).astype(BF16))
+
+    widen(normed[0])
+    normed[1], act[0] = lax.optimization_barrier((normed[1], act[0]))
+    widen(normed[1])
+    down_theirs = flip(nn(act[1], down_weight).astype(BF16), "tp")
+    final = hidden + (nn(act[0], down_weight) + down_theirs.astype(F32))
     difference = final - teacher.reshape(own_rows, width).astype(F32)
     local_error = jnp.sum(jnp.mean(difference * difference, axis=1) * keep)
     token_total = group_rows * sizes["ctx"] * sizes["shard"]
     grad_final = token_total / count * keep[:, None] * difference
     grad_round = grad_final.astype(BF16)
-    grad_act = [times_turned(grad_round, w) for w in downs]
-    grad_gate = [
-        (a * u * s * (1.0 + g * (1.0 - s))).astype(BF16)
-        for a, u, s, g in zip(grad_act, up, logistic, gate)
-    ]
-    grad_up = [(a * g * s).astype(BF16) for a, g, s in zip(grad_act, gate, logistic)]
-    grad_gate[0], act_two, round_sent = lax.optimization_barrier(
-        (grad_gate[0], act_two, grad_round)
-    )
-    round_two = flip(round_sent, "tp")
-    grad_two = (
-        nt(grad_gate[0], gates[0])
-        + nt(grad_gate[1], gates[1])
-        + nt(grad_up[0], ups[0])
-        + nt(grad_up[1], ups[1])
-    )
+    rounds = [grad_round, flip(grad_round, "tp")]
+    grad_gate, grad_up = [], []
+
+    def back(at):
+        grad_act = nt(rounds[at], down_weight)
+        part = grad_act * logistic[at]
+        grad_gate.append((part * up[at] * (1.0 + gate[at] * (1.0 - logistic[at]))).astype(BF16))
+        grad_up.append((part * gate[at]).astype(BF16))
+
+    back(0)
+    rounds[1], grad_gate[0], grad_up[0] = lax.optimization_barrier(
+        (rounds[1], grad_gate[0], grad_up[0])
+    )
+    back(1)
+    two_sent = (nt(grad_gate[1], gate_weight) + nt(grad_up[1], up_weight)).astype(BF16)
+    two_theirs = flip(two_sent, "tp")
+    gate_part = over_rows(normed, grad_gate, True)
+    up_part = over_rows(normed, grad_up, True)
+    down_part = over_rows(rounds, act, True)
+    two_own = nt(grad_gate[0], gate_weight) + nt(grad_up[0], up_weight)
+    two_theirs, two_own, gate_part, up_part, down_part = lax.optimization_barrier(
+        (two_theirs, two_own, gate_part, up_part, down_part)
+    )
+    grad_two = two_own + two_theirs.astype(F32)
     hidden_part, gain_ffn_term = jax.vjp(rms_norm, hidden, gain_ffn)[1](grad_two)
     grad_hidden = grad_final + hidden_part
     hidden_round = grad_hidden.astype(BF16)
     grad_att = [times_turned(hidden_round, w).astype(BF16) for w in outs]
-    grad_theirs, round_two = lax.optimization_barrier((flip(grad_att[1], "tp"), round_two))
+    grad_theirs = flip(grad_att[1], "tp")
     sent, stat = pack_gradient(
         tp.reshape(1).astype(jnp.int32), grad_att[0], grad_theirs, attended, lse
     )
 
-    sent, hidden_sent, gate_sent = lax.optimization_barrier((sent, hidden_round, grad_gate[1]))
-    hidden_two, gate_two = flip(hidden_sent, "tp"), flip(gate_sent, "tp")
-
-    def shard_reduce(term, slice_rows):
-        if sizes["shard"] == 2:
-            return term(shard) + flip(term(1 - shard).astype(BF16), "shard").astype(F32)
-        whole = jnp.concatenate(
-            [term(i) for i in range(sizes["shard"])], axis=0 if slice_rows else 1
-        )
-        return lax.psum_scatter(
-            whole.astype(BF16), "shard", scatter_dimension=0 if slice_rows else 1, tiled=True
-        ).astype(F32)
-
-    def over_rows(lefts, rights, slice_left):
-        def term(position):
-            if slice_left:
-                return sum(tn(cols_of(a, position, part), b) for a, b in zip(lefts, rights))
-            return sum(tn(a, cols_of(b, position, part)) for a, b in zip(lefts, rights))
-
-        return shard_reduce(term, slice_left).astype(BF16)
+    hidden_two = flip(hidden_round, "tp")
 
     kv_pieces = [(kv, ctx), (kv_next, jnp.where(ctx + 1 < 2 * line, ctx + 1, -1))]
     kv_pieces += [piece for stage in stages for piece in stage]
@@ -726,28 +756,30 @@
 
     def grad_between(at, arrays):
         if at == 0:
-            parts["query_grad"] = query_gradient(queries, sent, stat, kv_pieces, qmark, kmark)
-            parts["hidden_two"], parts["gate_two"] = hidden_two, gate_two
-            hold = ["query_grad", "hidden_two", "gate_two"]
-        elif at == 1:
-            query_grad, up_sent = lax.optimization_barrier((parts["query_grad"], grad_up[1]))
-            parts["query_grad"] = query_grad
-            parts["up_two"] = flip(up_sent, "tp")
-            parts["down"] = over_rows([grad_round, round_two], [act[0], act_two], True)
+            *arrays, hidden_held = lax.optimization_barrier((*arrays[:-1], arrays[-1], hidden_two)) if len(arrays) < 3 else (
+                *arrays[:2],
+                *lax.optimization_barrier((arrays[2], hidden_two)),
+            )
             parts["out"] = over_rows(
-                [hidden_round, parts["hidden_two"]],
+                [hidden_round, hidden_held],
                 [rows_of(attended, tp), rows_of(attended, 1 - tp)],
                 True,
             )
-            hold = ["down", "out", "up_two"]
-        elif at == 2:
-            parts["gate"] = over_rows([normed_two, normed_pair], [grad_gate[0], parts["gate_two"]], True)
-            parts["up"] = over_rows([normed_two, normed_pair], [grad_up[0], parts["up_two"]], True)
-            parts["query"] = over_rows([normed_one], [parts["query_grad"]], True)
             parts["all"] = jnp.concatenate(
-                [parts[name] for name in ("gate", "up", "down", "query", "out")], axis=1
+                [gate_part, up_part, down_part, parts["out"]], axis=1
             )
             hold = ["all"]
+        elif at == 1:
+            held_stat, parts["q_all"], parts["all"] = lax.optimization_barrier(
+                (stat, q_all, parts["all"])
+            )
+            parts["query_grad"] = query_gradient(
+                queries, sent, held_stat, kv_pieces, qmark, kmark
+            )
+            hold = ["query_grad"]
+        elif at == 2:
+            parts["query"] = over_rows([normed_one], [parts["query_grad"]], True)
+            hold = ["query"]
         else:
             return arrays
         held = lax.optimization_barrier((*arrays, *[parts[name] for name in hold]))
@@ -758,32 +790,48 @@
         sent, -1, slice(group_rows - BOUNDARY, None), grad_between
     )
     query_grad = parts["query_grad"]
-    weight_grads = lax.all_gather(
-        lax.psum_scatter(parts["all"], "ctx", scatter_dimension=0, tiled=True),
-        "ctx",
-        axis=0,
-        tiled=True,
-    ).astype(F32)
-    hidden_half = w_gate.shape[1]
-    ends = [hidden_half, 2 * hidden_half, 3 * hidden_half, 3 * hidden_half + half]
-    w_gate_grad, w_up_grad, w_down_grad, w_query_grad, w_out_grad = jnp.split(
-        weight_grads, ends, axis=1
-    )
+    scattered = lax.psum_scatter(parts["all"], "ctx", scatter_dimension=0, tiled=True)
     grad_pieces = [(sent, ctx), (sent_before, ctx - 1)]
     grad_pieces += [piece for stage in grad_stages for piece in stage]
     key_grad, value_half = key_gradient(
-        kv, q_all, grad_pieces, key_marks.reshape(1, -1), query_marks.reshape(-1, 1)
+        kv, parts["q_all"], grad_pieces, key_marks.reshape(1, -1), query_marks.reshape(-1, 1)
+    )
+    scattered, key_grad, value_half = lax.optimization_barrier(
+        (scattered, key_grad, value_half)
+    )
+    weight_grads = lax.all_gather(scattered, "ctx", axis=0, tiled=True).astype(F32)
+    hidden_half = w_gate.shape[1]
+    w_gate_grad, w_up_grad, w_down_grad, w_out_grad = jnp.split(
+        weight_grads, [hidden_half, 2 * hidden_half, 3 * hidden_half], axis=1
     )
     grads = jnp.concatenate([query_grad, key_grad, value_half], axis=1)
-    kv_part = over_rows([normed_one], [grads[:, half:]], True)
-    kv_grad = lax.psum(kv_part, "ctx").astype(F32)
-    grad_one_theirs = flip(nt(rows_of(grads, 1 - tp), weight_qkv).astype(BF16), "tp")
-    grad_one = nt(rows_of(grads, tp), weight_qkv) + grad_one_theirs.astype(F32)
+    key_part = over_rows([normed_one], [key_grad], True)
+    value_part = over_rows([normed_one], [value_half], True)
+    last = {}
+
+    def finish(step, parts):
+        if step == 0:
+            *parts, held = lax.optimization_barrier((*parts, grads))
+            theirs = flip(nt(rows_of(held, 1 - tp), weight_qkv).astype(BF16), "tp")
+            last["own"] = nt(rows_of(held, tp), weight_qkv)
+            last["theirs"] = theirs
+            last["value"] = flip(rows_of(held[:, 2 * half :], 1 - tp), "tp")
+        if step == 1:
+            *parts, last["own"], last["theirs"], last["value"] = lax.optimization_barrier(
+                (*parts, last["own"], last["theirs"], last["value"])
+            )
+        return parts
+
+    bits = list(ctx_bits())
+    w_query_grad, w_key_grad, w_value_grad = reduce_ctx(
+        [parts["query"], key_part, value_part],
+        [bits[2:] + bits[:2], bits, bits[1:] + bits[:1]],
+        finish,
+    )
+    grad_one = last["own"] + last["theirs"].astype(F32)
     input_part, gain_attn_term = jax.vjp(rms_norm, inputs, gain_attn)[1](grad_one)
     tokens_grad = grad_hidden + input_part
-    first_grad = in_order(
-        tp, rows_of(value_half, tp), flip(rows_of(value_half, 1 - tp), "tp"), 1
-    ).astype(F32)
+    first_grad = in_order(tp, rows_of(value_half, tp), last["value"], 1).astype(F32)
 
     small = jnp.concatenate(
         [gain_attn_term, gain_ffn_term, jnp.broadcast_to(local_error, (128,))]
@@ -796,9 +844,9 @@
         first_grad.reshape(1, own_rows, width),
         small[:width],
         small[width : 2 * width],
-        w_query_grad,
-        kv_grad[:, :half],
-        kv_grad[:, half:],
+        w_query_grad.astype(F32),
+        w_key_grad.astype(F32),
+        w_value_grad.astype(F32),
         w_out_grad.T,
         w_gate_grad,
         w_up_grad,

time: 674 us -> 565 us (0.84)
  waiting for transfers between devices: 347 us -> 260 us
  matrix products: 77.7 us -> 49.4 us
  local copies, waits for them, and re-layouts: 42.6 us -> 27 us
  starting transfers between devices: 75.1 us -> 88.9 us
  other arithmetic: 18.6 us -> 29.4 us
    all_gather x3 -> x1, waiting for transfers between devices: 86.5 us -> 0.01 us  [on_device(): lax.all_gather(scattered, 'ctx', axis=0, tiled=True).astype(F32)]
    ppermute x43 -> x61, waiting for transfers between devices: 160 us -> 222 us  [flip(): lax.ppermute(values, axis, [(i, i ^ bit) for i in range(sizes[axis])])]
    psum x1 -> x0, waiting for transfers between devices: 40.7 us -> none  [on_device(): kv_grad = lax.psum(kv_part, 'ctx').astype(F32)]
    reduce_scatter x1, waiting for transfers between devices: 34.9 us -> 0.02 us  [on_device(): lax.psum_scatter(parts['all'], 'ctx', scatter_dimension=0, tiled=True)]
    dot_general x47 -> x45, matrix products: 77.7 us -> 49.4 us  [dot(): lax.dot_general(left, right, (((left_dim,), (right_dim,)), ((), ())), pre...]
    ppermute x43 -> x61, starting transfers between devices: 53.7 us -> 69.9 us  [flip(): lax.ppermute(values, axis, [(i, i ^ bit) for i in range(sizes[axis])])]
    unnamed x167 -> x172, local copies, waits for them, and re-layouts: 22 us -> 11.4 us
    ppermute x4, waiting for transfers between devices: 24.4 us -> 34 us  [spread(): moving = lax.ppermute(moving, 'ctx', along)]
  transfers between devices with their start and end apart: 57 -> 72, of which waited for: 31 -> 40; matrix products, arithmetic and copies ran while one was open for 16% -> 14% of each run, Pallas kernels for 13% -> 15%
where the time goes in v3:
time: 565 us; the launch traced here: 557 us
  waiting for transfers between devices  260 us (46%)
  starting transfers between devices  88.9 us (16%)
  Pallas kernels  83.7 us (15%)
  matrix products  49.4 us (9%)
  other arithmetic  29.4 us (5%)
  local copies, waits for them, and re-layouts  27 us (5%)
  between operations  18.8 us (3%)
    ppermute x61, waiting for transfers between devices, flip(): lax.ppermute(values, axis, [(i, i ^ bit) for i in range(sizes[axis])])  222 us
    ppermute x61, starting transfers between devices, flip(): lax.ppermute(values, axis, [(i, i ^ bit) for i in range(sizes[axis])])  69.9 us
    pallas_call x1, Pallas kernels, key_gradient(): pl.pallas_call(functools.partial(key_kernel, sizes, step_queries), grid_s...  53 us
    dot_general x45, matrix products, dot(): lax.dot_general(left, right, (((left_dim,), (right_dim,)), ((), ())), pre...  49.4 us
    ppermute x4, waiting for transfers between devices, spread(): moving = lax.ppermute(moving, 'ctx', along)  34 us
    pallas_call x1, Pallas kernels, query_gradient(): pl.pallas_call(functools.partial(query_kernel, sizes, step_keys), grid_sp...  14.4 us
    pallas_call x5, Pallas kernels, forward_stage(): pl.pallas_call(functools.partial(forward_kernel, [m is not None for _, _,...  13.9 us
    unnamed x172, local copies, waits for them, and re-layouts  11.4 us
  transfers between devices with their start and end apart: 72, of which 40 were waited for; matrix products, arithmetic and copies ran while one was open for 14% of the time, Pallas kernels for 15%

profile of v3, /device:TPU:0, one launch (start us, length us, event | category | flops | bytes accessed | tf_op | source)
XLA Modules:
  0.0 557.2 jit_solution(10971413901181347200)
XLA Ops:
  54.4 17.6 %collective-permute-done.8.refs_4_.refs_5_.refs_2_ = bf16[512,1024]{1,0:T(8,128)(2,1)S(1)} collective-permute-done((bf16[512,1024]{1,0:T(8,128)(2,1)S(1)}, bf16[512,1024]{1,0:T(8,128)(2,1)S(1)}, u32[]{:S(2)}, u32[]{:S(2)}) %collective-permute-start.8) | collective-permute-done | bytes 1048608 | tf_op jit(solution)/shard_map/ppermute | solution.py:488
  85.7 7.0 %collective-permute-done.11.refs_1_.refs_2_.refs_4_ = bf16[512,1024]{1,0:T(8,128)(2,1)S(1)} collective-permute-done((bf16[512,1024]{1,0:T(8,128)(2,1)}, bf16[512,1024]{1,0:T(8,128)(2,1)S(1)}, u32[]{:S(2)}, u32[]{:S(2)}) %collective-permute-start.11) | collective-permute-done | bytes 1048608 | tf_op jit(solution)/shard_map/ppermute | solution.py:488
  102.4 16.5 %collective-permute-done.13.refs_1_.refs_2_.refs_6_ = bf16[512,1024]{1,0:T(8,128)(2,1)S(1)} collective-permute-done((bf16[512,1024]{1,0:T(8,128)(2,1)S(1)}, bf16[512,1024]{1,0:T(8,128)(2,1)S(1)}, u32[]{:S(2)}, u32[]{:S(2)}) %collective-permute-start.13) | collective-permute-done | bytes 1048608 | tf_op jit(solution)/shard_map/ppermute | solution.py:488
  123.9 21.8 %collective-permute-done.15.refs_1_.refs_2_.refs_8_ = bf16[512,1024]{1,0:T(8,128)(2,1)S(1)} collective-permute-done((bf16[512,1024]{1,0:T(8,128)(2,1)S(1)}, bf16[512,1024]{1,0:T(8,128)(2,1)S(1)}, u32[]{:S(2)}, u32[]{:S(2)}) %collective-permute-start.15) | collective-permute-done | bytes 1048608 | tf_op jit(solution)/shard_map/ppermute | solution.py:488
  159.3 7.1 %collective-permute-done.20 = bf16[256,1024]{1,0:T(8,128)(2,1)S(1)} collective-permute-done((bf16[256,1024]{1,0:T(8,128)(2,1)S(1)}, bf16[256,1024]{1,0:T(8,128)(2,1)S(1)}, u32[]{:S(2)}, u32[]{:S(2)}) %collective-permute-start.20) | collective-permute-done | bytes 524320 | tf_op jit(solution)/shard_map/ppermute | solution.py:488
  174.1 8.0 %collective-permute-done.24 = bf16[256,1024]{1,0:T(8,128)(2,1)} collective-permute-done((bf16[256,1024]{1,0:T(8,128)(2,1)}, bf16[256,1024]{1,0:T(8,128)(2,1)}, u32[]{:S(2)}, u32[]{:S(2)}) %collective-permute-start.24) | collective-permute-done | bytes 524320 | tf_op jit(solution)/shard_map/ppermute | solution.py:488
  187.8 7.0 %collective-permute-done.25 = bf16[256,1024]{1,0:T(8,128)(2,1)S(1)} collective-permute-done((bf16[256,1024]{1,0:T(8,128)(2,1)S(1)}, bf16[256,1024]{1,0:T(8,128)(2,1)S(1)}, u32[]{:S(2)}, u32[]{:S(2)}) %collective-permute-start.25) | collective-permute-done | bytes 524320 | tf_op jit(solution)/shard_map/ppermute | solution.py:488
  213.8 7.3 %collective-permute-done.26 = bf16[256,1024]{1,0:T(8,128)(2,1)S(1)} collective-permute-done((bf16[256,1024]{1,0:T(8,128)(2,1)S(1)}, bf16[256,1024]{1,0:T(8,128)(2,1)S(1)}, u32[]{:S(2)}, u32[]{:S(2)}) %collective-permute-start.26) | collective-permute-done | bytes 524320 | tf_op jit(solution)/shard_map/ppermute | solution.py:488
  228.1 5.7 %collective-permute-done.30.other_ref = bf16[256,512]{1,0:T(8,128)(2,1)S(1)} collective-permute-done((bf16[256,512]{1,0:T(8,128)(2,1)S(1)}, bf16[256,512]{1,0:T(8,128)(2,1)S(1)}, u32[]{:S(2)}, u32[]{:S(2)}) %collective-permute-start.30) | collective-permute-done | bytes 262176 | tf_op jit(solution)/shard_map/ppermute | solution.py:488
  245.7 10.7 %collective-permute-start.31 = (bf16[560,512]{1,0:T(8,128)(2,1)}, bf16[560,512]{1,0:T(8,128)(2,1)S(1)}, u32[]{:S(2)}, u32[]{:S(2)}) collective-permute-start(bf16[560,512]{1,0:T(8,128)(2,1)} %get-tuple-element.129.grad_ref.refs_0_), channel_id=1, source_target_pairs={{0,2},{2,0},{4,6},{6,4},{8,10},{10,8},{12,14},{14,12},{1,3},{3,1},... | collective-permute-start | bytes 1720328 | tf_op jit(solution)/shard_map/ppermute | solution.py:488
  261.4 8.8 %collective-permute-done.31.refs_2_ = bf16[560,512]{1,0:T(8,128)(2,1)S(1)} collective-permute-done((bf16[560,512]{1,0:T(8,128)(2,1)}, bf16[560,512]{1,0:T(8,128)(2,1)S(1)}, u32[]{:S(2)}, u32[]{:S(2)}) %collective-permute-start.31) | collective-permute-done | bytes 573472 | tf_op jit(solution)/shard_map/ppermute | solution.py:488
  280.2 14.4 %shard_map.243 = bf16[512,512]{1,0:T(8,128)(2,1)} custom-call(s32[9]{0:T(128)} %stack.107.place_ref, bf16[512,512]{1,0:T(8,128)(2,1)} %copy-done.3, bf16[560,512]{1,0:T(8,128)(2,1)} %get-tuple-element.129.grad_ref.refs_0_, f32[16,512]{1,0:T(8,128)} %get-tuple-element.139.stat_ref, s32[1,512]{1,0:T(1,128)} %copy-done.8, s32[4096,1]{1,0:T(8,128)} %copy.35.kmark_ref, ...), custom_call_target="tpu_custom_call" | custom-call | flops 1073741824 | bytes 8388608 | tf_op jit(solution)/shard_map/pallas_call | solution.py:295
  295.6 16.1 %collective-permute-done.37.refs_5_ = bf16[560,512]{1,0:T(8,128)(2,1)} collective-permute-done((bf16[560,512]{1,0:T(8,128)(2,1)}, bf16[560,512]{1,0:T(8,128)(2,1)}, u32[]{:S(2)}, u32[]{:S(2)}) %collective-permute-start.37) | collective-permute-done | bytes 573472 | tf_op jit(solution)/shard_map/ppermute | solution.py:573
  317.7 12.0 %collective-permute-done.38.refs_6_ = bf16[560,512]{1,0:T(8,128)(2,1)} collective-permute-done((bf16[560,512]{1,0:T(8,128)(2,1)}, bf16[560,512]{1,0:T(8,128)(2,1)}, u32[]{:S(2)}, u32[]{:S(2)}) %collective-permute-start.38) | collective-permute-done | bytes 573472 | tf_op jit(solution)/shard_map/ppermute | solution.py:488
  329.7 14.2 %collective-permute-done.39.refs_7_ = bf16[560,512]{1,0:T(8,128)(2,1)} collective-permute-done((bf16[560,512]{1,0:T(8,128)(2,1)}, bf16[560,512]{1,0:T(8,128)(2,1)}, u32[]{:S(2)}, u32[]{:S(2)}) %collective-permute-start.39) | collective-permute-done | bytes 573472 | tf_op jit(solution)/shard_map/ppermute | solution.py:573
  349.8 15.1 %collective-permute-done.42.refs_8_ = bf16[560,512]{1,0:T(8,128)(2,1)S(1)} collective-permute-done((bf16[560,512]{1,0:T(8,128)(2,1)}, bf16[560,512]{1,0:T(8,128)(2,1)S(1)}, u32[]{:S(2)}, u32[]{:S(2)}) %collective-permute-start.42) | collective-permute-done | bytes 573472 | tf_op jit(solution)/shard_map/ppermute | solution.py:488
  365.7 53.0 %shard_map.244 = (bf16[512,512]{1,0:T(8,128)(2,1)}, bf16[512,512]{1,0:T(8,128)(2,1)}) custom-call(s32[9]{0:T(128)} %stack.116.place_ref, bf16[512,1024]{1,0:T(8,128)(2,1)} %copy-done.2, bf16[512,1024]{1,0:T(8,128)(2,1)} %copy-done.2, bf16[4096,512]{1,0:T(8,128)(2,1)} %all-gather.3.cloned.1.call-done.q_ref, s32[1,4096]{1,0:T(1,128)} %qmark_ref.1, ...), custom_call_target="tpu_custom_call" | custom-call | flops 1073741824 | bytes 8388608 | tf_op jit(solution)/shard_map/pallas_call | solution.py:431
  429.1 9.1 %collective-permute-done.44 = bf16[256,512]{1,0:T(8,128)(2,1)S(1)} collective-permute-done((bf16[256,512]{1,0:T(8,128)(2,1)S(1)}, bf16[256,512]{1,0:T(8,128)(2,1)S(1)}, u32[]{:S(2)}, u32[]{:S(2)}) %collective-permute-start.44) | collective-permute-done | bytes 262176 | tf_op jit(solution)/shard_map/ppermute | solution.py:488
  438.3 9.7 %collective-permute-done.46 = bf16[256,512]{1,0:T(8,128)(2,1)S(1)} collective-permute-done((bf16[256,512]{1,0:T(8,128)(2,1)S(1)}, bf16[256,512]{1,0:T(8,128)(2,1)S(1)}, u32[]{:S(2)}, u32[]{:S(2)}) %collective-permute-start.46) | collective-permute-done | bytes 262176 | tf_op jit(solution)/shard_map/ppermute | solution.py:488
  456.2 6.1 %collective-permute-done.48 = bf16[128,512]{1,0:T(8,128)(2,1)S(1)} collective-permute-done((bf16[128,512]{1,0:T(8,128)(2,1)S(1)}, bf16[128,512]{1,0:T(8,128)(2,1)S(1)}, u32[]{:S(2)}, u32[]{:S(2)}) %collective-permute-start.48) | collective-permute-done | bytes 131104 | tf_op jit(solution)/shard_map/ppermute | solution.py:488
  480.5 5.3 collective-permute-done.55
  505.7 9.1 %collective-permute-done.63 = bf16[128,512]{1,0:T(8,128)(2,1)S(1)} collective-permute-done((bf16[128,512]{1,0:T(8,128)(2,1)S(1)}, bf16[128,512]{1,0:T(8,128)(2,1)S(1)}, u32[]{:S(2)}, u32[]{:S(2)}) %collective-permute-start.63) | collective-permute-done | bytes 131104 | tf_op jit(solution)/shard_map/ppermute | solution.py:488
  516.7 7.8 %collective-permute-done.67 = bf16[128,512]{1,0:T(8,128)(2,1)S(1)} collective-permute-done((bf16[128,512]{1,0:T(8,128)(2,1)S(1)}, bf16[128,512]{1,0:T(8,128)(2,1)S(1)}, u32[]{:S(2)}, u32[]{:S(2)}) %collective-permute-start.67) | collective-permute-done | bytes 131104 | tf_op jit(solution)/shard_map/ppermute | solution.py:488
  524.6 6.8 %collective-permute-done.60 = bf16[256,512]{1,0:T(8,128)(2,1)S(1)} collective-permute-done((bf16[256,512]{1,0:T(8,128)(2,1)S(1)}, bf16[256,512]{1,0:T(8,128)(2,1)S(1)}, u32[]{:S(2)}, u32[]{:S(2)}) %collective-permute-start.60) | collective-permute-done | bytes 262176 | tf_op jit(solution)/shard_map/ppermute | solution.py:488
  (453 shorter events, 242.2 us)
Async XLA Ops:
  7.2 267.1 %all-gather.3.cloned.1.call-start = ((), (), s32[]{:S(2)}) async-start(), calls=%async_computation.1 | async-start | bytes 4718592 | tf_op jit(solution)/shard_map/all_gather | solution.py:694
  7.3 25.9 %collective-permute-start = (bf16[256,1024]{1,0:T(8,128)(2,1)}, bf16[256,1024]{1,0:T(8,128)(2,1)S(1)}, u32[]{:S(2)}, u32[]{:S(2)}) collective-permute-start(bf16[256,1024]{1,0:T(8,128)(2,1)} %bitcast.115), channel_id=1, source_target_pairs={{0,1},{1,0},{2,3},{3,2},{4,5},{5,4},{6,7},{7,6},{8,9},{9,8},{10,11... | collective-permute-start | bytes 1572872 | tf_op jit(solution)/shard_map/ppermute | solution.py:488
  12.6 21.5 %collective-permute-start.1 = (bf16[512,1536]{1,0:T(8,128)(2,1)S(1)}, bf16[512,1536]{1,0:T(8,128)(2,1)}, u32[]{:S(2)}, u32[]{:S(2)}) collective-permute-start(bf16[512,1536]{1,0:T(8,128)(2,1)S(1)} %constant_dynamic-update-slice_fusion), channel_id=1, source_target_pairs={{0,16},{16,0},{1,17},{17,1},{2,18},{18,2},{3,19},{19,3},{4,20},{20... | collective-permute-start | bytes 4718600 | tf_op jit(solution)/shard_map/ppermute | solution.py:488
  38.6 33.4 %collective-permute-start.8 = (bf16[512,1024]{1,0:T(8,128)(2,1)S(1)}, bf16[512,1024]{1,0:T(8,128)(2,1)S(1)}, u32[]{:S(2)}, u32[]{:S(2)}) collective-permute-start(bf16[512,1024]{1,0:T(8,128)(2,1)S(1)} %pad_maximum_fusion.7.refs_1_.refs_2_.refs_0_.k_ref.v_ref), channel_id=1, source_target_pairs={{0,2},{2,0},{4,6},{6,4},{8,10},{10,8},{12,14},{14,12},{1,3},{3,1},... | collective-permute-start | bytes 3145736 | tf_op jit(solution)/shard_map/ppermute | solution.py:488
  40.1 31.9 %collective-permute-start.9 = (bf16[512,1024]{1,0:T(8,128)(2,1)S(1)}, bf16[512,1024]{1,0:T(8,128)(2,1)}, u32[]{:S(2)}, u32[]{:S(2)}) collective-permute-start(bf16[512,1024]{1,0:T(8,128)(2,1)S(1)} %pad_maximum_fusion.7.refs_1_.refs_2_.refs_0_.k_ref.v_ref), channel_id=1, source_target_pairs={{0,4},{2,6},{4,8},{6,10},{8,12},{10,14},{1,5},{3,7},{5,9},{7,11},{... | collective-permute-start | bytes 3145736 | tf_op jit(solution)/shard_map/ppermute | solution.py:563
  44.6 38.8 %collective-permute-start.21 = (bf16[512,1408]{1,0:T(8,128)(2,1)}, bf16[512,1408]{1,0:T(8,128)(2,1)}, u32[]{:S(2)}, u32[]{:S(2)}) collective-permute-start(bf16[512,1408]{1,0:T(8,128)(2,1)} %param.25), channel_id=1, source_target_pairs={{0,16},{16,0},{1,17},{17,1},{2,18},{18,2},{3,19},{19,3},{4,20},{20... | collective-permute-start | bytes 4325384 | tf_op jit(solution)/shard_map/ppermute | solution.py:488
  48.2 47.0 %collective-permute-start.22 = (bf16[512,1408]{1,0:T(8,128)(2,1)}, bf16[512,1408]{1,0:T(8,128)(2,1)}, u32[]{:S(2)}, u32[]{:S(2)}) collective-permute-start(bf16[512,1408]{1,0:T(8,128)(2,1)} %param.26), channel_id=1, source_target_pairs={{0,16},{16,0},{1,17},{17,1},{2,18},{18,2},{3,19},{19,3},{4,20},{20... | collective-permute-start | bytes 4325384 | tf_op jit(solution)/shard_map/ppermute | solution.py:488
  53.1 32.1 %collective-permute-start.17 = (bf16[512,512]{1,0:T(8,128)(2,1)S(1)}, bf16[512,512]{1,0:T(8,128)(2,1)S(1)}, u32[]{:S(2)}, u32[]{:S(2)}) collective-permute-start(bf16[512,512]{1,0:T(8,128)(2,1)S(1)} %copy-done.22), channel_id=1, source_target_pairs={{0,1},{1,0},{2,3},{3,2},{4,5},{5,4},{6,7},{7,6},{8,9},{9,8},{10,11... | collective-permute-start | bytes 1572872 | tf_op jit(solution)/shard_map/ppermute | solution.py:488
  83.4 38.3 %collective-permute-start.23 = (bf16[1408,512]{1,0:T(8,128)(2,1)S(1)}, bf16[1408,512]{1,0:T(8,128)(2,1)S(1)}, u32[]{:S(2)}, u32[]{:S(2)}) collective-permute-start(bf16[1408,512]{1,0:T(8,128)(2,1)S(1)} %copy-done.38), channel_id=1, source_target_pairs={{0,16},{16,0},{1,17},{17,1},{2,18},{18,2},{3,19},{19,3},{4,20},{20... | collective-permute-start | bytes 4325384 | tf_op jit(solution)/shard_map/ppermute | solution.py:488
  85.2 63.3 %collective-permute-start.18 = (bf16[512,512]{1,0:T(8,128)(2,1)S(1)}, bf16[512,512]{1,0:T(8,128)(2,1)S(1)}, u32[]{:S(2)}, u32[]{:S(2)}) collective-permute-start(bf16[512,512]{1,0:T(8,128)(2,1)S(1)} %copy-done.22), channel_id=1, source_target_pairs={{0,16},{16,0},{1,17},{17,1},{2,18},{18,2},{3,19},{19,3},{4,20},{20... | collective-permute-start | bytes 1572872 | tf_op jit(solution)/shard_map/ppermute | solution.py:488
  92.7 61.3 %collective-permute-start.19 = (bf16[512,512]{1,0:T(8,128)(2,1)S(1)}, bf16[512,512]{1,0:T(8,128)(2,1)S(1)}, u32[]{:S(2)}, u32[]{:S(2)}) collective-permute-start(bf16[512,512]{1,0:T(8,128)(2,1)S(1)} %collective-permute-done.17), channel_id=1, source_target_pairs={{0,16},{16,0},{1,17},{17,1},{2,18},{18,2},{3,19},{19,3},{4,20},{20... | collective-permute-start | bytes 1572872 | tf_op jit(solution)/shard_map/ppermute | solution.py:488
  93.9 25.0 %collective-permute-start.13 = (bf16[512,1024]{1,0:T(8,128)(2,1)S(1)}, bf16[512,1024]{1,0:T(8,128)(2,1)S(1)}, u32[]{:S(2)}, u32[]{:S(2)}) collective-permute-start(bf16[512,1024]{1,0:T(8,128)(2,1)S(1)} %collective-permute-done.12.refs_3_.refs_4_.refs_5_), channel_id=1, source_target_pairs={{0,2},{2,0},{4,6},{6,4},{8,10},{10,8},{12,14},{14,12},{1,3},{3,1},... | collective-permute-start | bytes 3145736 | tf_op jit(solution)/shard_map/ppermute | solution.py:488
  95.1 26.2 %collective-permute-start.14 = (bf16[512,1024]{1,0:T(8,128)(2,1)S(1)}, bf16[512,1024]{1,0:T(8,128)(2,1)S(1)}, u32[]{:S(2)}, u32[]{:S(2)}) collective-permute-start(bf16[512,1024]{1,0:T(8,128)(2,1)S(1)} %collective-permute-done.12.refs_3_.refs_4_.refs_5_), channel_id=1, source_target_pairs={{0,4},{2,6},{4,8},{6,10},{8,12},{10,14},{1,5},{3,7},{5,9},{7,11},{... | collective-permute-start | bytes 3145736 | tf_op jit(solution)/shard_map/ppermute | solution.py:573
  121.3 24.4 %collective-permute-start.15 = (bf16[512,1024]{1,0:T(8,128)(2,1)S(1)}, bf16[512,1024]{1,0:T(8,128)(2,1)S(1)}, u32[]{:S(2)}, u32[]{:S(2)}) collective-permute-start(bf16[512,1024]{1,0:T(8,128)(2,1)S(1)} %collective-permute-done.14.refs_3_.refs_4_.refs_7_), channel_id=1, source_target_pairs={{0,2},{2,0},{4,6},{6,4},{8,10},{10,8},{12,14},{14,12},{1,3},{3,1},... | collective-permute-start | bytes 3145736 | tf_op jit(solution)/shard_map/ppermute | solution.py:488
  173.8 244.9 %reduce-scatter.2.cloned.1.call-start = ((), (), s32[]{:S(2)}) async-start(), calls=%async_computation.2 | async-start | bytes 5455872 | tf_op jit(solution)/shard_map/reduce_scatter | solution.py:793
  245.7 24.5 %collective-permute-start.31 = (bf16[560,512]{1,0:T(8,128)(2,1)}, bf16[560,512]{1,0:T(8,128)(2,1)S(1)}, u32[]{:S(2)}, u32[]{:S(2)}) collective-permute-start(bf16[560,512]{1,0:T(8,128)(2,1)} %get-tuple-element.129.grad_ref.refs_0_), channel_id=1, source_target_pairs={{0,2},{2,0},{4,6},{6,4},{8,10},{10,8},{12,14},{14,12},{1,3},{3,1},... | collective-permute-start | bytes 1720328 | tf_op jit(solution)/shard_map/ppermute | solution.py:488
  274.3 261.0 %all-gather.5.cloned.1.call-start = ((), (), s32[]{:S(2)}) async-start(), calls=%async_computation.3 | async-start | bytes 5455872 | tf_op jit(solution)/shard_map/all_gather | solution.py:802
  274.4 21.2 %collective-permute-start.36 = (bf16[560,512]{1,0:T(8,128)(2,1)}, bf16[560,512]{1,0:T(8,128)(2,1)S(1)}, u32[]{:S(2)}, u32[]{:S(2)}) collective-permute-start(bf16[560,512]{1,0:T(8,128)(2,1)} %collective-permute-done.32.refs_3_), channel_id=1, source_target_pairs={{0,2},{2,0},{4,6},{6,4},{8,10},{10,8},{12,14},{14,12},{1,3},{3,1},... | collective-permute-start | bytes 1720328 | tf_op jit(solution)/shard_map/ppermute | solution.py:488
  276.2 35.5 %collective-permute-start.37 = (bf16[560,512]{1,0:T(8,128)(2,1)}, bf16[560,512]{1,0:T(8,128)(2,1)}, u32[]{:S(2)}, u32[]{:S(2)}) collective-permute-start(bf16[560,512]{1,0:T(8,128)(2,1)} %collective-permute-done.32.refs_3_), channel_id=1, source_target_pairs={{4,0},{6,2},{8,4},{10,6},{12,8},{14,10},{5,1},{7,3},{9,5},{11,7},{... | collective-permute-start | bytes 1720328 | tf_op jit(solution)/shard_map/ppermute | solution.py:573
  314.0 29.9 %collective-permute-start.39 = (bf16[560,512]{1,0:T(8,128)(2,1)}, bf16[560,512]{1,0:T(8,128)(2,1)}, u32[]{:S(2)}, u32[]{:S(2)}) collective-permute-start(bf16[560,512]{1,0:T(8,128)(2,1)} %collective-permute-done.37.refs_5_), channel_id=1, source_target_pairs={{4,0},{6,2},{8,4},{10,6},{12,8},{14,10},{5,1},{7,3},{9,5},{11,7},{... | collective-permute-start | bytes 1720328 | tf_op jit(solution)/shard_map/ppermute | solution.py:573
  346.1 78.5 %collective-permute-start.41 = (bf16[256,512]{1,0:T(8,128)(2,1)S(1)}, bf16[256,512]{1,0:T(8,128)(2,1)}, u32[]{:S(2)}, u32[]{:S(2)}) collective-permute-start(bf16[256,512]{1,0:T(8,128)(2,1)S(1)} %constant_dynamic-slice_fusion.9), channel_id=1, source_target_pairs={{0,8},{2,10},{4,12},{6,14},{8,0},{10,2},{12,4},{14,6},{1,9},{3,11}... | collective-permute-start | bytes 786440 | tf_op jit(solution)/shard_map/ppermute | solution.py:488
  466.2 25.1 %collective-permute-start.57 = (bf16[64,512]{1,0:T(8,128)(2,1)S(1)}, bf16[64,512]{1,0:T(8,128)(2,1)S(1)}, u32[]{:S(2)}, u32[]{:S(2)}) collective-permute-start(bf16[64,512]{1,0:T(8,128)(2,1)S(1)} %constant_dynamic-slice_fusion.2), channel_id=1, source_target_pairs={{0,4},{2,6},{4,0},{6,2},{8,12},{10,14},{12,8},{14,10},{1,5},{3,7},... | collective-permute-start | bytes 196616 | tf_op jit(solution)/shard_map/ppermute | solution.py:488
  501.9 22.5 %collective-permute-start.67 = (bf16[128,512]{1,0:T(8,128)(2,1)S(1)}, bf16[128,512]{1,0:T(8,128)(2,1)S(1)}, u32[]{:S(2)}, u32[]{:S(2)}) collective-permute-start(bf16[128,512]{1,0:T(8,128)(2,1)S(1)} %pad_maximum_fusion.16), channel_id=1, source_target_pairs={{0,8},{2,10},{4,12},{6,14},{8,0},{10,2},{12,4},{14,6},{1,9},{3,11}... | collective-permute-start | bytes 393224 | tf_op jit(solution)/shard_map/ppermute | solution.py:488
  504.6 26.8 %collective-permute-start.60 = (bf16[256,512]{1,0:T(8,128)(2,1)S(1)}, bf16[256,512]{1,0:T(8,128)(2,1)S(1)}, u32[]{:S(2)}, u32[]{:S(2)}) collective-permute-start(bf16[256,512]{1,0:T(8,128)(2,1)S(1)} %pad_maximum_fusion.11), channel_id=1, source_target_pairs={{0,8},{2,10},{4,12},{6,14},{8,0},{10,2},{12,4},{14,6},{1,9},{3,11}... | collective-permute-start | bytes 786440 | tf_op jit(solution)/shard_map/ppermute | solution.py:488
  (132 other events, 1910.8 us)
Sparse Core Ops, SparseCore 0:
  173.9 76.7 all-gather.2
  274.4 118.3 reduce-scatter.1
  425.7 102.5 all-gather.4

commit v4 on v3

--- a/solution.py
+++ b/solution.py
@@ -15,6 +15,8 @@
 BF16 = jnp.bfloat16
 BOUNDARY = 256
 STAT_ROWS = 3
+
+CTX = ("line", "side")
 
 epsilon = 1e-06
 
@@ -210,7 +212,7 @@
 
 
 def query_kernel(
-    sizes, step_keys, place_ref, q_ref, grad_ref, stat_ref, qmark_ref, kmark_ref, *refs
+    sizes, step_keys, first_pair, place_ref, q_ref, grad_ref, stat_ref, qmark_ref, kmark_ref, *refs
 ):
     count = len(sizes)
     pieces, out_ref, kv_ref, kt_ref, sems = refs[:count], *refs[count:]
@@ -223,16 +225,29 @@
         ((index + 1) * rows + BOUNDARY + step_keys - 1) // step_keys, length // step_keys
     )
 
-    def copy(at):
+    def copies(at):
         start = pl.multiple_of(place_ref[at] * rows, rows)
-        return pltpu.make_async_copy(
-            pieces[at], kv_ref.at[pl.ds(start, sizes[at]), :], sems.at[at]
-        )
+        whole = pieces[at].shape[1] // 2
+        return [
+            pltpu.make_async_copy(
+                pieces[at].at[:, pl.ds(part * whole + first_pair * PAIR, width)],
+                kv_ref.at[pl.ds(start, sizes[at]), pl.ds(part * width, width)],
+                sems.at[2 * at + part],
+            )
+            for part in range(2)
+        ]
+
+    def each(act):
+        for at in range(count):
+
+            @pl.when(place_ref[at] >= 0)
+            def _(at=at):
+                for one in copies(at):
+                    act(one)
 
     @pl.when(pair == 0)
     def _():
-        for at in range(count):
-            pl.when(place_ref[at] >= 0)(lambda at=at: copy(at).start())
+        each(lambda one: one.start())
 
         def clear(at, _):
             start = pl.multiple_of(at * BOUNDARY, BOUNDARY)
@@ -241,16 +256,14 @@
 
         ratio = rows // BOUNDARY
         lax.fori_loop((index + 1) * ratio + 1, end * (step_keys // BOUNDARY), clear, 0)
-        for at in range(count):
-            pl.when(place_ref[at] >= 0)(lambda at=at: copy(at).wait())
+        each(lambda one: one.wait())
 
     queries, grads = split_heads(q_ref[...]), split_heads(grad_ref[...])
     k_columns = pl.ds(pl.multiple_of(pair * PAIR, PAIR), PAIR)
     v_columns = pl.ds(pl.multiple_of(width + pair * PAIR, PAIR), PAIR)
-    lse = [stat_ref[pl.ds(2 * pair + h, 1), :] for h in range(2)]
-    delta = [
-        stat_ref[pl.ds(stat_ref.shape[0] // 2 + 2 * pair + h, 1), :] for h in range(2)
-    ]
+    head = 2 * (first_pair + pair)
+    lse = [stat_ref[pl.ds(head + h, 1), :] for h in range(2)]
+    delta = [stat_ref[pl.ds(stat_ref.shape[0] // 2 + head + h, 1), :] for h in range(2)]
 
     def turn(at, _):
         start = pl.multiple_of(at * step_keys, step_keys)
@@ -286,20 +299,21 @@
     out_ref[...] = (jnp.concatenate(state, axis=0).T * HEAD_DIM ** (-0.5)).astype(out_ref.dtype)
 
 
-def query_gradient(queries, sent, stat, pieces, qmark, kmark, step_keys=1024):
-    rows, width = queries.shape
+def query_gradient(
+    queries, sent, stat, pieces, qmark, kmark, first_pair, pairs, step_keys=1024
+):
+    rows, width = queries.shape[0], pairs * PAIR
     length = kmark.shape[0]
-    pairs = width // PAIR
     places = jnp.stack([jnp.asarray(place, jnp.int32) for _, place in pieces])
     sizes = [kv.shape[0] for kv, _ in pieces]
     return pl.pallas_call(
-        functools.partial(query_kernel, sizes, step_keys),
+        functools.partial(query_kernel, sizes, step_keys, first_pair),
         grid_spec=pltpu.PrefetchScalarGridSpec(
             num_scalar_prefetch=1,
             grid=(pairs,),
             in_specs=[
-                pl.BlockSpec((rows, PAIR), lambda h, s: (0, h)),
-                pl.BlockSpec((rows, PAIR), lambda h, s: (0, h)),
+                pl.BlockSpec((rows, PAIR), lambda h, s: (0, first_pair + h)),
+                pl.BlockSpec((rows, PAIR), lambda h, s: (0, first_pair + h)),
                 pl.BlockSpec(stat.shape, lambda h, s: (0, 0)),
                 pl.BlockSpec((1, rows), lambda h, s: (0, 0)),
                 pl.BlockSpec((length, 1), lambda h, s: (0, 0)),
@@ -309,7 +323,7 @@
             scratch_shapes=[
                 pltpu.VMEM((length, 2 * width), BF16),
                 pltpu.VMEM((PAIR, length), BF16),
-                pltpu.SemaphoreType.DMA((len(pieces),)),
+                pltpu.SemaphoreType.DMA((2 * len(pieces),)),
             ],
         ),
         out_shape=jax.ShapeDtypeStruct((rows, width), BF16),
@@ -323,7 +337,7 @@
 
 
 def key_kernel(
-    sizes, step_queries, place_ref, k_ref, v_ref, q_ref, qmark_ref, kmark_ref, *refs
+    sizes, step_queries, first_pair, place_ref, k_ref, v_ref, q_ref, qmark_ref, kmark_ref, *refs
 ):
     count = len(sizes)
     pieces = refs[:count]
@@ -340,7 +354,7 @@
         start = pl.multiple_of(place_ref[at] * rows + rows - size, BOUNDARY)
         return (
             pltpu.make_async_copy(
-                pieces[at].at[pl.ds(0, size), :],
+                pieces[at].at[pl.ds(0, size), pl.ds(first_pair * PAIR, width)],
                 grad_ref.at[pl.ds(start, size), :],
                 sems.at[2 * at],
             ),
@@ -383,6 +397,7 @@
 
     keys, values = split_heads(k_ref[...]), split_heads(v_ref[...])
     columns = pl.ds(pl.multiple_of(pair * PAIR, PAIR), PAIR)
+    head = 2 * (first_pair + pair)
 
     def step(masked):
         def body(at, state):
@@ -394,8 +409,8 @@
                 allowed = kmark_ref[...] <= qmark_ref[:, span]
             new = []
             for h in range(2):
-                lse = stat_ref[pl.ds(2 * pair + h, 1), span]
-                delta = stat_ref[pl.ds(stat_rows // 2 + 2 * pair + h, 1), span]
+                lse = stat_ref[pl.ds(head + h, 1), span]
+                delta = stat_ref[pl.ds(stat_rows // 2 + head + h, 1), span]
                 score = nt(keys[h], queries)
                 slope = nt(values[h], grads)
                 prob = jnp.exp2(score - lse)
@@ -420,23 +435,24 @@
     dv_ref[...] = (0.5 * jnp.where(lane < HEAD_DIM, state[1], state[3])).astype(dv_ref.dtype)
 
 
-def key_gradient(kv, q_all, pieces, qmark, kmark, step_queries=512):
+def key_gradient(kv, q_all, pieces, qmark, kmark, first_pair, pairs, step_queries=512):
     rows = kv.shape[0]
-    length, width = q_all.shape
-    pairs = width // PAIR
-    stat_rows = 2 * width // HEAD_DIM
+    length, whole = q_all.shape
+    width = pairs * PAIR
+    stat_rows = 2 * whole // HEAD_DIM
+    values_at = whole // PAIR + first_pair
     packed = STAT_ROWS * stat_rows
     places = jnp.stack([jnp.asarray(place, jnp.int32) for _, place in pieces])
     sizes = [sent.shape[0] - packed for sent, _ in pieces]
     return pl.pallas_call(
-        functools.partial(key_kernel, sizes, step_queries),
+        functools.partial(key_kernel, sizes, step_queries, first_pair),
         grid_spec=pltpu.PrefetchScalarGridSpec(
             num_scalar_prefetch=1,
             grid=(pairs,),
             in_specs=[
-                pl.BlockSpec((rows, PAIR), lambda h, s: (0, h)),
-                pl.BlockSpec((rows, PAIR), lambda h, s: (0, pairs + h)),
-                pl.BlockSpec((length, PAIR), lambda h, s: (0, h)),
+                pl.BlockSpec((rows, PAIR), lambda h, s: (0, first_pair + h)),
+                pl.BlockSpec((rows, PAIR), lambda h, s: (0, values_at + h)),
+                pl.BlockSpec((length, PAIR), lambda h, s: (0, first_pair + h)),
                 pl.BlockSpec((1, length), lambda h, s: (0, 0)),
                 pl.BlockSpec((rows, 1), lambda h, s: (0, 0)),
             ]
@@ -477,15 +493,15 @@
 ):
     width = tokens.shape[2]
     own_rows = tokens.shape[1]
-    sizes = {axis: lax.axis_size(axis) for axis in ("shard", "ctx", "tp")}
-    shard, ctx, tp = (lax.axis_index(axis) for axis in ("shard", "ctx", "tp"))
+    sizes = {axis: lax.axis_size(axis) for axis in ("shard", CTX, "tp")}
+    shard, ctx, tp = (lax.axis_index(axis) for axis in ("shard", CTX, "tp"))
     group_rows = own_rows * sizes["tp"]
     half = w_query.shape[1]
     part = w_query.shape[0]
-    line = sizes["ctx"] // 2
+    line = sizes[CTX] // 2
 
     def flip(values, axis, bit=1):
-        return lax.ppermute(values, axis, [(i, i ^ bit) for i in range(sizes[axis])])
+        return lax.ppermute(values, axis, [(i, i ^ bit) for i in range(lax.axis_size(axis))])
 
     def tree_sum(values):
         for axis, size in sizes.items():
@@ -501,14 +517,47 @@
             [jnp.where(first, mine, other), jnp.where(first, other, mine)], axis=axis
         )
 
-    def shard_gather(values, axis):
+    def shard_blocks(values):
         if sizes["shard"] == 2:
-            return in_order(shard, values, flip(values, "shard"), axis)
-        return lax.all_gather(values, "shard", axis=axis, tiled=True)
+            return [values, flip(values, "shard")]
+        gathered = lax.all_gather(values, "shard", axis=0, tiled=False)
+        return [gathered[i] for i in range(sizes["shard"])]
+
+    def block_of(values, at):
+        if sizes["shard"] == 2:
+            return cols_of(values, shard if at == 0 else 1 - shard, part)
+        return values[:, at * part : (at + 1) * part]
+
+    def join_blocks(terms):
+        if sizes["shard"] == 2:
+            return in_order(shard, terms[0], terms[1], 1)
+        return jnp.concatenate(terms, axis=1)
+
+    def times_blocks(lefts, blocks_of):
+        return join_blocks(
+            [
+                sum(nn(left, blocks[at]) for left, blocks in zip(lefts, blocks_of))
+                for at in range(sizes["shard"])
+            ]
+        )
+
+    def times_turned(left, blocks):
+        return sum(nt(block_of(left, at), block) for at, block in enumerate(blocks))
+
+    def times_rows(left, blocks):
+        return sum(nn(block_of(left, at), block) for at, block in enumerate(blocks))
+
+    def times_rows_turned(lefts, blocks_of):
+        return join_blocks(
+            [
+                sum(nt(left, blocks[at]) for left, blocks in zip(lefts, blocks_of))
+                for at in range(sizes["shard"])
+            ]
+        )
 
     def ctx_bits():
         bit = 1
-        while bit < sizes["ctx"]:
+        while bit < sizes[CTX]:
             yield bit
             bit *= 2
 
@@ -520,13 +569,14 @@
                 side = (ctx // order[step]) % 2
                 kept = lax.dynamic_slice_in_dim(parts[at], side * size, size, 0)
                 sent = lax.dynamic_slice_in_dim(parts[at], (1 - side) * size, size, 0)
-                got = flip(sent, "ctx", order[step])
+                got = flip(sent, CTX, order[step])
                 parts[at] = (kept.astype(F32) + got.astype(F32)).astype(BF16)
             parts = between(step, parts)
         for step in reversed(range(steps)):
             for at, order in enumerate(orders):
                 side = (ctx // order[step]) % 2
-                parts[at] = in_order(side, parts[at], flip(parts[at], "ctx", order[step]), 0)
+                parts[at] = in_order(side, parts[at], flip(parts[at], CTX, order[step]), 0)
+            parts = between(2 * steps - 1 - step, parts)
         return parts
 
     def rows_of(values, position):
@@ -539,7 +589,7 @@
 
     def spread(own, step, edge, between):
         if line != 4:
-            gathered = lax.all_gather(own, "ctx", axis=0, tiled=False)
+            gathered = lax.all_gather(own, CTX, axis=0, tiled=False)
             below = [(place < ctx) if step == 1 else (place > ctx) for place in range(2 * line)]
             pieces = [
                 (gathered[place], jnp.where(below[place], place, -1)) for place in range(2 * line)
@@ -553,28 +603,32 @@
                 (first,) = between(i // 2, [pieces[i][0]])
                 stages.append([(first, pieces[i][1]), pieces[i + 1]])
             return stages, rows
-        along = [(i, i + 2 * step) for i in range(2 * line) if 0 <= i + 2 * step < 2 * line]
-        across = flip(own, "ctx")
+        inside = range(2 * line)
+        along = [(i, i + 2 * step) for i in inside if i + 2 * step in inside]
         near = 1 if step == 1 else 0
-        diagonal = [
-            (i + step, i) for i in range(2 * line) if i % 2 == near and 0 <= i + step < 2 * line
-        ]
-        beside = lax.ppermute(own[edge], "ctx", diagonal)
-        moving = lax.ppermute(own, "ctx", along)
-        across, moving, beside = between(0, [across, moving, beside])
-        rows = jnp.where(column == near, beside, across[edge])
-        stages = [[(across, jnp.where(column == near, ctx - step, -1))]]
-        for hop in range(1, line):
+        against = [(i, i - 2 * step) for i in inside if i % 2 == near and i - 2 * step in inside]
+
+        def place(hop, aside):
             there = level - step * hop
-            exists = (there >= 0) & (there < line)
-            stages[-1].append((moving, jnp.where(exists, 2 * there + column, -1)))
-            across = flip(moving, "ctx")
-            if hop + 1 < line:
-                moving = lax.ppermute(moving, "ctx", along)
-                across, moving = between(hop, [across, moving])
-            else:
-                (across,) = between(hop, [across])
-            stages.append([(across, jnp.where(exists, 2 * there + 1 - column, -1))])
+            at = 2 * there + ((1 - column) if aside else column)
+            return jnp.where((there >= 0) & (there < line), at, -1)
+
+        across, moving = between(0, [flip(own, CTX), lax.ppermute(own, CTX, along)])
+        stages = [[(across, jnp.where(column == near, ctx - step, -1)), (moving, place(1, False))]]
+        beside = lax.ppermute(across[edge], CTX, against)
+        beside_here = across[edge]
+        across, moving, beside = between(
+            1, [flip(moving, CTX), lax.ppermute(moving, CTX, along), beside]
+        )
+        rows = jnp.where(column == near, beside, beside_here)
+        stages.append([(across, place(1, True)), (moving, place(2, False))])
+        across, moving = between(2, [flip(moving, CTX), lax.ppermute(moving, CTX, along)])
+        stages.append([(across, place(2, True)), (moving, place(3, False))])
+        cut = own.shape[0] // 32 * 16
+        last = between(
+            3, [flip(moving[:cut], CTX), lax.ppermute(across[cut:], CTX, along)]
+        )
+        stages.append([(jnp.concatenate(last, axis=0), place(3, True))])
         return stages, rows
 
     def shard_reduce(term, slice_rows):
@@ -605,53 +659,27 @@
 
     theirs = flip(mine, "tp")
     first_theirs = flip(cols_of(first_own, 1 - tp, half), "tp")
-    weight_qkv = shard_gather(jnp.concatenate([w_query, w_key, w_value], axis=1), 0)
+    weight_qkv = shard_blocks(jnp.concatenate([w_query, w_key, w_value], axis=1))
     count = tree_sum(jnp.broadcast_to(jnp.sum(keep), (1, 128)))[0, 0]
 
     group = in_order(tp, mine, theirs, 0).astype(F32)
     normed_one = rms_norm(group, gain_attn).astype(BF16)
     first_group = in_order(tp, cols_of(first_own, tp, half), first_theirs, 0).astype(F32)
-    qkv = nn(normed_one, weight_qkv)
+    qkv = times_rows(normed_one, weight_qkv)
     queries = (qkv[:, :half] * QUERY_SCALE).astype(BF16)
     kv = jnp.concatenate(
         [qkv[:, half : 2 * half], 0.5 * qkv[:, 2 * half :] + 0.5 * first_group], axis=1
     ).astype(BF16)
 
-    def gather_blocks(values):
-        if sizes["shard"] == 2:
-            both = [values, flip(values, "tp")]
-            return [[one, flip(one, "shard")] for one in both]
-        both = [values, flip(values, "tp")]
-        gathered = [lax.all_gather(one, "shard", axis=0, tiled=False) for one in both]
-        return [[one[i] for i in range(sizes["shard"])] for one in gathered]
-
-    def block_of(values, at):
-        if sizes["shard"] == 2:
-            return cols_of(values, shard if at == 0 else 1 - shard, part)
-        return values[:, at * part : (at + 1) * part]
-
-    def join_blocks(terms):
-        if sizes["shard"] == 2:
-            return in_order(shard, terms[0], terms[1], 1)
-        return jnp.concatenate(terms, axis=1)
-
-    def times_blocks(lefts, blocks_of):
-        return join_blocks(
-            [
-                sum(nn(left, blocks[at]) for left, blocks in zip(lefts, blocks_of))
-                for at in range(sizes["shard"])
-            ]
-        )
-
-    def times_turned(left, blocks):
-        return sum(nt(block_of(left, at), block) for at, block in enumerate(blocks))
-
     kv, w_gate, w_up, w_down, w_out, count = lax.optimization_barrier(
         (kv, w_gate, w_up, w_down, w_out, count)
     )
-    outs = gather_blocks(w_out)
-    gate_weight, up_weight = shard_gather(w_gate, 0), shard_gather(w_up, 0)
-    down_weight = shard_gather(w_down, 1)
+    gathered = {
+        "gate": shard_blocks(w_gate),
+        "up": shard_blocks(w_up),
+        "down": shard_blocks(w_down),
+        "outs": [shard_blocks(w_out), shard_blocks(flip(w_out, "tp"))],
+    }
 
     qmark, kmark = query_marks.reshape(1, -1), key_marks.reshape(-1, 1)
     forward = {"state": None, "pieces": [(kv, 0, query_marks.reshape(-1, 1))]}
@@ -666,16 +694,21 @@
         advance(False)
         *arrays, out = lax.optimization_barrier((*arrays, forward["state"][2]))
         forward["state"] = (*forward["state"][:2], out)
-        if sizes["ctx"] == 8:
-            there = level - at
-            if at == 0:
-                rows = jnp.where(column == 1, arrays[2], arrays[0][:BOUNDARY])
-                forward["pieces"] = [(rows, 0, next_marks.reshape(-1, 1))]
-                forward["pieces"].append((arrays[0], jnp.where(column == 1, 0, -1), None))
-            else:
-                forward["pieces"].append((arrays[0], jnp.where(there >= 0, 0, -1), None))
-            if len(arrays) > 1:
-                forward["pieces"].append((arrays[1], jnp.where(there >= 1, 0, -1), None))
+        if line != 4:
+            return arrays
+        here = (column == 1) if at == 0 else (level >= at)
+        if at == 3:
+            forward["pieces"] = [(jnp.concatenate(arrays, axis=0), jnp.where(here, 0, -1), None)]
+            return arrays
+        forward["pieces"] = [
+            (arrays[0], jnp.where(here, 0, -1), None),
+            (arrays[1], jnp.where(level > at, 0, -1), None),
+        ]
+        if at == 0:
+            forward["beside"] = arrays[0][:BOUNDARY]
+        if at == 1:
+            rows = jnp.where(column == 1, arrays[2], forward["beside"])
+            forward["pieces"].insert(0, (rows, 0, next_marks.reshape(-1, 1)))
         return arrays
 
     if line == 4:
@@ -690,8 +723,11 @@
         advance(True)
     attended, lse = forward["state"]
 
-    attended, q_sent = lax.optimization_barrier((attended, queries))
-    q_all = lax.all_gather(q_sent, "ctx", axis=0, tiled=True)
+    outs, gate_weight = gathered["outs"], gathered["gate"]
+    up_weight, down_weight = gathered["up"], gathered["down"]
+    attended, q_own = lax.optimization_barrier((attended, queries))
+    q_pair = in_order(column, q_own, flip(q_own, "side"), 0)
+    q_all = lax.all_gather(q_pair, "line", axis=0, tiled=True)
     att = [rows_of(attended, tp), flip(rows_of(attended, 1 - tp), "tp")]
     inputs = mine.astype(F32)
     hidden = inputs + times_blocks(att, outs)
@@ -700,26 +736,27 @@
     gate, up, logistic, act = [], [], [], []
 
     def widen(rows):
-        gate.append(nn(rows, gate_weight))
-        up.append(nn(rows, up_weight))
+        gate.append(times_rows(rows, gate_weight))
+        up.append(times_rows(rows, up_weight))
         logistic.append(jax.nn.sigmoid(gate[-1]))
         act.append((gate[-1] * logistic[-1] * up[-1]).astype(BF16))
 
     widen(normed[0])
     normed[1], act[0] = lax.optimization_barrier((normed[1], act[0]))
     widen(normed[1])
-    down_theirs = flip(nn(act[1], down_weight).astype(BF16), "tp")
-    final = hidden + (nn(act[0], down_weight) + down_theirs.astype(F32))
+    down_theirs = flip(times_blocks([act[1]], [down_weight]).astype(BF16), "tp")
+    down_theirs, q_pair = lax.optimization_barrier((down_theirs, q_pair))
+    final = hidden + (times_blocks([act[0]], [down_weight]) + down_theirs.astype(F32))
     difference = final - teacher.reshape(own_rows, width).astype(F32)
     local_error = jnp.sum(jnp.mean(difference * difference, axis=1) * keep)
-    token_total = group_rows * sizes["ctx"] * sizes["shard"]
+    token_total = group_rows * sizes[CTX] * sizes["shard"]
     grad_final = token_total / count * keep[:, None] * difference
     grad_round = grad_final.astype(BF16)
     rounds = [grad_round, flip(grad_round, "tp")]
     grad_gate, grad_up = [], []
 
     def back(at):
-        grad_act = nt(rounds[at], down_weight)
+        grad_act = times_turned(rounds[at], down_weight)
         part = grad_act * logistic[at]
         grad_gate.append((part * up[at] * (1.0 + gate[at] * (1.0 - logistic[at]))).astype(BF16))
         grad_up.append((part * gate[at]).astype(BF16))
@@ -729,15 +766,17 @@
         (rounds[1], grad_gate[0], grad_up[0])
     )
     back(1)
-    two_sent = (nt(grad_gate[1], gate_weight) + nt(grad_up[1], up_weight)).astype(BF16)
+    both_weights = [gate_weight, up_weight]
+    two_sent = times_rows_turned([grad_gate[1], grad_up[1]], both_weights).astype(BF16)
     two_theirs = flip(two_sent, "tp")
     gate_part = over_rows(normed, grad_gate, True)
     up_part = over_rows(normed, grad_up, True)
     down_part = over_rows(rounds, act, True)
-    two_own = nt(grad_gate[0], gate_weight) + nt(grad_up[0], up_weight)
+    two_own = times_rows_turned([grad_gate[0], grad_up[0]], both_weights)
     two_theirs, two_own, gate_part, up_part, down_part = lax.optimization_barrier(
         (two_theirs, two_own, gate_part, up_part, down_part)
     )
+    ffn_part = jnp.concatenate([gate_part, up_part, down_part], axis=1)
     grad_two = two_own + two_theirs.astype(F32)
     hidden_part, gain_ffn_term = jax.vjp(rms_norm, hidden, gain_ffn)[1](grad_two)
     grad_hidden = grad_final + hidden_part
@@ -754,80 +793,86 @@
     kv_pieces += [piece for stage in stages for piece in stage]
     parts = {}
 
+    pairs = half // PAIR
+    quarters = max(pairs // 4, 1)
+
+    def query_part(at):
+        first = at * quarters
+        count = quarters if at < 3 else pairs - first
+        return query_gradient(
+            queries, sent, parts["stat"], kv_pieces, qmark, kmark, first, count
+        )
+
     def grad_between(at, arrays):
         if at == 0:
-            *arrays, hidden_held = lax.optimization_barrier((*arrays[:-1], arrays[-1], hidden_two)) if len(arrays) < 3 else (
-                *arrays[:2],
-                *lax.optimization_barrier((arrays[2], hidden_two)),
-            )
-            parts["out"] = over_rows(
-                [hidden_round, hidden_held],
+            parts["stat"], parts["q_all"], parts["hidden_two"] = stat, q_all, hidden_two
+        if at > 3:
+            return arrays
+        name = "query" + str(at)
+        parts[name] = query_part(at)
+        hold = [name, "stat"]
+        if at == 0:
+            hold += ["q_all", "hidden_two"]
+        if at == 3:
+            parts["ffn"] = ffn_part
+            hold.append("ffn")
+        arrays, held = lax.optimization_barrier((arrays, [parts[name] for name in hold]))
+        parts.update(zip(hold, held))
+        return arrays
+
+    grad_stages, sent_before = spread(
+        sent, -1, slice(group_rows - BOUNDARY, None), grad_between
+    )
+    scattered = lax.psum_scatter(parts["ffn"], CTX, scatter_dimension=0, tiled=True)
+    query_grad = jnp.concatenate([parts["query" + str(at)] for at in range(4)], axis=1)
+    grad_pieces = [(sent, ctx), (sent_before, ctx - 1)]
+    grad_pieces += [piece for stage in grad_stages for piece in stage]
+    marks = (key_marks.reshape(1, -1), query_marks.reshape(-1, 1))
+    key_grad, value_half = key_gradient(kv, parts["q_all"], grad_pieces, *marks, 0, pairs)
+    key_grad, normed_held, parts["hidden_two"] = lax.optimization_barrier(
+        (key_grad, normed_one, parts["hidden_two"])
+    )
+    early_part = jnp.concatenate(
+        [
+            over_rows([normed_held], [query_grad], True),
+            over_rows(
+                [hidden_round, parts["hidden_two"]],
                 [rows_of(attended, tp), rows_of(attended, 1 - tp)],
                 True,
-            )
-            parts["all"] = jnp.concatenate(
-                [gate_part, up_part, down_part, parts["out"]], axis=1
-            )
-            hold = ["all"]
-        elif at == 1:
-            held_stat, parts["q_all"], parts["all"] = lax.optimization_barrier(
-                (stat, q_all, parts["all"])
-            )
-            parts["query_grad"] = query_gradient(
-                queries, sent, held_stat, kv_pieces, qmark, kmark
-            )
-            hold = ["query_grad"]
-        elif at == 2:
-            parts["query"] = over_rows([normed_one], [parts["query_grad"]], True)
-            hold = ["query"]
-        else:
-            return arrays
-        held = lax.optimization_barrier((*arrays, *[parts[name] for name in hold]))
-        parts.update(zip(hold, held[len(arrays) :]))
-        return list(held[: len(arrays)])
-
-    grad_stages, sent_before = spread(
-        sent, -1, slice(group_rows - BOUNDARY, None), grad_between
-    )
-    query_grad = parts["query_grad"]
-    scattered = lax.psum_scatter(parts["all"], "ctx", scatter_dimension=0, tiled=True)
-    grad_pieces = [(sent, ctx), (sent_before, ctx - 1)]
-    grad_pieces += [piece for stage in grad_stages for piece in stage]
-    key_grad, value_half = key_gradient(
-        kv, parts["q_all"], grad_pieces, key_marks.reshape(1, -1), query_marks.reshape(-1, 1)
-    )
-    scattered, key_grad, value_half = lax.optimization_barrier(
-        (scattered, key_grad, value_half)
-    )
-    weight_grads = lax.all_gather(scattered, "ctx", axis=0, tiled=True).astype(F32)
+            ),
+        ],
+        axis=1,
+    )
+    grads = jnp.concatenate([query_grad, key_grad, value_half], axis=1)
+    kv_part = over_rows([normed_one], [grads[:, half:]], True)
+    last = {}
     hidden_half = w_gate.shape[1]
-    w_gate_grad, w_up_grad, w_down_grad, w_out_grad = jnp.split(
-        weight_grads, [hidden_half, 2 * hidden_half, 3 * hidden_half], axis=1
-    )
-    grads = jnp.concatenate([query_grad, key_grad, value_half], axis=1)
-    key_part = over_rows([normed_one], [key_grad], True)
-    value_part = over_rows([normed_one], [value_half], True)
-    last = {}
 
     def finish(step, parts):
         if step == 0:
-            *parts, held = lax.optimization_barrier((*parts, grads))
-            theirs = flip(nt(rows_of(held, 1 - tp), weight_qkv).astype(BF16), "tp")
-            last["own"] = nt(rows_of(held, tp), weight_qkv)
+            parts, held, ready = lax.optimization_barrier((parts, grads, scattered))
+            last["spread"] = lax.all_gather(ready, CTX, axis=0, tiled=True)
+            theirs = times_rows_turned([rows_of(held, 1 - tp)], [weight_qkv]).astype(BF16)
+            theirs = flip(theirs, "tp")
+            last["own"] = times_rows_turned([rows_of(held, tp)], [weight_qkv])
             last["theirs"] = theirs
             last["value"] = flip(rows_of(held[:, 2 * half :], 1 - tp), "tp")
         if step == 1:
             *parts, last["own"], last["theirs"], last["value"] = lax.optimization_barrier(
                 (*parts, last["own"], last["theirs"], last["value"])
             )
+        if step == len(bits) + 1:
+            parts, spread_out = lax.optimization_barrier((parts, last["spread"]))
+            last["grads"] = [
+                spread_out[:, at * hidden_half : (at + 1) * hidden_half].astype(F32)
+                for at in range(3)
+            ]
         return parts
 
     bits = list(ctx_bits())
-    w_query_grad, w_key_grad, w_value_grad = reduce_ctx(
-        [parts["query"], key_part, value_part],
-        [bits[2:] + bits[:2], bits, bits[1:] + bits[:1]],
-        finish,
-    )
+    early, late = reduce_ctx([early_part, kv_part], [bits, bits[1:] + bits[:1]], finish)
+    early, late = early.astype(F32), late.astype(F32)
+    w_gate_grad, w_up_grad, w_down_grad = last["grads"]
     grad_one = last["own"] + last["theirs"].astype(F32)
     input_part, gain_attn_term = jax.vjp(rms_norm, inputs, gain_attn)[1](grad_one)
     tokens_grad = grad_hidden + input_part
@@ -844,10 +889,10 @@
         first_grad.reshape(1, own_rows, width),
         small[:width],
         small[width : 2 * width],
-        w_query_grad.astype(F32),
-        w_key_grad.astype(F32),
-        w_value_grad.astype(F32),
-        w_out_grad.T,
+        early[:, :half],
+        late[:, :half],
+        late[:, half:],
+        early[:, half:].T,
         w_gate_grad,
         w_up_grad,
         w_down_grad.T,
@@ -855,16 +900,18 @@
 
 
 def solution(mesh):
-    rows = P("shard", ("ctx", "tp"), None)
+    places = dict(mesh.shape)
+    devices = mesh.devices.reshape(places["shard"], places["ctx"] // 2, 2, places["tp"])
+    rows = P("shard", (*CTX, "tp"), None)
     wide, tall = P("shard", "tp"), P("tp", "shard")
     return jax.shard_map(
         on_device,
-        mesh=mesh,
+        mesh=jax.sharding.Mesh(devices, ("shard", *CTX, "tp")),
         in_specs=(
             rows,
             rows,
             rows,
-            P("shard", ("ctx", "tp")),
+            P("shard", (*CTX, "tp")),
             P("shard", None),
             P(),
             P(),

time: 565 us -> 546 us (0.966)
  waiting for transfers between devices: 260 us -> 190 us
  matrix products: 49.4 us -> 83.9 us
  Pallas kernels: 83.7 us -> 97.2 us
    ppermute x69 -> x65, waiting for transfers between devices: 260 us -> 172 us  [the longest x55 149 us: flip(): lax.ppermute(values, axis, [(i, i ^ bit) for i in range(lax.axis_size(axi...]
    dot_general x45 -> x58, matrix products: 49.4 us -> 83.9 us  [dot(): lax.dot_general(left, right, (((left_dim,), (right_dim,)), ((), ())), pre...]
    reduce_scatter x1, waiting for transfers between devices: 0.02 us -> 18.4 us  [on_device(): lax.psum_scatter(parts['ffn'], CTX, scatter_dimension=0, tiled=True)]
    pallas_call x2 -> x5, Pallas kernels: 67.4 us -> 79.7 us  [the longest x1 52.7 us: key_gradient(): pl.pallas_call(functools.partial(key_kernel, sizes, step_queries, first_p...]
    unnamed x172 -> x156, local copies, waits for them, and re-layouts: 11.4 us -> 16.3 us
    ppermute x69 -> x65, starting transfers between devices: 88.6 us -> 89.1 us  [the longest x55 58.6 us: flip(): lax.ppermute(values, axis, [(i, i ^ bit) for i in range(lax.axis_size(axi...]
  transfers between devices with their start and end apart: 72 -> 68, of which waited for: 40 -> 37; matrix products, arithmetic and copies ran while one was open for 14% -> 23% of each run, Pallas kernels for 15% -> 18%
where the time goes in v4:
time: 546 us; the launch traced here: 536 us
  waiting for transfers between devices  190 us (35%)
  Pallas kernels  97.2 us (18%)
  starting transfers between devices  89.6 us (16%)
  matrix products  83.9 us (15%)
  other arithmetic  29.2 us (5%)
  local copies, waits for them, and re-layouts  28.3 us (5%)
  between operations  17.8 us (3%)
    ppermute x55, waiting for transfers between devices, flip(): lax.ppermute(values, axis, [(i, i ^ bit) for i in range(lax.axis_size(axi...  149 us
    dot_general x58, matrix products, dot(): lax.dot_general(left, right, (((left_dim,), (right_dim,)), ((), ())), pre...  83.9 us
    ppermute x55, starting transfers between devices, flip(): lax.ppermute(values, axis, [(i, i ^ bit) for i in range(lax.axis_size(axi...  58.6 us
    pallas_call x1, Pallas kernels, key_gradient(): pl.pallas_call(functools.partial(key_kernel, sizes, step_queries, first_p...  52.7 us
    pallas_call x4, Pallas kernels, query_gradient(): pl.pallas_call(functools.partial(query_kernel, sizes, step_keys, first_pa...  27 us
    reduce_scatter x1, waiting for transfers between devices, on_device(): lax.psum_scatter(parts['ffn'], CTX, scatter_dimension=0, tiled=True)  18.4 us
    unnamed x156, local copies, waits for them, and re-layouts  16.3 us
    pallas_call x5, Pallas kernels, forward_stage(): pl.pallas_call(functools.partial(forward_kernel, [m is not None for _, _,...  15.1 us
  transfers between devices with their start and end apart: 68, of which 37 were waited for; matrix products, arithmetic and copies ran while one was open for 23% of the time, Pallas kernels for 18%

profile of v4, /device:TPU:0, one launch (start us, length us, event | category | flops | bytes accessed | tf_op | source)
XLA Modules:
  0.0 536.5 jit_solution(14262806609777255316)
XLA Ops:
  39.1 4.4 collective-permute-start.9
  49.2 9.9 %collective-permute-done.8.refs_1_.refs_2_ = bf16[512,1024]{1,0:T(8,128)(2,1)S(1)} collective-permute-done((bf16[512,1024]{1,0:T(8,128)(2,1)S(1)}, bf16[512,1024]{1,0:T(8,128)(2,1)S(1)}, u32[]{:S(2)}, u32[]{:S(2)}) %collective-permute-start.8) | collective-permute-done | bytes 1048608 | tf_op jit(solution)/shard_map/ppermute | solution.py:504
  61.8 5.5 %collective-permute-start.11 = (bf16[512,1024]{1,0:T(8,128)(2,1)}, bf16[512,1024]{1,0:T(8,128)(2,1)}, u32[]{:S(2)}, u32[]{:S(2)}) collective-permute-start(bf16[512,1024]{1,0:T(8,128)(2,1)} %collective-permute-done.9.refs_3_.refs_4_), channel_id=1, source_target_pairs={{0,4},{2,6},{4,8},{6,10},{8,12},{10,14},{1,5},{3,7},{5,9},{7,11},{... | collective-permute-start | bytes 3145736 | tf_op jit(solution)/shard_map/ppermute | solution.py:621
  74.3 8.3 %collective-permute-done.10.refs_4_.refs_5_ = bf16[512,1024]{1,0:T(8,128)(2,1)S(1)} collective-permute-done((bf16[512,1024]{1,0:T(8,128)(2,1)}, bf16[512,1024]{1,0:T(8,128)(2,1)S(1)}, u32[]{:S(2)}, u32[]{:S(2)}) %collective-permute-start.10) | collective-permute-done | bytes 1048608 | tf_op jit(solution)/shard_map/ppermute | solution.py:504
  86.5 4.4 collective-permute-start.14
  96.3 4.9 shard_map.239
  108.2 4.5 collective-permute-start.16
  159.8 6.1 %collective-permute-done.25 = bf16[256,1024]{1,0:T(8,128)(2,1)S(1)} collective-permute-done((bf16[256,1024]{1,0:T(8,128)(2,1)S(1)}, bf16[256,1024]{1,0:T(8,128)(2,1)S(1)}, u32[]{:S(2)}, u32[]{:S(2)}) %collective-permute-start.25) | collective-permute-done | bytes 524320 | tf_op jit(solution)/shard_map/ppermute | solution.py:504
  216.0 5.0 collective-permute-done.32.other_ref
  229.9 6.5 %shard_map.243 = bf16[512,128]{1,0:T(8,128)(2,1)} custom-call(s32[9]{0:T(128)} %stack.146.place_ref, bf16[512,512]{1,0:T(8,128)(2,1)} %copy-done.5, bf16[560,512]{1,0:T(8,128)(2,1)} %get-tuple-element.140.grad_ref.refs_0_, f32[16,512]{1,0:T(8,128)} %get-tuple-element.152.stat_ref, s32[1,512]{1,0:T(1,128)} %copy-done.13, s32[4096,1]{1,0:T(8,128)} %copy.34.kmark_ref, ...), custom_call_target="tpu_custom_call" | custom-call | flops 268435456 | bytes 2097152 | tf_op jit(solution)/shard_map/pallas_call | solution.py:309
  239.8 6.5 %collective-permute-done.34.refs_3_ = bf16[560,512]{1,0:T(8,128)(2,1)S(1)} collective-permute-done((bf16[560,512]{1,0:T(8,128)(2,1)}, bf16[560,512]{1,0:T(8,128)(2,1)S(1)}, u32[]{:S(2)}, u32[]{:S(2)}) %collective-permute-start.34) | collective-permute-done | bytes 573472 | tf_op jit(solution)/shard_map/ppermute | solution.py:616
  249.3 5.0 collective-permute-start.38
  254.3 6.9 %shard_map.244 = bf16[512,128]{1,0:T(8,128)(2,1)} custom-call(s32[9]{0:T(128)} %stack.146.place_ref, bf16[512,512]{1,0:T(8,128)(2,1)} %copy-done.5, bf16[560,512]{1,0:T(8,128)(2,1)} %get-tuple-element.140.grad_ref.refs_0_, f32[16,512]{1,0:T(8,128)} %get-tuple-element.152.stat_ref, s32[1,512]{1,0:T(1,128)} %copy-done.13, s32[4096,1]{1,0:T(8,128)} %copy.34.kmark_ref, ...), custom_call_target="tpu_custom_call" | custom-call | flops 268435456 | bytes 2097152 | tf_op jit(solution)/shard_map/pallas_call | solution.py:309
  265.8 7.0 %shard_map.245 = bf16[512,128]{1,0:T(8,128)(2,1)} custom-call(s32[9]{0:T(128)} %stack.146.place_ref, bf16[512,512]{1,0:T(8,128)(2,1)} %copy-done.5, bf16[560,512]{1,0:T(8,128)(2,1)} %get-tuple-element.140.grad_ref.refs_0_, f32[16,512]{1,0:T(8,128)} %get-tuple-element.152.stat_ref, s32[1,512]{1,0:T(1,128)} %copy-done.13, s32[4096,1]{1,0:T(8,128)} %copy.34.kmark_ref, ...), custom_call_target="tpu_custom_call" | custom-call | flops 268435456 | bytes 2097152 | tf_op jit(solution)/shard_map/pallas_call | solution.py:309
  277.3 5.0 collective-permute-done.40.refs_7_
  288.2 6.5 %shard_map.246 = bf16[512,128]{1,0:T(8,128)(2,1)} custom-call(s32[9]{0:T(128)} %stack.146.place_ref, bf16[512,512]{1,0:T(8,128)(2,1)} %copy-done.5, bf16[560,512]{1,0:T(8,128)(2,1)} %get-tuple-element.140.grad_ref.refs_0_, f32[16,512]{1,0:T(8,128)} %get-tuple-element.152.stat_ref, s32[1,512]{1,0:T(1,128)} %copy-done.13, s32[4096,1]{1,0:T(8,128)} %copy.34.kmark_ref, ...), custom_call_target="tpu_custom_call" | custom-call | flops 268435456 | bytes 2097152 | tf_op jit(solution)/shard_map/pallas_call | solution.py:309
  298.3 52.7 %shard_map.247 = (bf16[512,512]{1,0:T(8,128)(2,1)}, bf16[512,512]{1,0:T(8,128)(2,1)}) custom-call(s32[9]{0:T(128)} %stack.137.place_ref, bf16[512,1024]{1,0:T(8,128)(2,1)} %copy-done, bf16[512,1024]{1,0:T(8,128)(2,1)} %copy-done, bf16[4096,512]{1,0:T(8,128)(2,1)} %all-gather.3.cloned.1.call-done.q_ref, s32[1,4096]{1,0:T(1,128)} %qmark_ref.1, ...), custom_call_target="tpu_custom_call" | custom-call | flops 1073741824 | bytes 8388608 | tf_op jit(solution)/shard_map/pallas_call | solution.py:447
  366.7 8.7 %collective-permute-done.45 = bf16[256,1024]{0,1:T(8,128)(2,1)} collective-permute-done((bf16[256,1024]{0,1:T(8,128)(2,1)S(1)}, bf16[256,1024]{0,1:T(8,128)(2,1)}, u32[]{:S(2)}, u32[]{:S(2)}) %collective-permute-start.45) | collective-permute-done | bytes 524320 | tf_op jit(solution)/shard_map/ppermute | solution.py:504
  382.1 18.4 %reduce-scatter.2.cloned.1.call-done = bf16[64,4224]{1,0:T(8,128)(2,1)} async-done(((bf16[512,4224]{1,0:T(8,128)(2,1)}), bf16[64,4224]{1,0:T(8,128)(2,1)}) %reduce-scatter.2.cloned.1.call-update) | async-done | bytes 540688 | tf_op jit(solution)/shard_map/reduce_scatter | solution.py:826
  419.7 8.8 %collective-permute-done.51 = bf16[256,512]{1,0:T(8,128)(2,1)S(1)} collective-permute-done((bf16[256,512]{1,0:T(8,128)(2,1)S(1)}, bf16[256,512]{1,0:T(8,128)(2,1)S(1)}, u32[]{:S(2)}, u32[]{:S(2)}) %collective-permute-start.51) | collective-permute-done | bytes 262176 | tf_op jit(solution)/shard_map/ppermute | solution.py:504
  441.7 25.0 %collective-permute-done.55 = f32[1,2176]{1,0:T(1,128)S(1)} collective-permute-done((f32[1,2176]{1,0:T(1,128)S(1)}, f32[1,2176]{1,0:T(1,128)S(1)}, u32[]{:S(2)}, u32[]{:S(2)}) %collective-permute-start.55) | collective-permute-done | bytes 8736 | tf_op jit(solution)/shard_map/ppermute | solution.py:504
  474.2 20.9 %collective-permute-done.58 = bf16[64,1024]{0,1:T(8,128)(2,1)S(1)} collective-permute-done((bf16[64,1024]{0,1:T(8,128)(2,1)S(1)}, bf16[64,1024]{0,1:T(8,128)(2,1)S(1)}, u32[]{:S(2)}, u32[]{:S(2)}) %collective-permute-start.58) | collective-permute-done | bytes 131104 | tf_op jit(solution)/shard_map/ppermute | solution.py:504
  497.9 9.4 %collective-permute-done.59 = bf16[128,1024]{0,1:T(8,128)(2,1)S(1)} collective-permute-done((bf16[128,1024]{0,1:T(8,128)(2,1)S(1)}, bf16[128,1024]{0,1:T(8,128)(2,1)S(1)}, u32[]{:S(2)}, u32[]{:S(2)}) %collective-permute-start.59) | collective-permute-done | bytes 262176 | tf_op jit(solution)/shard_map/ppermute | solution.py:504
  510.9 5.3 convert_bitcast_fusion
  (442 shorter events, 273.0 us)
Async XLA Ops:
  7.2 239.1 %all-gather.3.cloned.1.call-start = ((), (), s32[]{:S(2)}) async-start(), calls=%async_computation.1 | async-start | bytes 5242880 | tf_op jit(solution)/shard_map/all_gather | solution.py:730
  7.2 24.9 %collective-permute-start = (bf16[256,1024]{1,0:T(8,128)(2,1)}, bf16[256,1024]{1,0:T(8,128)(2,1)S(1)}, u32[]{:S(2)}, u32[]{:S(2)}) collective-permute-start(bf16[256,1024]{1,0:T(8,128)(2,1)} %bitcast.142), channel_id=1, source_target_pairs={{0,1},{1,0},{2,3},{3,2},{4,5},{5,4},{6,7},{7,6},{8,9},{9,8},{10,11... | collective-permute-start | bytes 1572872 | tf_op jit(solution)/shard_map/ppermute | solution.py:504
  12.0 20.0 %collective-permute-start.2 = (bf16[256,512]{1,0:T(8,128)(2,1)}, bf16[256,512]{1,0:T(8,128)(2,1)S(1)}, u32[]{:S(2)}, u32[]{:S(2)}) collective-permute-start(bf16[256,512]{1,0:T(8,128)(2,1)} %dynamic-slice_bitcast_fusion), channel_id=1, source_target_pairs={{0,1},{1,0},{2,3},{3,2},{4,5},{5,4},{6,7},{7,6},{8,9},{9,8},{10,11... | collective-permute-start | bytes 786440 | tf_op jit(solution)/shard_map/ppermute | solution.py:504
  37.2 21.8 %collective-permute-start.8 = (bf16[512,1024]{1,0:T(8,128)(2,1)S(1)}, bf16[512,1024]{1,0:T(8,128)(2,1)S(1)}, u32[]{:S(2)}, u32[]{:S(2)}) collective-permute-start(bf16[512,1024]{1,0:T(8,128)(2,1)S(1)} %pad_maximum_fusion.2.refs_1_.refs_2_.refs_0_.k_ref.v_ref), channel_id=1, source_target_pairs={{0,2},{2,0},{4,6},{6,4},{8,10},{10,8},{12,14},{14,12},{1,3},{3,1},... | collective-permute-start | bytes 3145736 | tf_op jit(solution)/shard_map/ppermute | solution.py:504
  39.1 22.2 %collective-permute-start.9 = (bf16[512,1024]{1,0:T(8,128)(2,1)S(1)}, bf16[512,1024]{1,0:T(8,128)(2,1)}, u32[]{:S(2)}, u32[]{:S(2)}) collective-permute-start(bf16[512,1024]{1,0:T(8,128)(2,1)S(1)} %pad_maximum_fusion.2.refs_1_.refs_2_.refs_0_.k_ref.v_ref), channel_id=1, source_target_pairs={{0,4},{2,6},{4,8},{6,10},{8,12},{10,14},{1,5},{3,7},{5,9},{7,11},{... | collective-permute-start | bytes 3145736 | tf_op jit(solution)/shard_map/ppermute | solution.py:616
  61.3 21.3 %collective-permute-start.10 = (bf16[512,1024]{1,0:T(8,128)(2,1)}, bf16[512,1024]{1,0:T(8,128)(2,1)S(1)}, u32[]{:S(2)}, u32[]{:S(2)}) collective-permute-start(bf16[512,1024]{1,0:T(8,128)(2,1)} %collective-permute-done.9.refs_3_.refs_4_), channel_id=1, source_target_pairs={{0,2},{2,0},{4,6},{6,4},{8,10},{10,8},{12,14},{14,12},{1,3},{3,1},... | collective-permute-start | bytes 3145736 | tf_op jit(solution)/shard_map/ppermute | solution.py:504
  61.8 22.3 %collective-permute-start.11 = (bf16[512,1024]{1,0:T(8,128)(2,1)}, bf16[512,1024]{1,0:T(8,128)(2,1)}, u32[]{:S(2)}, u32[]{:S(2)}) collective-permute-start(bf16[512,1024]{1,0:T(8,128)(2,1)} %collective-permute-done.9.refs_3_.refs_4_), channel_id=1, source_target_pairs={{0,4},{2,6},{4,8},{6,10},{8,12},{10,14},{1,5},{3,7},{5,9},{7,11},{... | collective-permute-start | bytes 3145736 | tf_op jit(solution)/shard_map/ppermute | solution.py:621
  84.1 20.4 %collective-permute-start.13 = (bf16[512,1024]{1,0:T(8,128)(2,1)}, bf16[512,1024]{1,0:T(8,128)(2,1)S(1)}, u32[]{:S(2)}, u32[]{:S(2)}) collective-permute-start(bf16[512,1024]{1,0:T(8,128)(2,1)} %collective-permute-done.11.refs_6_.refs_7_.refs_5_), channel_id=1, source_target_pairs={{0,2},{2,0},{4,6},{6,4},{8,10},{10,8},{12,14},{14,12},{1,3},{3,1},... | collective-permute-start | bytes 3145736 | tf_op jit(solution)/shard_map/ppermute | solution.py:504
  86.5 20.2 %collective-permute-start.14 = (bf16[512,1024]{1,0:T(8,128)(2,1)}, bf16[512,1024]{1,0:T(8,128)(2,1)S(1)}, u32[]{:S(2)}, u32[]{:S(2)}) collective-permute-start(bf16[512,1024]{1,0:T(8,128)(2,1)} %collective-permute-done.11.refs_6_.refs_7_.refs_5_), channel_id=1, source_target_pairs={{0,4},{2,6},{4,8},{6,10},{8,12},{10,14},{1,5},{3,7},{5,9},{7,11},{... | collective-permute-start | bytes 3145736 | tf_op jit(solution)/shard_map/ppermute | solution.py:625
  91.3 23.1 %collective-permute-start.18 = (bf16[512,512]{1,0:T(8,128)(2,1)}, bf16[512,512]{1,0:T(8,128)(2,1)}, u32[]{:S(2)}, u32[]{:S(2)}) collective-permute-start(bf16[512,512]{1,0:T(8,128)(2,1)} %param.24), channel_id=1, source_target_pairs={{0,1},{1,0},{2,3},{3,2},{4,5},{5,4},{6,7},{7,6},{8,9},{9,8},{10,11... | collective-permute-start | bytes 1572872 | tf_op jit(solution)/shard_map/ppermute | solution.py:504
  92.8 29.6 %collective-permute-start.19 = (bf16[512,512]{1,0:T(8,128)(2,1)}, bf16[512,512]{1,0:T(8,128)(2,1)}, u32[]{:S(2)}, u32[]{:S(2)}) collective-permute-start(bf16[512,512]{1,0:T(8,128)(2,1)} %param.24), channel_id=1, source_target_pairs={{0,16},{16,0},{1,17},{17,1},{2,18},{18,2},{3,19},{19,3},{4,20},{20... | collective-permute-start | bytes 1572872 | tf_op jit(solution)/shard_map/ppermute | solution.py:504
  92.9 42.0 %collective-permute-start.22 = (bf16[512,1408]{1,0:T(8,128)(2,1)}, bf16[512,1408]{1,0:T(8,128)(2,1)}, u32[]{:S(2)}, u32[]{:S(2)}) collective-permute-start(bf16[512,1408]{1,0:T(8,128)(2,1)} %param.25), channel_id=1, source_target_pairs={{0,16},{16,0},{1,17},{17,1},{2,18},{18,2},{3,19},{19,3},{4,20},{20... | collective-permute-start | bytes 4325384 | tf_op jit(solution)/shard_map/ppermute | solution.py:504
  114.4 24.2 %collective-permute-start.23 = (bf16[512,1408]{1,0:T(8,128)(2,1)S(1)}, bf16[512,1408]{1,0:T(8,128)(2,1)S(1)}, u32[]{:S(2)}, u32[]{:S(2)}) collective-permute-start(bf16[512,1408]{1,0:T(8,128)(2,1)S(1)} %copy-done.20), channel_id=1, source_target_pairs={{0,16},{16,0},{1,17},{17,1},{2,18},{18,2},{3,19},{19,3},{4,20},{20... | collective-permute-start | bytes 4325384 | tf_op jit(solution)/shard_map/ppermute | solution.py:504
  122.4 29.6 %collective-permute-start.24 = (bf16[1408,512]{1,0:T(8,128)(2,1)}, bf16[1408,512]{1,0:T(8,128)(2,1)}, u32[]{:S(2)}, u32[]{:S(2)}) collective-permute-start(bf16[1408,512]{1,0:T(8,128)(2,1)} %param.27), channel_id=1, source_target_pairs={{0,16},{16,0},{1,17},{17,1},{2,18},{18,2},{3,19},{19,3},{4,20},{20... | collective-permute-start | bytes 4325384 | tf_op jit(solution)/shard_map/ppermute | solution.py:504
  142.7 257.8 %reduce-scatter.2.cloned.1.call-start = ((), (), s32[]{:S(2)}) async-start(), calls=%async_computation.2 | async-start | bytes 4866048 | tf_op jit(solution)/shard_map/reduce_scatter | solution.py:826
  188.1 20.3 %collective-permute-start.28 = (bf16[256,1024]{1,0:T(8,128)(2,1)S(1)}, bf16[256,1024]{1,0:T(8,128)(2,1)S(1)}, u32[]{:S(2)}, u32[]{:S(2)}) collective-permute-start(bf16[256,1024]{1,0:T(8,128)(2,1)S(1)} %pad_maximum_fusion.8), channel_id=1, source_target_pairs={{0,1},{1,0},{2,3},{3,2},{4,5},{5,4},{6,7},{7,6},{8,9},{9,8},{10,11... | collective-permute-start | bytes 1572872 | tf_op jit(solution)/shard_map/ppermute | solution.py:504
  225.1 21.2 %collective-permute-start.34 = (bf16[560,512]{1,0:T(8,128)(2,1)}, bf16[560,512]{1,0:T(8,128)(2,1)S(1)}, u32[]{:S(2)}, u32[]{:S(2)}) collective-permute-start(bf16[560,512]{1,0:T(8,128)(2,1)} %get-tuple-element.140.grad_ref.refs_0_), channel_id=1, source_target_pairs={{4,0},{6,2},{8,4},{10,6},{12,8},{14,10},{5,1},{7,3},{9,5},{11,7},{... | collective-permute-start | bytes 1720328 | tf_op jit(solution)/shard_map/ppermute | solution.py:616
  295.5 214.1 %all-gather.5.cloned.1.call-start = ((), (), s32[]{:S(2)}) async-start(), calls=%async_computation.3 | async-start | bytes 4866048 | tf_op jit(solution)/shard_map/all_gather | solution.py:854
  409.6 18.9 %collective-permute-start.50 = (bf16[256,1024]{1,0:T(8,128)(2,1)S(1)}, bf16[256,1024]{1,0:T(8,128)(2,1)S(1)}, u32[]{:S(2)}, u32[]{:S(2)}) collective-permute-start(bf16[256,1024]{1,0:T(8,128)(2,1)S(1)} %pad_maximum_fusion.9), channel_id=1, source_target_pairs={{0,1},{1,0},{2,3},{3,2},{4,5},{5,4},{6,7},{7,6},{8,9},{9,8},{10,11... | collective-permute-start | bytes 1572872 | tf_op jit(solution)/shard_map/ppermute | solution.py:504
  436.4 35.9 %collective-permute-start.57 = (bf16[64,1024]{0,1:T(8,128)(2,1)S(1)}, bf16[64,1024]{0,1:T(8,128)(2,1)S(1)}, u32[]{:S(2)}, u32[]{:S(2)}) collective-permute-start(bf16[64,1024]{0,1:T(8,128)(2,1)S(1)} %constant_dynamic-slice_fusion.1), channel_id=1, source_target_pairs={{0,8},{2,10},{4,12},{6,14},{8,0},{10,2},{12,4},{14,6},{1,9},{3,11}... | collective-permute-start | bytes 393224 | tf_op jit(solution)/shard_map/ppermute | solution.py:504
  438.5 28.2 %collective-permute-start.55 = (f32[1,2176]{1,0:T(1,128)S(1)}, f32[1,2176]{1,0:T(1,128)S(1)}, u32[]{:S(2)}, u32[]{:S(2)}) collective-permute-start(f32[1,2176]{1,0:T(1,128)S(1)} %add.473), channel_id=1, source_target_pairs={{0,8},{2,10},{4,12},{6,14},{8,0},{10,2},{12,4},{14,6},{1,9},{3,11}... | collective-permute-start | bytes 26120 | tf_op jit(solution)/shard_map/ppermute | solution.py:504
  440.3 32.2 %collective-permute-start.60 = (bf16[64,1024]{1,0:T(8,128)(2,1)S(1)}, bf16[64,1024]{1,0:T(8,128)(2,1)S(1)}, u32[]{:S(2)}, u32[]{:S(2)}) collective-permute-start(bf16[64,1024]{1,0:T(8,128)(2,1)S(1)} %constant_dynamic-slice_fusion), channel_id=1, source_target_pairs={{0,2},{2,0},{4,6},{6,4},{8,10},{10,8},{12,14},{14,12},{1,3},{3,1},... | collective-permute-start | bytes 393224 | tf_op jit(solution)/shard_map/ppermute | solution.py:504
  472.5 22.6 %collective-permute-start.58 = (bf16[64,1024]{0,1:T(8,128)(2,1)S(1)}, bf16[64,1024]{0,1:T(8,128)(2,1)S(1)}, u32[]{:S(2)}, u32[]{:S(2)}) collective-permute-start(bf16[64,1024]{0,1:T(8,128)(2,1)S(1)} %add_convert_fusion.4), channel_id=1, source_target_pairs={{0,8},{2,10},{4,12},{6,14},{8,0},{10,2},{12,4},{14,6},{1,9},{3,11}... | collective-permute-start | bytes 393224 | tf_op jit(solution)/shard_map/ppermute | solution.py:504
  472.6 22.7 %collective-permute-start.61 = (bf16[64,1024]{1,0:T(8,128)(2,1)S(1)}, bf16[64,1024]{1,0:T(8,128)(2,1)S(1)}, u32[]{:S(2)}, u32[]{:S(2)}) collective-permute-start(bf16[64,1024]{1,0:T(8,128)(2,1)S(1)} %add_convert_fusion.7), channel_id=1, source_target_pairs={{0,2},{2,0},{4,6},{6,4},{8,10},{10,8},{12,14},{14,12},{1,3},{3,1},... | collective-permute-start | bytes 393224 | tf_op jit(solution)/shard_map/ppermute | solution.py:504
  (117 other events, 1150.6 us)
Sparse Core Ops, SparseCore 0:
  142.8 87.8 all-gather.2
  295.2 105.2 reduce-scatter.1
  402.9 94.3 all-gather.4

commit v5 on v4

--- a/solution.py
+++ b/solution.py
@@ -15,6 +15,7 @@
 BF16 = jnp.bfloat16
 BOUNDARY = 256
 STAT_ROWS = 3
+KEY_STEP = 1024
 
 CTX = ("line", "side")
 
@@ -278,7 +279,8 @@
             keys = kv_ref[pl.ds(start, step_keys), k_columns]
             values = kv_ref[pl.ds(start, step_keys), v_columns]
             if masked:
-                allowed = kmark_ref[pl.ds(start, step_keys), :] <= qmark_ref[...]
+                window = pl.multiple_of((at - full) * step_keys, step_keys)
+                allowed = kmark_ref[pl.ds(window, step_keys), :] <= qmark_ref[...]
             new = []
             for h in range(2):
                 score = nt(keys, queries[h])
@@ -300,10 +302,9 @@
 
 
 def query_gradient(
-    queries, sent, stat, pieces, qmark, kmark, first_pair, pairs, step_keys=1024
+    queries, sent, stat, pieces, qmark, kmark, length, first_pair, pairs, step_keys=KEY_STEP
 ):
     rows, width = queries.shape[0], pairs * PAIR
-    length = kmark.shape[0]
     places = jnp.stack([jnp.asarray(place, jnp.int32) for _, place in pieces])
     sizes = [kv.shape[0] for kv, _ in pieces]
     return pl.pallas_call(
@@ -316,7 +317,7 @@
                 pl.BlockSpec((rows, PAIR), lambda h, s: (0, first_pair + h)),
                 pl.BlockSpec(stat.shape, lambda h, s: (0, 0)),
                 pl.BlockSpec((1, rows), lambda h, s: (0, 0)),
-                pl.BlockSpec((length, 1), lambda h, s: (0, 0)),
+                pl.BlockSpec((2 * step_keys, 1), lambda h, s: (0, 0)),
             ]
             + [pl.BlockSpec(memory_space=pl.ANY)] * len(pieces),
             out_specs=pl.BlockSpec((rows, PAIR), lambda h, s: (0, h)),
@@ -681,7 +682,13 @@
         "outs": [shard_blocks(w_out), shard_blocks(flip(w_out, "tp"))],
     }
 
-    qmark, kmark = query_marks.reshape(1, -1), key_marks.reshape(-1, 1)
+    qmark = query_marks.reshape(1, -1)
+    far_marks = jnp.concatenate(
+        [key_marks, jnp.full((2 * KEY_STEP,), 1 << 30, key_marks.dtype)]
+    )
+    kmark = lax.dynamic_slice_in_dim(
+        far_marks, ctx * group_rows // KEY_STEP * KEY_STEP, 2 * KEY_STEP, 0
+    ).reshape(-1, 1)
     forward = {"state": None, "pieces": [(kv, 0, query_marks.reshape(-1, 1))]}
 
     def advance(last):
@@ -800,7 +807,7 @@
         first = at * quarters
         count = quarters if at < 3 else pairs - first
         return query_gradient(
-            queries, sent, parts["stat"], kv_pieces, qmark, kmark, first, count
+            queries, sent, parts["stat"], kv_pieces, qmark, kmark, key_marks.shape[0], first, count
         )
 
     def grad_between(at, arrays):

time: 546 us -> 545 us (level)
  no operation moved by 1% of the time
where the time goes in v5:
time: 545 us; the launch traced here: 535 us
  waiting for transfers between devices  191 us (35%)
  Pallas kernels  95.7 us (18%)
  starting transfers between devices  89.3 us (16%)
  matrix products  84 us (15%)
  other arithmetic  29.2 us (5%)
  local copies, waits for them, and re-layouts  27.6 us (5%)
  between operations  17.8 us (3%)
    ppermute x55, waiting for transfers between devices, flip(): lax.ppermute(values, axis, [(i, i ^ bit) for i in range(lax.axis_size(axi...  151 us
    dot_general x58, matrix products, dot(): lax.dot_general(left, right, (((left_dim,), (right_dim,)), ((), ())), pre...  84 us
    ppermute x55, starting transfers between devices, flip(): lax.ppermute(values, axis, [(i, i ^ bit) for i in range(lax.axis_size(axi...  58.3 us
    pallas_call x1, Pallas kernels, key_gradient(): pl.pallas_call(functools.partial(key_kernel, sizes, step_queries, first_p...  52.7 us
    pallas_call x4, Pallas kernels, query_gradient(): pl.pallas_call(functools.partial(query_kernel, sizes, step_keys, first_pa...  25.5 us
    reduce_scatter x1, waiting for transfers between devices, on_device(): lax.psum_scatter(parts['ffn'], CTX, scatter_dimension=0, tiled=True)  18 us
    unnamed x156, local copies, waits for them, and re-layouts  16.3 us
    pallas_call x5, Pallas kernels, forward_stage(): pl.pallas_call(functools.partial(forward_kernel, [m is not None for _, _,...  15.1 us
  transfers between devices with their start and end apart: 68, of which 37 were waited for; matrix products, arithmetic and copies ran while one was open for 23% of the time, Pallas kernels for 18%

profile of v5, /device:TPU:0, one launch (start us, length us, event | category | flops | bytes accessed | tf_op | source)
XLA Modules:
  0.0 534.9 jit_solution(1968388807280343915)
XLA Ops:
  39.1 4.4 collective-permute-start.9
  49.1 9.9 %collective-permute-done.8.refs_1_.refs_2_ = bf16[512,1024]{1,0:T(8,128)(2,1)S(1)} collective-permute-done((bf16[512,1024]{1,0:T(8,128)(2,1)S(1)}, bf16[512,1024]{1,0:T(8,128)(2,1)S(1)}, u32[]{:S(2)}, u32[]{:S(2)}) %collective-permute-start.8) | collective-permute-done | bytes 1048608 | tf_op jit(solution)/shard_map/ppermute | solution.py:505
  61.8 5.5 %collective-permute-start.11 = (bf16[512,1024]{1,0:T(8,128)(2,1)}, bf16[512,1024]{1,0:T(8,128)(2,1)}, u32[]{:S(2)}, u32[]{:S(2)}) collective-permute-start(bf16[512,1024]{1,0:T(8,128)(2,1)} %collective-permute-done.9.refs_3_.refs_4_), channel_id=1, source_target_pairs={{0,4},{2,6},{4,8},{6,10},{8,12},{10,14},{1,5},{3,7},{5,9},{7,11},{... | collective-permute-start | bytes 3145736 | tf_op jit(solution)/shard_map/ppermute | solution.py:622
  74.2 8.3 %collective-permute-done.10.refs_4_.refs_5_ = bf16[512,1024]{1,0:T(8,128)(2,1)S(1)} collective-permute-done((bf16[512,1024]{1,0:T(8,128)(2,1)}, bf16[512,1024]{1,0:T(8,128)(2,1)S(1)}, u32[]{:S(2)}, u32[]{:S(2)}) %collective-permute-start.10) | collective-permute-done | bytes 1048608 | tf_op jit(solution)/shard_map/ppermute | solution.py:505
  86.5 4.4 collective-permute-start.14
  96.3 4.9 shard_map.239
  108.2 4.5 collective-permute-start.16
  159.9 6.1 %collective-permute-done.25 = bf16[256,1024]{1,0:T(8,128)(2,1)S(1)} collective-permute-done((bf16[256,1024]{1,0:T(8,128)(2,1)S(1)}, bf16[256,1024]{1,0:T(8,128)(2,1)S(1)}, u32[]{:S(2)}, u32[]{:S(2)}) %collective-permute-start.25) | collective-permute-done | bytes 524320 | tf_op jit(solution)/shard_map/ppermute | solution.py:505
  216.1 5.0 collective-permute-done.32.other_ref
  229.3 6.1 %shard_map.243 = bf16[512,128]{1,0:T(8,128)(2,1)} custom-call(s32[9]{0:T(128)} %stack.146.place_ref, bf16[512,512]{1,0:T(8,128)(2,1)} %copy-done.5, bf16[560,512]{1,0:T(8,128)(2,1)} %get-tuple-element.140.grad_ref.refs_0_, f32[16,512]{1,0:T(8,128)} %get-tuple-element.152.stat_ref, s32[1,512]{1,0:T(1,128)} %copy-done.13, s32[2048,1]{1,0:T(8,128)} %copy.34.kmark_ref, ...), custom_call_target="tpu_custom_call" | custom-call | flops 268435456 | bytes 2097152 | tf_op jit(solution)/shard_map/pallas_call | solution.py:310
  239.8 6.5 %collective-permute-done.34.refs_3_ = bf16[560,512]{1,0:T(8,128)(2,1)S(1)} collective-permute-done((bf16[560,512]{1,0:T(8,128)(2,1)}, bf16[560,512]{1,0:T(8,128)(2,1)S(1)}, u32[]{:S(2)}, u32[]{:S(2)}) %collective-permute-start.34) | collective-permute-done | bytes 573472 | tf_op jit(solution)/shard_map/ppermute | solution.py:617
  249.3 5.0 collective-permute-start.38
  254.3 6.5 %shard_map.244 = bf16[512,128]{1,0:T(8,128)(2,1)} custom-call(s32[9]{0:T(128)} %stack.146.place_ref, bf16[512,512]{1,0:T(8,128)(2,1)} %copy-done.5, bf16[560,512]{1,0:T(8,128)(2,1)} %get-tuple-element.140.grad_ref.refs_0_, f32[16,512]{1,0:T(8,128)} %get-tuple-element.152.stat_ref, s32[1,512]{1,0:T(1,128)} %copy-done.13, s32[2048,1]{1,0:T(8,128)} %copy.34.kmark_ref, ...), custom_call_target="tpu_custom_call" | custom-call | flops 268435456 | bytes 2097152 | tf_op jit(solution)/shard_map/pallas_call | solution.py:310
  265.9 6.7 %shard_map.245 = bf16[512,128]{1,0:T(8,128)(2,1)} custom-call(s32[9]{0:T(128)} %stack.146.place_ref, bf16[512,512]{1,0:T(8,128)(2,1)} %copy-done.5, bf16[560,512]{1,0:T(8,128)(2,1)} %get-tuple-element.140.grad_ref.refs_0_, f32[16,512]{1,0:T(8,128)} %get-tuple-element.152.stat_ref, s32[1,512]{1,0:T(1,128)} %copy-done.13, s32[2048,1]{1,0:T(8,128)} %copy.34.kmark_ref, ...), custom_call_target="tpu_custom_call" | custom-call | flops 268435456 | bytes 2097152 | tf_op jit(solution)/shard_map/pallas_call | solution.py:310
  272.5 4.8 collective-permute-done.39.refs_6_
  287.1 6.1 %shard_map.246 = bf16[512,128]{1,0:T(8,128)(2,1)} custom-call(s32[9]{0:T(128)} %stack.146.place_ref, bf16[512,512]{1,0:T(8,128)(2,1)} %copy-done.5, bf16[560,512]{1,0:T(8,128)(2,1)} %get-tuple-element.140.grad_ref.refs_0_, f32[16,512]{1,0:T(8,128)} %get-tuple-element.152.stat_ref, s32[1,512]{1,0:T(1,128)} %copy-done.13, s32[2048,1]{1,0:T(8,128)} %copy.34.kmark_ref, ...), custom_call_target="tpu_custom_call" | custom-call | flops 268435456 | bytes 2097152 | tf_op jit(solution)/shard_map/pallas_call | solution.py:310
  296.8 52.7 %shard_map.247 = (bf16[512,512]{1,0:T(8,128)(2,1)}, bf16[512,512]{1,0:T(8,128)(2,1)}) custom-call(s32[9]{0:T(128)} %stack.137.place_ref, bf16[512,1024]{1,0:T(8,128)(2,1)} %copy-done, bf16[512,1024]{1,0:T(8,128)(2,1)} %copy-done, bf16[4096,512]{1,0:T(8,128)(2,1)} %all-gather.3.cloned.1.call-done.q_ref, s32[1,4096]{1,0:T(1,128)} %qmark_ref.1, ...), custom_call_target="tpu_custom_call" | custom-call | flops 1073741824 | bytes 8388608 | tf_op jit(solution)/shard_map/pallas_call | solution.py:448
  365.2 8.7 %collective-permute-done.45 = bf16[256,1024]{0,1:T(8,128)(2,1)} collective-permute-done((bf16[256,1024]{0,1:T(8,128)(2,1)S(1)}, bf16[256,1024]{0,1:T(8,128)(2,1)}, u32[]{:S(2)}, u32[]{:S(2)}) %collective-permute-start.45) | collective-permute-done | bytes 524320 | tf_op jit(solution)/shard_map/ppermute | solution.py:505
  380.6 18.0 %reduce-scatter.2.cloned.1.call-done = bf16[64,4224]{1,0:T(8,128)(2,1)} async-done(((bf16[512,4224]{1,0:T(8,128)(2,1)}), bf16[64,4224]{1,0:T(8,128)(2,1)}) %reduce-scatter.2.cloned.1.call-update) | async-done | bytes 540688 | tf_op jit(solution)/shard_map/reduce_scatter | solution.py:833
  417.9 8.8 %collective-permute-done.51 = bf16[256,512]{1,0:T(8,128)(2,1)S(1)} collective-permute-done((bf16[256,512]{1,0:T(8,128)(2,1)S(1)}, bf16[256,512]{1,0:T(8,128)(2,1)S(1)}, u32[]{:S(2)}, u32[]{:S(2)}) %collective-permute-start.51) | collective-permute-done | bytes 262176 | tf_op jit(solution)/shard_map/ppermute | solution.py:505
  439.9 25.0 %collective-permute-done.55 = f32[1,2176]{1,0:T(1,128)S(1)} collective-permute-done((f32[1,2176]{1,0:T(1,128)S(1)}, f32[1,2176]{1,0:T(1,128)S(1)}, u32[]{:S(2)}, u32[]{:S(2)}) %collective-permute-start.55) | collective-permute-done | bytes 8736 | tf_op jit(solution)/shard_map/ppermute | solution.py:505
  472.4 20.8 %collective-permute-done.58 = bf16[64,1024]{0,1:T(8,128)(2,1)S(1)} collective-permute-done((bf16[64,1024]{0,1:T(8,128)(2,1)S(1)}, bf16[64,1024]{0,1:T(8,128)(2,1)S(1)}, u32[]{:S(2)}, u32[]{:S(2)}) %collective-permute-start.58) | collective-permute-done | bytes 131104 | tf_op jit(solution)/shard_map/ppermute | solution.py:505
  496.2 9.6 %collective-permute-done.59 = bf16[128,1024]{0,1:T(8,128)(2,1)S(1)} collective-permute-done((bf16[128,1024]{0,1:T(8,128)(2,1)S(1)}, bf16[128,1024]{0,1:T(8,128)(2,1)S(1)}, u32[]{:S(2)}, u32[]{:S(2)}) %collective-permute-start.59) | collective-permute-done | bytes 262176 | tf_op jit(solution)/shard_map/ppermute | solution.py:505
  508.9 5.3 convert_bitcast_fusion
  (443 shorter events, 273.3 us)
Async XLA Ops:
  7.2 239.1 %all-gather.3.cloned.1.call-start = ((), (), s32[]{:S(2)}) async-start(), calls=%async_computation.1 | async-start | bytes 5242880 | tf_op jit(solution)/shard_map/all_gather | solution.py:737
  7.2 24.9 %collective-permute-start = (bf16[256,1024]{1,0:T(8,128)(2,1)}, bf16[256,1024]{1,0:T(8,128)(2,1)S(1)}, u32[]{:S(2)}, u32[]{:S(2)}) collective-permute-start(bf16[256,1024]{1,0:T(8,128)(2,1)} %bitcast.142), channel_id=1, source_target_pairs={{0,1},{1,0},{2,3},{3,2},{4,5},{5,4},{6,7},{7,6},{8,9},{9,8},{10,11... | collective-permute-start | bytes 1572872 | tf_op jit(solution)/shard_map/ppermute | solution.py:505
  12.0 20.0 %collective-permute-start.2 = (bf16[256,512]{1,0:T(8,128)(2,1)}, bf16[256,512]{1,0:T(8,128)(2,1)S(1)}, u32[]{:S(2)}, u32[]{:S(2)}) collective-permute-start(bf16[256,512]{1,0:T(8,128)(2,1)} %dynamic-slice_bitcast_fusion), channel_id=1, source_target_pairs={{0,1},{1,0},{2,3},{3,2},{4,5},{5,4},{6,7},{7,6},{8,9},{9,8},{10,11... | collective-permute-start | bytes 786440 | tf_op jit(solution)/shard_map/ppermute | solution.py:505
  37.2 21.8 %collective-permute-start.8 = (bf16[512,1024]{1,0:T(8,128)(2,1)S(1)}, bf16[512,1024]{1,0:T(8,128)(2,1)S(1)}, u32[]{:S(2)}, u32[]{:S(2)}) collective-permute-start(bf16[512,1024]{1,0:T(8,128)(2,1)S(1)} %pad_maximum_fusion.2.refs_1_.refs_2_.refs_0_.k_ref.v_ref), channel_id=1, source_target_pairs={{0,2},{2,0},{4,6},{6,4},{8,10},{10,8},{12,14},{14,12},{1,3},{3,1},... | collective-permute-start | bytes 3145736 | tf_op jit(solution)/shard_map/ppermute | solution.py:505
  39.1 22.2 %collective-permute-start.9 = (bf16[512,1024]{1,0:T(8,128)(2,1)S(1)}, bf16[512,1024]{1,0:T(8,128)(2,1)}, u32[]{:S(2)}, u32[]{:S(2)}) collective-permute-start(bf16[512,1024]{1,0:T(8,128)(2,1)S(1)} %pad_maximum_fusion.2.refs_1_.refs_2_.refs_0_.k_ref.v_ref), channel_id=1, source_target_pairs={{0,4},{2,6},{4,8},{6,10},{8,12},{10,14},{1,5},{3,7},{5,9},{7,11},{... | collective-permute-start | bytes 3145736 | tf_op jit(solution)/shard_map/ppermute | solution.py:617
  61.3 21.3 %collective-permute-start.10 = (bf16[512,1024]{1,0:T(8,128)(2,1)}, bf16[512,1024]{1,0:T(8,128)(2,1)S(1)}, u32[]{:S(2)}, u32[]{:S(2)}) collective-permute-start(bf16[512,1024]{1,0:T(8,128)(2,1)} %collective-permute-done.9.refs_3_.refs_4_), channel_id=1, source_target_pairs={{0,2},{2,0},{4,6},{6,4},{8,10},{10,8},{12,14},{14,12},{1,3},{3,1},... | collective-permute-start | bytes 3145736 | tf_op jit(solution)/shard_map/ppermute | solution.py:505
  61.8 22.3 %collective-permute-start.11 = (bf16[512,1024]{1,0:T(8,128)(2,1)}, bf16[512,1024]{1,0:T(8,128)(2,1)}, u32[]{:S(2)}, u32[]{:S(2)}) collective-permute-start(bf16[512,1024]{1,0:T(8,128)(2,1)} %collective-permute-done.9.refs_3_.refs_4_), channel_id=1, source_target_pairs={{0,4},{2,6},{4,8},{6,10},{8,12},{10,14},{1,5},{3,7},{5,9},{7,11},{... | collective-permute-start | bytes 3145736 | tf_op jit(solution)/shard_map/ppermute | solution.py:622
  84.1 20.4 %collective-permute-start.13 = (bf16[512,1024]{1,0:T(8,128)(2,1)}, bf16[512,1024]{1,0:T(8,128)(2,1)S(1)}, u32[]{:S(2)}, u32[]{:S(2)}) collective-permute-start(bf16[512,1024]{1,0:T(8,128)(2,1)} %collective-permute-done.11.refs_6_.refs_7_.refs_5_), channel_id=1, source_target_pairs={{0,2},{2,0},{4,6},{6,4},{8,10},{10,8},{12,14},{14,12},{1,3},{3,1},... | collective-permute-start | bytes 3145736 | tf_op jit(solution)/shard_map/ppermute | solution.py:505
  86.5 20.2 %collective-permute-start.14 = (bf16[512,1024]{1,0:T(8,128)(2,1)}, bf16[512,1024]{1,0:T(8,128)(2,1)S(1)}, u32[]{:S(2)}, u32[]{:S(2)}) collective-permute-start(bf16[512,1024]{1,0:T(8,128)(2,1)} %collective-permute-done.11.refs_6_.refs_7_.refs_5_), channel_id=1, source_target_pairs={{0,4},{2,6},{4,8},{6,10},{8,12},{10,14},{1,5},{3,7},{5,9},{7,11},{... | collective-permute-start | bytes 3145736 | tf_op jit(solution)/shard_map/ppermute | solution.py:626
  91.3 23.1 %collective-permute-start.18 = (bf16[512,512]{1,0:T(8,128)(2,1)}, bf16[512,512]{1,0:T(8,128)(2,1)}, u32[]{:S(2)}, u32[]{:S(2)}) collective-permute-start(bf16[512,512]{1,0:T(8,128)(2,1)} %param.24), channel_id=1, source_target_pairs={{0,1},{1,0},{2,3},{3,2},{4,5},{5,4},{6,7},{7,6},{8,9},{9,8},{10,11... | collective-permute-start | bytes 1572872 | tf_op jit(solution)/shard_map/ppermute | solution.py:505
  92.8 29.6 %collective-permute-start.19 = (bf16[512,512]{1,0:T(8,128)(2,1)}, bf16[512,512]{1,0:T(8,128)(2,1)}, u32[]{:S(2)}, u32[]{:S(2)}) collective-permute-start(bf16[512,512]{1,0:T(8,128)(2,1)} %param.24), channel_id=1, source_target_pairs={{0,16},{16,0},{1,17},{17,1},{2,18},{18,2},{3,19},{19,3},{4,20},{20... | collective-permute-start | bytes 1572872 | tf_op jit(solution)/shard_map/ppermute | solution.py:505
  92.9 42.0 %collective-permute-start.22 = (bf16[512,1408]{1,0:T(8,128)(2,1)}, bf16[512,1408]{1,0:T(8,128)(2,1)}, u32[]{:S(2)}, u32[]{:S(2)}) collective-permute-start(bf16[512,1408]{1,0:T(8,128)(2,1)} %param.25), channel_id=1, source_target_pairs={{0,16},{16,0},{1,17},{17,1},{2,18},{18,2},{3,19},{19,3},{4,20},{20... | collective-permute-start | bytes 4325384 | tf_op jit(solution)/shard_map/ppermute | solution.py:505
  114.4 24.2 %collective-permute-start.23 = (bf16[512,1408]{1,0:T(8,128)(2,1)S(1)}, bf16[512,1408]{1,0:T(8,128)(2,1)S(1)}, u32[]{:S(2)}, u32[]{:S(2)}) collective-permute-start(bf16[512,1408]{1,0:T(8,128)(2,1)S(1)} %copy-done.20), channel_id=1, source_target_pairs={{0,16},{16,0},{1,17},{17,1},{2,18},{18,2},{3,19},{19,3},{4,20},{20... | collective-permute-start | bytes 4325384 | tf_op jit(solution)/shard_map/ppermute | solution.py:505
  122.4 29.7 %collective-permute-start.24 = (bf16[1408,512]{1,0:T(8,128)(2,1)}, bf16[1408,512]{1,0:T(8,128)(2,1)}, u32[]{:S(2)}, u32[]{:S(2)}) collective-permute-start(bf16[1408,512]{1,0:T(8,128)(2,1)} %param.27), channel_id=1, source_target_pairs={{0,16},{16,0},{1,17},{17,1},{2,18},{18,2},{3,19},{19,3},{4,20},{20... | collective-permute-start | bytes 4325384 | tf_op jit(solution)/shard_map/ppermute | solution.py:505
  142.7 256.0 %reduce-scatter.2.cloned.1.call-start = ((), (), s32[]{:S(2)}) async-start(), calls=%async_computation.2 | async-start | bytes 4866048 | tf_op jit(solution)/shard_map/reduce_scatter | solution.py:833
  188.1 20.3 %collective-permute-start.28 = (bf16[256,1024]{1,0:T(8,128)(2,1)S(1)}, bf16[256,1024]{1,0:T(8,128)(2,1)S(1)}, u32[]{:S(2)}, u32[]{:S(2)}) collective-permute-start(bf16[256,1024]{1,0:T(8,128)(2,1)S(1)} %pad_maximum_fusion.8), channel_id=1, source_target_pairs={{0,1},{1,0},{2,3},{3,2},{4,5},{5,4},{6,7},{7,6},{8,9},{9,8},{10,11... | collective-permute-start | bytes 1572872 | tf_op jit(solution)/shard_map/ppermute | solution.py:505
  225.1 21.2 %collective-permute-start.34 = (bf16[560,512]{1,0:T(8,128)(2,1)}, bf16[560,512]{1,0:T(8,128)(2,1)S(1)}, u32[]{:S(2)}, u32[]{:S(2)}) collective-permute-start(bf16[560,512]{1,0:T(8,128)(2,1)} %get-tuple-element.140.grad_ref.refs_0_), channel_id=1, source_target_pairs={{4,0},{6,2},{8,4},{10,6},{12,8},{14,10},{5,1},{7,3},{9,5},{11,7},{... | collective-permute-start | bytes 1720328 | tf_op jit(solution)/shard_map/ppermute | solution.py:617
  294.0 214.0 %all-gather.5.cloned.1.call-start = ((), (), s32[]{:S(2)}) async-start(), calls=%async_computation.3 | async-start | bytes 4866048 | tf_op jit(solution)/shard_map/all_gather | solution.py:861
  407.8 18.9 %collective-permute-start.50 = (bf16[256,1024]{1,0:T(8,128)(2,1)S(1)}, bf16[256,1024]{1,0:T(8,128)(2,1)S(1)}, u32[]{:S(2)}, u32[]{:S(2)}) collective-permute-start(bf16[256,1024]{1,0:T(8,128)(2,1)S(1)} %pad_maximum_fusion.9), channel_id=1, source_target_pairs={{0,1},{1,0},{2,3},{3,2},{4,5},{5,4},{6,7},{7,6},{8,9},{9,8},{10,11... | collective-permute-start | bytes 1572872 | tf_op jit(solution)/shard_map/ppermute | solution.py:505
  434.6 35.9 %collective-permute-start.57 = (bf16[64,1024]{0,1:T(8,128)(2,1)S(1)}, bf16[64,1024]{0,1:T(8,128)(2,1)S(1)}, u32[]{:S(2)}, u32[]{:S(2)}) collective-permute-start(bf16[64,1024]{0,1:T(8,128)(2,1)S(1)} %constant_dynamic-slice_fusion.1), channel_id=1, source_target_pairs={{0,8},{2,10},{4,12},{6,14},{8,0},{10,2},{12,4},{14,6},{1,9},{3,11}... | collective-permute-start | bytes 393224 | tf_op jit(solution)/shard_map/ppermute | solution.py:505
  436.7 28.3 %collective-permute-start.55 = (f32[1,2176]{1,0:T(1,128)S(1)}, f32[1,2176]{1,0:T(1,128)S(1)}, u32[]{:S(2)}, u32[]{:S(2)}) collective-permute-start(f32[1,2176]{1,0:T(1,128)S(1)} %add.480), channel_id=1, source_target_pairs={{0,8},{2,10},{4,12},{6,14},{8,0},{10,2},{12,4},{14,6},{1,9},{3,11}... | collective-permute-start | bytes 26120 | tf_op jit(solution)/shard_map/ppermute | solution.py:505
  438.5 32.2 %collective-permute-start.60 = (bf16[64,1024]{1,0:T(8,128)(2,1)S(1)}, bf16[64,1024]{1,0:T(8,128)(2,1)S(1)}, u32[]{:S(2)}, u32[]{:S(2)}) collective-permute-start(bf16[64,1024]{1,0:T(8,128)(2,1)S(1)} %constant_dynamic-slice_fusion), channel_id=1, source_target_pairs={{0,2},{2,0},{4,6},{6,4},{8,10},{10,8},{12,14},{14,12},{1,3},{3,1},... | collective-permute-start | bytes 393224 | tf_op jit(solution)/shard_map/ppermute | solution.py:505
  470.7 22.6 %collective-permute-start.58 = (bf16[64,1024]{0,1:T(8,128)(2,1)S(1)}, bf16[64,1024]{0,1:T(8,128)(2,1)S(1)}, u32[]{:S(2)}, u32[]{:S(2)}) collective-permute-start(bf16[64,1024]{0,1:T(8,128)(2,1)S(1)} %add_convert_fusion.4), channel_id=1, source_target_pairs={{0,8},{2,10},{4,12},{6,14},{8,0},{10,2},{12,4},{14,6},{1,9},{3,11}... | collective-permute-start | bytes 393224 | tf_op jit(solution)/shard_map/ppermute | solution.py:505
  470.8 22.7 %collective-permute-start.61 = (bf16[64,1024]{1,0:T(8,128)(2,1)S(1)}, bf16[64,1024]{1,0:T(8,128)(2,1)S(1)}, u32[]{:S(2)}, u32[]{:S(2)}) collective-permute-start(bf16[64,1024]{1,0:T(8,128)(2,1)S(1)} %add_convert_fusion.7), channel_id=1, source_target_pairs={{0,2},{2,0},{4,6},{6,4},{8,10},{10,8},{12,14},{14,12},{1,3},{3,1},... | collective-permute-start | bytes 393224 | tf_op jit(solution)/shard_map/ppermute | solution.py:505
  (117 other events, 1142.5 us)
Sparse Core Ops, SparseCore 0:
  142.8 87.8 all-gather.2
  293.7 104.8 reduce-scatter.1
  401.1 94.3 all-gather.4

commit v6 on v5

--- a/solution.py
+++ b/solution.py
@@ -870,10 +870,11 @@
             )
         if step == len(bits) + 1:
             parts, spread_out = lax.optimization_barrier((parts, last["spread"]))
-            last["grads"] = [
-                spread_out[:, at * hidden_half : (at + 1) * hidden_half].astype(F32)
-                for at in range(3)
+            pieces = [
+                spread_out[:, at * hidden_half : (at + 1) * hidden_half] for at in range(3)
             ]
+            pieces[2] = lax.optimization_barrier(pieces[2].T)
+            last["grads"] = [piece.astype(F32) for piece in pieces]
         return parts
 
     bits = list(ctx_bits())
@@ -902,7 +903,7 @@
         early[:, half:].T,
         w_gate_grad,
         w_up_grad,
-        w_down_grad.T,
+        w_down_grad,
     )
 
 

time: 545 us -> 541 us (level)
  no operation moved by 1% of the time
where the time goes in v6:
time: 541 us; the launch traced here: 532 us
  waiting for transfers between devices  191 us (35%)
  Pallas kernels  95.7 us (18%)
  starting transfers between devices  89.3 us (17%)
  matrix products  84 us (16%)
  local copies, waits for them, and re-layouts  27.4 us (5%)
  other arithmetic  26.1 us (5%)
  between operations  17.9 us (3%)
    ppermute x55, waiting for transfers between devices, flip(): lax.ppermute(values, axis, [(i, i ^ bit) for i in range(lax.axis_size(axi...  151 us
    dot_general x58, matrix products, dot(): lax.dot_general(left, right, (((left_dim,), (right_dim,)), ((), ())), pre...  84 us
    ppermute x55, starting transfers between devices, flip(): lax.ppermute(values, axis, [(i, i ^ bit) for i in range(lax.axis_size(axi...  58.3 us
    pallas_call x1, Pallas kernels, key_gradient(): pl.pallas_call(functools.partial(key_kernel, sizes, step_queries, first_p...  52.7 us
    pallas_call x4, Pallas kernels, query_gradient(): pl.pallas_call(functools.partial(query_kernel, sizes, step_keys, first_pa...  25.5 us
    reduce_scatter x1, waiting for transfers between devices, on_device(): lax.psum_scatter(parts['ffn'], CTX, scatter_dimension=0, tiled=True)  18 us
    unnamed x156, local copies, waits for them, and re-layouts  16 us
    pallas_call x5, Pallas kernels, forward_stage(): pl.pallas_call(functools.partial(forward_kernel, [m is not None for _, _,...  15.1 us
  transfers between devices with their start and end apart: 68, of which 37 were waited for; matrix products, arithmetic and copies ran while one was open for 23% of the time, Pallas kernels for 18%

profile of v6, /device:TPU:0, one launch (start us, length us, event | category | flops | bytes accessed | tf_op | source)
XLA Modules:
  0.0 531.6 jit_solution(2414131950365430600)
XLA Ops:
  39.1 4.4 collective-permute-start.9
  49.1 9.9 %collective-permute-done.8.refs_1_.refs_2_ = bf16[512,1024]{1,0:T(8,128)(2,1)S(1)} collective-permute-done((bf16[512,1024]{1,0:T(8,128)(2,1)S(1)}, bf16[512,1024]{1,0:T(8,128)(2,1)S(1)}, u32[]{:S(2)}, u32[]{:S(2)}) %collective-permute-start.8) | collective-permute-done | bytes 1048608 | tf_op jit(solution)/shard_map/ppermute | solution.py:505
  61.8 5.5 %collective-permute-start.11 = (bf16[512,1024]{1,0:T(8,128)(2,1)}, bf16[512,1024]{1,0:T(8,128)(2,1)}, u32[]{:S(2)}, u32[]{:S(2)}) collective-permute-start(bf16[512,1024]{1,0:T(8,128)(2,1)} %collective-permute-done.9.refs_3_.refs_4_), channel_id=1, source_target_pairs={{0,4},{2,6},{4,8},{6,10},{8,12},{10,14},{1,5},{3,7},{5,9},{7,11},{... | collective-permute-start | bytes 3145736 | tf_op jit(solution)/shard_map/ppermute | solution.py:622
  74.2 8.3 %collective-permute-done.10.refs_4_.refs_5_ = bf16[512,1024]{1,0:T(8,128)(2,1)S(1)} collective-permute-done((bf16[512,1024]{1,0:T(8,128)(2,1)}, bf16[512,1024]{1,0:T(8,128)(2,1)S(1)}, u32[]{:S(2)}, u32[]{:S(2)}) %collective-permute-start.10) | collective-permute-done | bytes 1048608 | tf_op jit(solution)/shard_map/ppermute | solution.py:505
  86.5 4.4 collective-permute-start.14
  96.3 4.9 shard_map.239
  108.2 4.5 collective-permute-start.16
  159.9 6.1 %collective-permute-done.25 = bf16[256,1024]{1,0:T(8,128)(2,1)S(1)} collective-permute-done((bf16[256,1024]{1,0:T(8,128)(2,1)S(1)}, bf16[256,1024]{1,0:T(8,128)(2,1)S(1)}, u32[]{:S(2)}, u32[]{:S(2)}) %collective-permute-start.25) | collective-permute-done | bytes 524320 | tf_op jit(solution)/shard_map/ppermute | solution.py:505
  216.1 5.0 collective-permute-done.32.other_ref
  229.3 6.1 %shard_map.243 = bf16[512,128]{1,0:T(8,128)(2,1)} custom-call(s32[9]{0:T(128)} %stack.146.place_ref, bf16[512,512]{1,0:T(8,128)(2,1)} %copy-done.5, bf16[560,512]{1,0:T(8,128)(2,1)} %get-tuple-element.140.grad_ref.refs_0_, f32[16,512]{1,0:T(8,128)} %get-tuple-element.152.stat_ref, s32[1,512]{1,0:T(1,128)} %copy-done.13, s32[2048,1]{1,0:T(8,128)} %copy.34.kmark_ref, ...), custom_call_target="tpu_custom_call" | custom-call | flops 268435456 | bytes 2097152 | tf_op jit(solution)/shard_map/pallas_call | solution.py:310
  239.8 6.5 %collective-permute-done.34.refs_3_ = bf16[560,512]{1,0:T(8,128)(2,1)S(1)} collective-permute-done((bf16[560,512]{1,0:T(8,128)(2,1)}, bf16[560,512]{1,0:T(8,128)(2,1)S(1)}, u32[]{:S(2)}, u32[]{:S(2)}) %collective-permute-start.34) | collective-permute-done | bytes 573472 | tf_op jit(solution)/shard_map/ppermute | solution.py:617
  249.3 5.0 collective-permute-start.38
  254.3 6.5 %shard_map.244 = bf16[512,128]{1,0:T(8,128)(2,1)} custom-call(s32[9]{0:T(128)} %stack.146.place_ref, bf16[512,512]{1,0:T(8,128)(2,1)} %copy-done.5, bf16[560,512]{1,0:T(8,128)(2,1)} %get-tuple-element.140.grad_ref.refs_0_, f32[16,512]{1,0:T(8,128)} %get-tuple-element.152.stat_ref, s32[1,512]{1,0:T(1,128)} %copy-done.13, s32[2048,1]{1,0:T(8,128)} %copy.34.kmark_ref, ...), custom_call_target="tpu_custom_call" | custom-call | flops 268435456 | bytes 2097152 | tf_op jit(solution)/shard_map/pallas_call | solution.py:310
  265.9 6.7 %shard_map.245 = bf16[512,128]{1,0:T(8,128)(2,1)} custom-call(s32[9]{0:T(128)} %stack.146.place_ref, bf16[512,512]{1,0:T(8,128)(2,1)} %copy-done.5, bf16[560,512]{1,0:T(8,128)(2,1)} %get-tuple-element.140.grad_ref.refs_0_, f32[16,512]{1,0:T(8,128)} %get-tuple-element.152.stat_ref, s32[1,512]{1,0:T(1,128)} %copy-done.13, s32[2048,1]{1,0:T(8,128)} %copy.34.kmark_ref, ...), custom_call_target="tpu_custom_call" | custom-call | flops 268435456 | bytes 2097152 | tf_op jit(solution)/shard_map/pallas_call | solution.py:310
  272.5 4.8 collective-permute-done.39.refs_6_
  287.1 6.1 %shard_map.246 = bf16[512,128]{1,0:T(8,128)(2,1)} custom-call(s32[9]{0:T(128)} %stack.146.place_ref, bf16[512,512]{1,0:T(8,128)(2,1)} %copy-done.5, bf16[560,512]{1,0:T(8,128)(2,1)} %get-tuple-element.140.grad_ref.refs_0_, f32[16,512]{1,0:T(8,128)} %get-tuple-element.152.stat_ref, s32[1,512]{1,0:T(1,128)} %copy-done.13, s32[2048,1]{1,0:T(8,128)} %copy.34.kmark_ref, ...), custom_call_target="tpu_custom_call" | custom-call | flops 268435456 | bytes 2097152 | tf_op jit(solution)/shard_map/pallas_call | solution.py:310
  296.8 52.7 %shard_map.247 = (bf16[512,512]{1,0:T(8,128)(2,1)}, bf16[512,512]{1,0:T(8,128)(2,1)}) custom-call(s32[9]{0:T(128)} %stack.137.place_ref, bf16[512,1024]{1,0:T(8,128)(2,1)} %copy-done, bf16[512,1024]{1,0:T(8,128)(2,1)} %copy-done, bf16[4096,512]{1,0:T(8,128)(2,1)} %all-gather.3.cloned.1.call-done.q_ref, s32[1,4096]{1,0:T(1,128)} %qmark_ref.1, ...), custom_call_target="tpu_custom_call" | custom-call | flops 1073741824 | bytes 8388608 | tf_op jit(solution)/shard_map/pallas_call | solution.py:448
  365.2 8.7 %collective-permute-done.45 = bf16[256,1024]{0,1:T(8,128)(2,1)} collective-permute-done((bf16[256,1024]{0,1:T(8,128)(2,1)S(1)}, bf16[256,1024]{0,1:T(8,128)(2,1)}, u32[]{:S(2)}, u32[]{:S(2)}) %collective-permute-start.45) | collective-permute-done | bytes 524320 | tf_op jit(solution)/shard_map/ppermute | solution.py:505
  380.6 18.0 %reduce-scatter.2.cloned.1.call-done = bf16[64,4224]{1,0:T(8,128)(2,1)} async-done(((bf16[512,4224]{1,0:T(8,128)(2,1)}), bf16[64,4224]{1,0:T(8,128)(2,1)}) %reduce-scatter.2.cloned.1.call-update) | async-done | bytes 540688 | tf_op jit(solution)/shard_map/reduce_scatter | solution.py:833
  417.9 8.8 %collective-permute-done.51 = bf16[256,512]{1,0:T(8,128)(2,1)S(1)} collective-permute-done((bf16[256,512]{1,0:T(8,128)(2,1)S(1)}, bf16[256,512]{1,0:T(8,128)(2,1)S(1)}, u32[]{:S(2)}, u32[]{:S(2)}) %collective-permute-start.51) | collective-permute-done | bytes 262176 | tf_op jit(solution)/shard_map/ppermute | solution.py:505
  439.9 25.0 %collective-permute-done.55 = f32[1,2176]{1,0:T(1,128)S(1)} collective-permute-done((f32[1,2176]{1,0:T(1,128)S(1)}, f32[1,2176]{1,0:T(1,128)S(1)}, u32[]{:S(2)}, u32[]{:S(2)}) %collective-permute-start.55) | collective-permute-done | bytes 8736 | tf_op jit(solution)/shard_map/ppermute | solution.py:505
  472.4 20.8 %collective-permute-done.58 = bf16[64,1024]{0,1:T(8,128)(2,1)S(1)} collective-permute-done((bf16[64,1024]{0,1:T(8,128)(2,1)S(1)}, bf16[64,1024]{0,1:T(8,128)(2,1)S(1)}, u32[]{:S(2)}, u32[]{:S(2)}) %collective-permute-start.58) | collective-permute-done | bytes 131104 | tf_op jit(solution)/shard_map/ppermute | solution.py:505
  496.2 9.6 %collective-permute-done.59 = bf16[128,1024]{0,1:T(8,128)(2,1)S(1)} collective-permute-done((bf16[128,1024]{0,1:T(8,128)(2,1)S(1)}, bf16[128,1024]{0,1:T(8,128)(2,1)S(1)}, u32[]{:S(2)}, u32[]{:S(2)}) %collective-permute-start.59) | collective-permute-done | bytes 262176 | tf_op jit(solution)/shard_map/ppermute | solution.py:505
  508.9 5.2 slice_bitcast_fusion
  (443 shorter events, 270.0 us)
Async XLA Ops:
  7.2 239.1 %all-gather.3.cloned.1.call-start = ((), (), s32[]{:S(2)}) async-start(), calls=%async_computation.1 | async-start | bytes 5242880 | tf_op jit(solution)/shard_map/all_gather | solution.py:737
  7.2 24.9 %collective-permute-start = (bf16[256,1024]{1,0:T(8,128)(2,1)}, bf16[256,1024]{1,0:T(8,128)(2,1)S(1)}, u32[]{:S(2)}, u32[]{:S(2)}) collective-permute-start(bf16[256,1024]{1,0:T(8,128)(2,1)} %bitcast.142), channel_id=1, source_target_pairs={{0,1},{1,0},{2,3},{3,2},{4,5},{5,4},{6,7},{7,6},{8,9},{9,8},{10,11... | collective-permute-start | bytes 1572872 | tf_op jit(solution)/shard_map/ppermute | solution.py:505
  12.0 20.0 %collective-permute-start.2 = (bf16[256,512]{1,0:T(8,128)(2,1)}, bf16[256,512]{1,0:T(8,128)(2,1)S(1)}, u32[]{:S(2)}, u32[]{:S(2)}) collective-permute-start(bf16[256,512]{1,0:T(8,128)(2,1)} %dynamic-slice_bitcast_fusion), channel_id=1, source_target_pairs={{0,1},{1,0},{2,3},{3,2},{4,5},{5,4},{6,7},{7,6},{8,9},{9,8},{10,11... | collective-permute-start | bytes 786440 | tf_op jit(solution)/shard_map/ppermute | solution.py:505
  37.2 21.8 %collective-permute-start.8 = (bf16[512,1024]{1,0:T(8,128)(2,1)S(1)}, bf16[512,1024]{1,0:T(8,128)(2,1)S(1)}, u32[]{:S(2)}, u32[]{:S(2)}) collective-permute-start(bf16[512,1024]{1,0:T(8,128)(2,1)S(1)} %pad_maximum_fusion.2.refs_1_.refs_2_.refs_0_.k_ref.v_ref), channel_id=1, source_target_pairs={{0,2},{2,0},{4,6},{6,4},{8,10},{10,8},{12,14},{14,12},{1,3},{3,1},... | collective-permute-start | bytes 3145736 | tf_op jit(solution)/shard_map/ppermute | solution.py:505
  39.1 22.2 %collective-permute-start.9 = (bf16[512,1024]{1,0:T(8,128)(2,1)S(1)}, bf16[512,1024]{1,0:T(8,128)(2,1)}, u32[]{:S(2)}, u32[]{:S(2)}) collective-permute-start(bf16[512,1024]{1,0:T(8,128)(2,1)S(1)} %pad_maximum_fusion.2.refs_1_.refs_2_.refs_0_.k_ref.v_ref), channel_id=1, source_target_pairs={{0,4},{2,6},{4,8},{6,10},{8,12},{10,14},{1,5},{3,7},{5,9},{7,11},{... | collective-permute-start | bytes 3145736 | tf_op jit(solution)/shard_map/ppermute | solution.py:617
  61.3 21.3 %collective-permute-start.10 = (bf16[512,1024]{1,0:T(8,128)(2,1)}, bf16[512,1024]{1,0:T(8,128)(2,1)S(1)}, u32[]{:S(2)}, u32[]{:S(2)}) collective-permute-start(bf16[512,1024]{1,0:T(8,128)(2,1)} %collective-permute-done.9.refs_3_.refs_4_), channel_id=1, source_target_pairs={{0,2},{2,0},{4,6},{6,4},{8,10},{10,8},{12,14},{14,12},{1,3},{3,1},... | collective-permute-start | bytes 3145736 | tf_op jit(solution)/shard_map/ppermute | solution.py:505
  61.8 22.3 %collective-permute-start.11 = (bf16[512,1024]{1,0:T(8,128)(2,1)}, bf16[512,1024]{1,0:T(8,128)(2,1)}, u32[]{:S(2)}, u32[]{:S(2)}) collective-permute-start(bf16[512,1024]{1,0:T(8,128)(2,1)} %collective-permute-done.9.refs_3_.refs_4_), channel_id=1, source_target_pairs={{0,4},{2,6},{4,8},{6,10},{8,12},{10,14},{1,5},{3,7},{5,9},{7,11},{... | collective-permute-start | bytes 3145736 | tf_op jit(solution)/shard_map/ppermute | solution.py:622
  84.1 20.4 %collective-permute-start.13 = (bf16[512,1024]{1,0:T(8,128)(2,1)}, bf16[512,1024]{1,0:T(8,128)(2,1)S(1)}, u32[]{:S(2)}, u32[]{:S(2)}) collective-permute-start(bf16[512,1024]{1,0:T(8,128)(2,1)} %collective-permute-done.11.refs_6_.refs_7_.refs_5_), channel_id=1, source_target_pairs={{0,2},{2,0},{4,6},{6,4},{8,10},{10,8},{12,14},{14,12},{1,3},{3,1},... | collective-permute-start | bytes 3145736 | tf_op jit(solution)/shard_map/ppermute | solution.py:505
  86.5 20.2 %collective-permute-start.14 = (bf16[512,1024]{1,0:T(8,128)(2,1)}, bf16[512,1024]{1,0:T(8,128)(2,1)S(1)}, u32[]{:S(2)}, u32[]{:S(2)}) collective-permute-start(bf16[512,1024]{1,0:T(8,128)(2,1)} %collective-permute-done.11.refs_6_.refs_7_.refs_5_), channel_id=1, source_target_pairs={{0,4},{2,6},{4,8},{6,10},{8,12},{10,14},{1,5},{3,7},{5,9},{7,11},{... | collective-permute-start | bytes 3145736 | tf_op jit(solution)/shard_map/ppermute | solution.py:626
  91.3 23.1 %collective-permute-start.18 = (bf16[512,512]{1,0:T(8,128)(2,1)}, bf16[512,512]{1,0:T(8,128)(2,1)}, u32[]{:S(2)}, u32[]{:S(2)}) collective-permute-start(bf16[512,512]{1,0:T(8,128)(2,1)} %param.24), channel_id=1, source_target_pairs={{0,1},{1,0},{2,3},{3,2},{4,5},{5,4},{6,7},{7,6},{8,9},{9,8},{10,11... | collective-permute-start | bytes 1572872 | tf_op jit(solution)/shard_map/ppermute | solution.py:505
  92.8 29.6 %collective-permute-start.19 = (bf16[512,512]{1,0:T(8,128)(2,1)}, bf16[512,512]{1,0:T(8,128)(2,1)}, u32[]{:S(2)}, u32[]{:S(2)}) collective-permute-start(bf16[512,512]{1,0:T(8,128)(2,1)} %param.24), channel_id=1, source_target_pairs={{0,16},{16,0},{1,17},{17,1},{2,18},{18,2},{3,19},{19,3},{4,20},{20... | collective-permute-start | bytes 1572872 | tf_op jit(solution)/shard_map/ppermute | solution.py:505
  92.9 42.0 %collective-permute-start.22 = (bf16[512,1408]{1,0:T(8,128)(2,1)}, bf16[512,1408]{1,0:T(8,128)(2,1)}, u32[]{:S(2)}, u32[]{:S(2)}) collective-permute-start(bf16[512,1408]{1,0:T(8,128)(2,1)} %param.25), channel_id=1, source_target_pairs={{0,16},{16,0},{1,17},{17,1},{2,18},{18,2},{3,19},{19,3},{4,20},{20... | collective-permute-start | bytes 4325384 | tf_op jit(solution)/shard_map/ppermute | solution.py:505
  114.4 24.2 %collective-permute-start.23 = (bf16[512,1408]{1,0:T(8,128)(2,1)S(1)}, bf16[512,1408]{1,0:T(8,128)(2,1)S(1)}, u32[]{:S(2)}, u32[]{:S(2)}) collective-permute-start(bf16[512,1408]{1,0:T(8,128)(2,1)S(1)} %copy-done.20), channel_id=1, source_target_pairs={{0,16},{16,0},{1,17},{17,1},{2,18},{18,2},{3,19},{19,3},{4,20},{20... | collective-permute-start | bytes 4325384 | tf_op jit(solution)/shard_map/ppermute | solution.py:505
  122.4 29.7 %collective-permute-start.24 = (bf16[1408,512]{1,0:T(8,128)(2,1)}, bf16[1408,512]{1,0:T(8,128)(2,1)}, u32[]{:S(2)}, u32[]{:S(2)}) collective-permute-start(bf16[1408,512]{1,0:T(8,128)(2,1)} %param.27), channel_id=1, source_target_pairs={{0,16},{16,0},{1,17},{17,1},{2,18},{18,2},{3,19},{19,3},{4,20},{20... | collective-permute-start | bytes 4325384 | tf_op jit(solution)/shard_map/ppermute | solution.py:505
  142.7 256.0 %reduce-scatter.2.cloned.1.call-start = ((), (), s32[]{:S(2)}) async-start(), calls=%async_computation.2 | async-start | bytes 4866048 | tf_op jit(solution)/shard_map/reduce_scatter | solution.py:833
  188.1 20.3 %collective-permute-start.28 = (bf16[256,1024]{1,0:T(8,128)(2,1)S(1)}, bf16[256,1024]{1,0:T(8,128)(2,1)S(1)}, u32[]{:S(2)}, u32[]{:S(2)}) collective-permute-start(bf16[256,1024]{1,0:T(8,128)(2,1)S(1)} %pad_maximum_fusion.8), channel_id=1, source_target_pairs={{0,1},{1,0},{2,3},{3,2},{4,5},{5,4},{6,7},{7,6},{8,9},{9,8},{10,11... | collective-permute-start | bytes 1572872 | tf_op jit(solution)/shard_map/ppermute | solution.py:505
  225.1 21.2 %collective-permute-start.34 = (bf16[560,512]{1,0:T(8,128)(2,1)}, bf16[560,512]{1,0:T(8,128)(2,1)S(1)}, u32[]{:S(2)}, u32[]{:S(2)}) collective-permute-start(bf16[560,512]{1,0:T(8,128)(2,1)} %get-tuple-element.140.grad_ref.refs_0_), channel_id=1, source_target_pairs={{4,0},{6,2},{8,4},{10,6},{12,8},{14,10},{5,1},{7,3},{9,5},{11,7},{... | collective-permute-start | bytes 1720328 | tf_op jit(solution)/shard_map/ppermute | solution.py:617
  294.0 214.0 %all-gather.5.cloned.1.call-start = ((), (), s32[]{:S(2)}) async-start(), calls=%async_computation.3 | async-start | bytes 4866048 | tf_op jit(solution)/shard_map/all_gather | solution.py:861
  407.8 18.9 %collective-permute-start.50 = (bf16[256,1024]{1,0:T(8,128)(2,1)S(1)}, bf16[256,1024]{1,0:T(8,128)(2,1)S(1)}, u32[]{:S(2)}, u32[]{:S(2)}) collective-permute-start(bf16[256,1024]{1,0:T(8,128)(2,1)S(1)} %pad_maximum_fusion.9), channel_id=1, source_target_pairs={{0,1},{1,0},{2,3},{3,2},{4,5},{5,4},{6,7},{7,6},{8,9},{9,8},{10,11... | collective-permute-start | bytes 1572872 | tf_op jit(solution)/shard_map/ppermute | solution.py:505
  434.6 35.9 %collective-permute-start.57 = (bf16[64,1024]{0,1:T(8,128)(2,1)S(1)}, bf16[64,1024]{0,1:T(8,128)(2,1)S(1)}, u32[]{:S(2)}, u32[]{:S(2)}) collective-permute-start(bf16[64,1024]{0,1:T(8,128)(2,1)S(1)} %constant_dynamic-slice_fusion.1), channel_id=1, source_target_pairs={{0,8},{2,10},{4,12},{6,14},{8,0},{10,2},{12,4},{14,6},{1,9},{3,11}... | collective-permute-start | bytes 393224 | tf_op jit(solution)/shard_map/ppermute | solution.py:505
  436.7 28.3 %collective-permute-start.55 = (f32[1,2176]{1,0:T(1,128)S(1)}, f32[1,2176]{1,0:T(1,128)S(1)}, u32[]{:S(2)}, u32[]{:S(2)}) collective-permute-start(f32[1,2176]{1,0:T(1,128)S(1)} %add.480), channel_id=1, source_target_pairs={{0,8},{2,10},{4,12},{6,14},{8,0},{10,2},{12,4},{14,6},{1,9},{3,11}... | collective-permute-start | bytes 26120 | tf_op jit(solution)/shard_map/ppermute | solution.py:505
  438.5 32.2 %collective-permute-start.60 = (bf16[64,1024]{1,0:T(8,128)(2,1)S(1)}, bf16[64,1024]{1,0:T(8,128)(2,1)S(1)}, u32[]{:S(2)}, u32[]{:S(2)}) collective-permute-start(bf16[64,1024]{1,0:T(8,128)(2,1)S(1)} %constant_dynamic-slice_fusion), channel_id=1, source_target_pairs={{0,2},{2,0},{4,6},{6,4},{8,10},{10,8},{12,14},{14,12},{1,3},{3,1},... | collective-permute-start | bytes 393224 | tf_op jit(solution)/shard_map/ppermute | solution.py:505
  470.7 22.6 %collective-permute-start.58 = (bf16[64,1024]{0,1:T(8,128)(2,1)S(1)}, bf16[64,1024]{0,1:T(8,128)(2,1)S(1)}, u32[]{:S(2)}, u32[]{:S(2)}) collective-permute-start(bf16[64,1024]{0,1:T(8,128)(2,1)S(1)} %add_convert_fusion.4), channel_id=1, source_target_pairs={{0,8},{2,10},{4,12},{6,14},{8,0},{10,2},{12,4},{14,6},{1,9},{3,11}... | collective-permute-start | bytes 393224 | tf_op jit(solution)/shard_map/ppermute | solution.py:505
  470.8 22.7 %collective-permute-start.61 = (bf16[64,1024]{1,0:T(8,128)(2,1)S(1)}, bf16[64,1024]{1,0:T(8,128)(2,1)S(1)}, u32[]{:S(2)}, u32[]{:S(2)}) collective-permute-start(bf16[64,1024]{1,0:T(8,128)(2,1)S(1)} %add_convert_fusion.7), channel_id=1, source_target_pairs={{0,2},{2,0},{4,6},{6,4},{8,10},{10,8},{12,14},{14,12},{1,3},{3,1},... | collective-permute-start | bytes 393224 | tf_op jit(solution)/shard_map/ppermute | solution.py:505
  (117 other events, 1139.1 us)
Sparse Core Ops, SparseCore 0:
  142.8 87.8 all-gather.2
  293.7 104.8 reduce-scatter.1
  401.1 94.3 all-gather.4

commit v7 on v6

--- a/solution.py
+++ b/solution.py
@@ -879,6 +879,7 @@
 
     bits = list(ctx_bits())
     early, late = reduce_ctx([early_part, kv_part], [bits, bits[1:] + bits[:1]], finish)
+    w_out_grad = lax.optimization_barrier(early[:, half:].T).astype(F32)
     early, late = early.astype(F32), late.astype(F32)
     w_gate_grad, w_up_grad, w_down_grad = last["grads"]
     grad_one = last["own"] + last["theirs"].astype(F32)
@@ -900,7 +901,7 @@
         early[:, :half],
         late[:, :half],
         late[:, half:],
-        early[:, half:].T,
+        w_out_grad,
         w_gate_grad,
         w_up_grad,
         w_down_grad,

time: 541 us -> 542 us (level)
  no operation moved by 1% of the time
where the time goes in v7:
time: 542 us; the launch traced here: 533 us
  waiting for transfers between devices  191 us (35%)
  Pallas kernels  95.7 us (18%)
  starting transfers between devices  89.3 us (16%)
  matrix products  84 us (15%)
  other arithmetic  28.1 us (5%)
  local copies, waits for them, and re-layouts  26.2 us (5%)
  between operations  17.9 us (3%)
    ppermute x55, waiting for transfers between devices, flip(): lax.ppermute(values, axis, [(i, i ^ bit) for i in range(lax.axis_size(axi...  151 us
    dot_general x58, matrix products, dot(): lax.dot_general(left, right, (((left_dim,), (right_dim,)), ((), ())), pre...  84 us
    ppermute x55, starting transfers between devices, flip(): lax.ppermute(values, axis, [(i, i ^ bit) for i in range(lax.axis_size(axi...  58.3 us
    pallas_call x1, Pallas kernels, key_gradient(): pl.pallas_call(functools.partial(key_kernel, sizes, step_queries, first_p...  52.7 us
    pallas_call x4, Pallas kernels, query_gradient(): pl.pallas_call(functools.partial(query_kernel, sizes, step_keys, first_pa...  25.5 us
    reduce_scatter x1, waiting for transfers between devices, on_device(): lax.psum_scatter(parts['ffn'], CTX, scatter_dimension=0, tiled=True)  18 us
    unnamed x156, local copies, waits for them, and re-layouts  16 us
    pallas_call x5, Pallas kernels, forward_stage(): pl.pallas_call(functools.partial(forward_kernel, [m is not None for _, _,...  15.1 us
  transfers between devices with their start and end apart: 68, of which 37 were waited for; matrix products, arithmetic and copies ran while one was open for 23% of the time, Pallas kernels for 18%

profile of v7, /device:TPU:0, one launch (start us, length us, event | category | flops | bytes accessed | tf_op | source)
XLA Modules:
  0.0 532.6 jit_solution(7085540743627600183)
XLA Ops:
  39.1 4.4 collective-permute-start.9
  49.1 9.9 %collective-permute-done.8.refs_1_.refs_2_ = bf16[512,1024]{1,0:T(8,128)(2,1)S(1)} collective-permute-done((bf16[512,1024]{1,0:T(8,128)(2,1)S(1)}, bf16[512,1024]{1,0:T(8,128)(2,1)S(1)}, u32[]{:S(2)}, u32[]{:S(2)}) %collective-permute-start.8) | collective-permute-done | bytes 1048608 | tf_op jit(solution)/shard_map/ppermute | solution.py:505
  61.8 5.5 %collective-permute-start.11 = (bf16[512,1024]{1,0:T(8,128)(2,1)}, bf16[512,1024]{1,0:T(8,128)(2,1)}, u32[]{:S(2)}, u32[]{:S(2)}) collective-permute-start(bf16[512,1024]{1,0:T(8,128)(2,1)} %collective-permute-done.9.refs_3_.refs_4_), channel_id=1, source_target_pairs={{0,4},{2,6},{4,8},{6,10},{8,12},{10,14},{1,5},{3,7},{5,9},{7,11},{... | collective-permute-start | bytes 3145736 | tf_op jit(solution)/shard_map/ppermute | solution.py:622
  74.2 8.3 %collective-permute-done.10.refs_4_.refs_5_ = bf16[512,1024]{1,0:T(8,128)(2,1)S(1)} collective-permute-done((bf16[512,1024]{1,0:T(8,128)(2,1)}, bf16[512,1024]{1,0:T(8,128)(2,1)S(1)}, u32[]{:S(2)}, u32[]{:S(2)}) %collective-permute-start.10) | collective-permute-done | bytes 1048608 | tf_op jit(solution)/shard_map/ppermute | solution.py:505
  86.5 4.4 collective-permute-start.14
  96.3 4.9 shard_map.239
  108.2 4.5 collective-permute-start.16
  159.9 6.1 %collective-permute-done.25 = bf16[256,1024]{1,0:T(8,128)(2,1)S(1)} collective-permute-done((bf16[256,1024]{1,0:T(8,128)(2,1)S(1)}, bf16[256,1024]{1,0:T(8,128)(2,1)S(1)}, u32[]{:S(2)}, u32[]{:S(2)}) %collective-permute-start.25) | collective-permute-done | bytes 524320 | tf_op jit(solution)/shard_map/ppermute | solution.py:505
  216.1 5.0 collective-permute-done.32.other_ref
  229.3 6.1 %shard_map.243 = bf16[512,128]{1,0:T(8,128)(2,1)} custom-call(s32[9]{0:T(128)} %stack.146.place_ref, bf16[512,512]{1,0:T(8,128)(2,1)} %copy-done.5, bf16[560,512]{1,0:T(8,128)(2,1)} %get-tuple-element.140.grad_ref.refs_0_, f32[16,512]{1,0:T(8,128)} %get-tuple-element.152.stat_ref, s32[1,512]{1,0:T(1,128)} %copy-done.13, s32[2048,1]{1,0:T(8,128)} %copy.34.kmark_ref, ...), custom_call_target="tpu_custom_call" | custom-call | flops 268435456 | bytes 2097152 | tf_op jit(solution)/shard_map/pallas_call | solution.py:310
  239.8 6.5 %collective-permute-done.34.refs_3_ = bf16[560,512]{1,0:T(8,128)(2,1)S(1)} collective-permute-done((bf16[560,512]{1,0:T(8,128)(2,1)}, bf16[560,512]{1,0:T(8,128)(2,1)S(1)}, u32[]{:S(2)}, u32[]{:S(2)}) %collective-permute-start.34) | collective-permute-done | bytes 573472 | tf_op jit(solution)/shard_map/ppermute | solution.py:617
  249.3 5.0 collective-permute-start.38
  254.3 6.5 %shard_map.244 = bf16[512,128]{1,0:T(8,128)(2,1)} custom-call(s32[9]{0:T(128)} %stack.146.place_ref, bf16[512,512]{1,0:T(8,128)(2,1)} %copy-done.5, bf16[560,512]{1,0:T(8,128)(2,1)} %get-tuple-element.140.grad_ref.refs_0_, f32[16,512]{1,0:T(8,128)} %get-tuple-element.152.stat_ref, s32[1,512]{1,0:T(1,128)} %copy-done.13, s32[2048,1]{1,0:T(8,128)} %copy.34.kmark_ref, ...), custom_call_target="tpu_custom_call" | custom-call | flops 268435456 | bytes 2097152 | tf_op jit(solution)/shard_map/pallas_call | solution.py:310
  265.9 6.7 %shard_map.245 = bf16[512,128]{1,0:T(8,128)(2,1)} custom-call(s32[9]{0:T(128)} %stack.146.place_ref, bf16[512,512]{1,0:T(8,128)(2,1)} %copy-done.5, bf16[560,512]{1,0:T(8,128)(2,1)} %get-tuple-element.140.grad_ref.refs_0_, f32[16,512]{1,0:T(8,128)} %get-tuple-element.152.stat_ref, s32[1,512]{1,0:T(1,128)} %copy-done.13, s32[2048,1]{1,0:T(8,128)} %copy.34.kmark_ref, ...), custom_call_target="tpu_custom_call" | custom-call | flops 268435456 | bytes 2097152 | tf_op jit(solution)/shard_map/pallas_call | solution.py:310
  272.5 4.8 collective-permute-done.39.refs_6_
  287.1 6.1 %shard_map.246 = bf16[512,128]{1,0:T(8,128)(2,1)} custom-call(s32[9]{0:T(128)} %stack.146.place_ref, bf16[512,512]{1,0:T(8,128)(2,1)} %copy-done.5, bf16[560,512]{1,0:T(8,128)(2,1)} %get-tuple-element.140.grad_ref.refs_0_, f32[16,512]{1,0:T(8,128)} %get-tuple-element.152.stat_ref, s32[1,512]{1,0:T(1,128)} %copy-done.13, s32[2048,1]{1,0:T(8,128)} %copy.34.kmark_ref, ...), custom_call_target="tpu_custom_call" | custom-call | flops 268435456 | bytes 2097152 | tf_op jit(solution)/shard_map/pallas_call | solution.py:310
  296.8 52.7 %shard_map.247 = (bf16[512,512]{1,0:T(8,128)(2,1)}, bf16[512,512]{1,0:T(8,128)(2,1)}) custom-call(s32[9]{0:T(128)} %stack.137.place_ref, bf16[512,1024]{1,0:T(8,128)(2,1)} %copy-done, bf16[512,1024]{1,0:T(8,128)(2,1)} %copy-done, bf16[4096,512]{1,0:T(8,128)(2,1)} %all-gather.3.cloned.1.call-done.q_ref, s32[1,4096]{1,0:T(1,128)} %qmark_ref.1, ...), custom_call_target="tpu_custom_call" | custom-call | flops 1073741824 | bytes 8388608 | tf_op jit(solution)/shard_map/pallas_call | solution.py:448
  365.2 8.7 %collective-permute-done.45 = bf16[256,1024]{0,1:T(8,128)(2,1)} collective-permute-done((bf16[256,1024]{0,1:T(8,128)(2,1)S(1)}, bf16[256,1024]{0,1:T(8,128)(2,1)}, u32[]{:S(2)}, u32[]{:S(2)}) %collective-permute-start.45) | collective-permute-done | bytes 524320 | tf_op jit(solution)/shard_map/ppermute | solution.py:505
  380.6 18.0 %reduce-scatter.2.cloned.1.call-done = bf16[64,4224]{1,0:T(8,128)(2,1)} async-done(((bf16[512,4224]{1,0:T(8,128)(2,1)}), bf16[64,4224]{1,0:T(8,128)(2,1)}) %reduce-scatter.2.cloned.1.call-update) | async-done | bytes 540688 | tf_op jit(solution)/shard_map/reduce_scatter | solution.py:833
  417.9 8.8 %collective-permute-done.51 = bf16[256,512]{1,0:T(8,128)(2,1)S(1)} collective-permute-done((bf16[256,512]{1,0:T(8,128)(2,1)S(1)}, bf16[256,512]{1,0:T(8,128)(2,1)S(1)}, u32[]{:S(2)}, u32[]{:S(2)}) %collective-permute-start.51) | collective-permute-done | bytes 262176 | tf_op jit(solution)/shard_map/ppermute | solution.py:505
  439.9 25.0 %collective-permute-done.55 = f32[1,2176]{1,0:T(1,128)S(1)} collective-permute-done((f32[1,2176]{1,0:T(1,128)S(1)}, f32[1,2176]{1,0:T(1,128)S(1)}, u32[]{:S(2)}, u32[]{:S(2)}) %collective-permute-start.55) | collective-permute-done | bytes 8736 | tf_op jit(solution)/shard_map/ppermute | solution.py:505
  472.4 20.8 %collective-permute-done.58 = bf16[64,1024]{0,1:T(8,128)(2,1)S(1)} collective-permute-done((bf16[64,1024]{0,1:T(8,128)(2,1)S(1)}, bf16[64,1024]{0,1:T(8,128)(2,1)S(1)}, u32[]{:S(2)}, u32[]{:S(2)}) %collective-permute-start.58) | collective-permute-done | bytes 131104 | tf_op jit(solution)/shard_map/ppermute | solution.py:505
  496.2 9.6 %collective-permute-done.59 = bf16[128,1024]{0,1:T(8,128)(2,1)S(1)} collective-permute-done((bf16[128,1024]{0,1:T(8,128)(2,1)S(1)}, bf16[128,1024]{0,1:T(8,128)(2,1)S(1)}, u32[]{:S(2)}, u32[]{:S(2)}) %collective-permute-start.59) | collective-permute-done | bytes 262176 | tf_op jit(solution)/shard_map/ppermute | solution.py:505
  508.9 5.2 slice_bitcast_fusion
  (443 shorter events, 271.0 us)
Async XLA Ops:
  7.2 239.1 %all-gather.3.cloned.1.call-start = ((), (), s32[]{:S(2)}) async-start(), calls=%async_computation.1 | async-start | bytes 5242880 | tf_op jit(solution)/shard_map/all_gather | solution.py:737
  7.2 24.9 %collective-permute-start = (bf16[256,1024]{1,0:T(8,128)(2,1)}, bf16[256,1024]{1,0:T(8,128)(2,1)S(1)}, u32[]{:S(2)}, u32[]{:S(2)}) collective-permute-start(bf16[256,1024]{1,0:T(8,128)(2,1)} %bitcast.142), channel_id=1, source_target_pairs={{0,1},{1,0},{2,3},{3,2},{4,5},{5,4},{6,7},{7,6},{8,9},{9,8},{10,11... | collective-permute-start | bytes 1572872 | tf_op jit(solution)/shard_map/ppermute | solution.py:505
  12.0 20.0 %collective-permute-start.2 = (bf16[256,512]{1,0:T(8,128)(2,1)}, bf16[256,512]{1,0:T(8,128)(2,1)S(1)}, u32[]{:S(2)}, u32[]{:S(2)}) collective-permute-start(bf16[256,512]{1,0:T(8,128)(2,1)} %dynamic-slice_bitcast_fusion), channel_id=1, source_target_pairs={{0,1},{1,0},{2,3},{3,2},{4,5},{5,4},{6,7},{7,6},{8,9},{9,8},{10,11... | collective-permute-start | bytes 786440 | tf_op jit(solution)/shard_map/ppermute | solution.py:505
  37.2 21.8 %collective-permute-start.8 = (bf16[512,1024]{1,0:T(8,128)(2,1)S(1)}, bf16[512,1024]{1,0:T(8,128)(2,1)S(1)}, u32[]{:S(2)}, u32[]{:S(2)}) collective-permute-start(bf16[512,1024]{1,0:T(8,128)(2,1)S(1)} %pad_maximum_fusion.2.refs_1_.refs_2_.refs_0_.k_ref.v_ref), channel_id=1, source_target_pairs={{0,2},{2,0},{4,6},{6,4},{8,10},{10,8},{12,14},{14,12},{1,3},{3,1},... | collective-permute-start | bytes 3145736 | tf_op jit(solution)/shard_map/ppermute | solution.py:505
  39.1 22.2 %collective-permute-start.9 = (bf16[512,1024]{1,0:T(8,128)(2,1)S(1)}, bf16[512,1024]{1,0:T(8,128)(2,1)}, u32[]{:S(2)}, u32[]{:S(2)}) collective-permute-start(bf16[512,1024]{1,0:T(8,128)(2,1)S(1)} %pad_maximum_fusion.2.refs_1_.refs_2_.refs_0_.k_ref.v_ref), channel_id=1, source_target_pairs={{0,4},{2,6},{4,8},{6,10},{8,12},{10,14},{1,5},{3,7},{5,9},{7,11},{... | collective-permute-start | bytes 3145736 | tf_op jit(solution)/shard_map/ppermute | solution.py:617
  61.3 21.3 %collective-permute-start.10 = (bf16[512,1024]{1,0:T(8,128)(2,1)}, bf16[512,1024]{1,0:T(8,128)(2,1)S(1)}, u32[]{:S(2)}, u32[]{:S(2)}) collective-permute-start(bf16[512,1024]{1,0:T(8,128)(2,1)} %collective-permute-done.9.refs_3_.refs_4_), channel_id=1, source_target_pairs={{0,2},{2,0},{4,6},{6,4},{8,10},{10,8},{12,14},{14,12},{1,3},{3,1},... | collective-permute-start | bytes 3145736 | tf_op jit(solution)/shard_map/ppermute | solution.py:505
  61.8 22.3 %collective-permute-start.11 = (bf16[512,1024]{1,0:T(8,128)(2,1)}, bf16[512,1024]{1,0:T(8,128)(2,1)}, u32[]{:S(2)}, u32[]{:S(2)}) collective-permute-start(bf16[512,1024]{1,0:T(8,128)(2,1)} %collective-permute-done.9.refs_3_.refs_4_), channel_id=1, source_target_pairs={{0,4},{2,6},{4,8},{6,10},{8,12},{10,14},{1,5},{3,7},{5,9},{7,11},{... | collective-permute-start | bytes 3145736 | tf_op jit(solution)/shard_map/ppermute | solution.py:622
  84.1 20.4 %collective-permute-start.13 = (bf16[512,1024]{1,0:T(8,128)(2,1)}, bf16[512,1024]{1,0:T(8,128)(2,1)S(1)}, u32[]{:S(2)}, u32[]{:S(2)}) collective-permute-start(bf16[512,1024]{1,0:T(8,128)(2,1)} %collective-permute-done.11.refs_6_.refs_7_.refs_5_), channel_id=1, source_target_pairs={{0,2},{2,0},{4,6},{6,4},{8,10},{10,8},{12,14},{14,12},{1,3},{3,1},... | collective-permute-start | bytes 3145736 | tf_op jit(solution)/shard_map/ppermute | solution.py:505
  86.5 20.2 %collective-permute-start.14 = (bf16[512,1024]{1,0:T(8,128)(2,1)}, bf16[512,1024]{1,0:T(8,128)(2,1)S(1)}, u32[]{:S(2)}, u32[]{:S(2)}) collective-permute-start(bf16[512,1024]{1,0:T(8,128)(2,1)} %collective-permute-done.11.refs_6_.refs_7_.refs_5_), channel_id=1, source_target_pairs={{0,4},{2,6},{4,8},{6,10},{8,12},{10,14},{1,5},{3,7},{5,9},{7,11},{... | collective-permute-start | bytes 3145736 | tf_op jit(solution)/shard_map/ppermute | solution.py:626
  91.3 23.1 %collective-permute-start.18 = (bf16[512,512]{1,0:T(8,128)(2,1)}, bf16[512,512]{1,0:T(8,128)(2,1)}, u32[]{:S(2)}, u32[]{:S(2)}) collective-permute-start(bf16[512,512]{1,0:T(8,128)(2,1)} %param.24), channel_id=1, source_target_pairs={{0,1},{1,0},{2,3},{3,2},{4,5},{5,4},{6,7},{7,6},{8,9},{9,8},{10,11... | collective-permute-start | bytes 1572872 | tf_op jit(solution)/shard_map/ppermute | solution.py:505
  92.8 29.6 %collective-permute-start.19 = (bf16[512,512]{1,0:T(8,128)(2,1)}, bf16[512,512]{1,0:T(8,128)(2,1)}, u32[]{:S(2)}, u32[]{:S(2)}) collective-permute-start(bf16[512,512]{1,0:T(8,128)(2,1)} %param.24), channel_id=1, source_target_pairs={{0,16},{16,0},{1,17},{17,1},{2,18},{18,2},{3,19},{19,3},{4,20},{20... | collective-permute-start | bytes 1572872 | tf_op jit(solution)/shard_map/ppermute | solution.py:505
  92.9 42.0 %collective-permute-start.22 = (bf16[512,1408]{1,0:T(8,128)(2,1)}, bf16[512,1408]{1,0:T(8,128)(2,1)}, u32[]{:S(2)}, u32[]{:S(2)}) collective-permute-start(bf16[512,1408]{1,0:T(8,128)(2,1)} %param.25), channel_id=1, source_target_pairs={{0,16},{16,0},{1,17},{17,1},{2,18},{18,2},{3,19},{19,3},{4,20},{20... | collective-permute-start | bytes 4325384 | tf_op jit(solution)/shard_map/ppermute | solution.py:505
  114.4 24.2 %collective-permute-start.23 = (bf16[512,1408]{1,0:T(8,128)(2,1)S(1)}, bf16[512,1408]{1,0:T(8,128)(2,1)S(1)}, u32[]{:S(2)}, u32[]{:S(2)}) collective-permute-start(bf16[512,1408]{1,0:T(8,128)(2,1)S(1)} %copy-done.20), channel_id=1, source_target_pairs={{0,16},{16,0},{1,17},{17,1},{2,18},{18,2},{3,19},{19,3},{4,20},{20... | collective-permute-start | bytes 4325384 | tf_op jit(solution)/shard_map/ppermute | solution.py:505
  122.4 29.7 %collective-permute-start.24 = (bf16[1408,512]{1,0:T(8,128)(2,1)}, bf16[1408,512]{1,0:T(8,128)(2,1)}, u32[]{:S(2)}, u32[]{:S(2)}) collective-permute-start(bf16[1408,512]{1,0:T(8,128)(2,1)} %param.27), channel_id=1, source_target_pairs={{0,16},{16,0},{1,17},{17,1},{2,18},{18,2},{3,19},{19,3},{4,20},{20... | collective-permute-start | bytes 4325384 | tf_op jit(solution)/shard_map/ppermute | solution.py:505
  142.7 256.0 %reduce-scatter.2.cloned.1.call-start = ((), (), s32[]{:S(2)}) async-start(), calls=%async_computation.2 | async-start | bytes 4866048 | tf_op jit(solution)/shard_map/reduce_scatter | solution.py:833
  188.1 20.3 %collective-permute-start.28 = (bf16[256,1024]{1,0:T(8,128)(2,1)S(1)}, bf16[256,1024]{1,0:T(8,128)(2,1)S(1)}, u32[]{:S(2)}, u32[]{:S(2)}) collective-permute-start(bf16[256,1024]{1,0:T(8,128)(2,1)S(1)} %pad_maximum_fusion.9), channel_id=1, source_target_pairs={{0,1},{1,0},{2,3},{3,2},{4,5},{5,4},{6,7},{7,6},{8,9},{9,8},{10,11... | collective-permute-start | bytes 1572872 | tf_op jit(solution)/shard_map/ppermute | solution.py:505
  225.1 21.2 %collective-permute-start.34 = (bf16[560,512]{1,0:T(8,128)(2,1)}, bf16[560,512]{1,0:T(8,128)(2,1)S(1)}, u32[]{:S(2)}, u32[]{:S(2)}) collective-permute-start(bf16[560,512]{1,0:T(8,128)(2,1)} %get-tuple-element.140.grad_ref.refs_0_), channel_id=1, source_target_pairs={{4,0},{6,2},{8,4},{10,6},{12,8},{14,10},{5,1},{7,3},{9,5},{11,7},{... | collective-permute-start | bytes 1720328 | tf_op jit(solution)/shard_map/ppermute | solution.py:617
  294.0 214.0 %all-gather.5.cloned.1.call-start = ((), (), s32[]{:S(2)}) async-start(), calls=%async_computation.3 | async-start | bytes 4866048 | tf_op jit(solution)/shard_map/all_gather | solution.py:861
  407.8 18.9 %collective-permute-start.50 = (bf16[256,1024]{1,0:T(8,128)(2,1)S(1)}, bf16[256,1024]{1,0:T(8,128)(2,1)S(1)}, u32[]{:S(2)}, u32[]{:S(2)}) collective-permute-start(bf16[256,1024]{1,0:T(8,128)(2,1)S(1)} %pad_maximum_fusion.10), channel_id=1, source_target_pairs={{0,1},{1,0},{2,3},{3,2},{4,5},{5,4},{6,7},{7,6},{8,9},{9,8},{10,11... | collective-permute-start | bytes 1572872 | tf_op jit(solution)/shard_map/ppermute | solution.py:505
  434.6 35.9 %collective-permute-start.57 = (bf16[64,1024]{0,1:T(8,128)(2,1)S(1)}, bf16[64,1024]{0,1:T(8,128)(2,1)S(1)}, u32[]{:S(2)}, u32[]{:S(2)}) collective-permute-start(bf16[64,1024]{0,1:T(8,128)(2,1)S(1)} %constant_dynamic-slice_fusion.1), channel_id=1, source_target_pairs={{0,8},{2,10},{4,12},{6,14},{8,0},{10,2},{12,4},{14,6},{1,9},{3,11}... | collective-permute-start | bytes 393224 | tf_op jit(solution)/shard_map/ppermute | solution.py:505
  436.7 28.3 %collective-permute-start.55 = (f32[1,2176]{1,0:T(1,128)S(1)}, f32[1,2176]{1,0:T(1,128)S(1)}, u32[]{:S(2)}, u32[]{:S(2)}) collective-permute-start(f32[1,2176]{1,0:T(1,128)S(1)} %add.480), channel_id=1, source_target_pairs={{0,8},{2,10},{4,12},{6,14},{8,0},{10,2},{12,4},{14,6},{1,9},{3,11}... | collective-permute-start | bytes 26120 | tf_op jit(solution)/shard_map/ppermute | solution.py:505
  438.5 32.2 %collective-permute-start.60 = (bf16[64,1024]{1,0:T(8,128)(2,1)S(1)}, bf16[64,1024]{1,0:T(8,128)(2,1)S(1)}, u32[]{:S(2)}, u32[]{:S(2)}) collective-permute-start(bf16[64,1024]{1,0:T(8,128)(2,1)S(1)} %constant_dynamic-slice_fusion), channel_id=1, source_target_pairs={{0,2},{2,0},{4,6},{6,4},{8,10},{10,8},{12,14},{14,12},{1,3},{3,1},... | collective-permute-start | bytes 393224 | tf_op jit(solution)/shard_map/ppermute | solution.py:505
  470.7 22.6 %collective-permute-start.58 = (bf16[64,1024]{0,1:T(8,128)(2,1)S(1)}, bf16[64,1024]{0,1:T(8,128)(2,1)S(1)}, u32[]{:S(2)}, u32[]{:S(2)}) collective-permute-start(bf16[64,1024]{0,1:T(8,128)(2,1)S(1)} %add_convert_fusion.4), channel_id=1, source_target_pairs={{0,8},{2,10},{4,12},{6,14},{8,0},{10,2},{12,4},{14,6},{1,9},{3,11}... | collective-permute-start | bytes 393224 | tf_op jit(solution)/shard_map/ppermute | solution.py:505
  470.8 22.7 %collective-permute-start.61 = (bf16[64,1024]{1,0:T(8,128)(2,1)S(1)}, bf16[64,1024]{1,0:T(8,128)(2,1)S(1)}, u32[]{:S(2)}, u32[]{:S(2)}) collective-permute-start(bf16[64,1024]{1,0:T(8,128)(2,1)S(1)} %add_convert_fusion.7), channel_id=1, source_target_pairs={{0,2},{2,0},{4,6},{6,4},{8,10},{10,8},{12,14},{14,12},{1,3},{3,1},... | collective-permute-start | bytes 393224 | tf_op jit(solution)/shard_map/ppermute | solution.py:505
  (117 other events, 1139.1 us)
Sparse Core Ops, SparseCore 0:
  142.8 87.8 all-gather.2
  293.7 104.8 reduce-scatter.1
  401.1 94.3 all-gather.4
